TPU v7x, 32 devices: a whole 2x2x4 slice. The times are simulated.
32 devices in a mesh: seq: 8 (over z, core), batch: 4 (over y, x).
Axes of the slice: x: 2, y: 2, z: 4, core: 2. Of those that a mesh axis runs over, the one named last changes fastest.
Arguments:
- tokens: bfloat16 [4, 2048, 1152], P('batch', 'seq'), may hold values from -6 to 6
- long_skip: bfloat16 [4, 2048, 1152], P('batch', 'seq'), may hold values from -6 to 6
- lengths: int32 [4, 4], P('batch'), may hold values from 0 to 1026, as said below
- skip_weight: bfloat16 [2304, 1152], replicated, may hold values from -0.125 to 0.125
- skip_bias: bfloat16 [1152], replicated, may hold values from -3 to 3
- attention_gain: bfloat16 [1152], replicated, may hold values from 0.099609375 to 1.8984375
- attention_shift: bfloat16 [1152], replicated, may hold values from -3 to 3
- qkv_weight: bfloat16 [1152, 3456], replicated, may hold values from -0.1875 to 0.1875
- out_weight: bfloat16 [1152, 1152], replicated, may hold values from -2 to 2
- out_bias: bfloat16 [1152], replicated, may hold values from -3 to 3
- mlp_gain: bfloat16 [1152], replicated, may hold values from 0.099609375 to 1.8984375
- mlp_shift: bfloat16 [1152], replicated, may hold values from -3 to 3
- hidden_weight: bfloat16 [1152, 4608], replicated, may hold values from -0.1875 to 0.1875
- hidden_bias: bfloat16 [4608], replicated, may hold values from -3 to 3
- down_weight: bfloat16 [4608, 1152], replicated, may hold values from -0.09375 to 0.09375
- down_bias: bfloat16 [1152], replicated, may hold values from -3 to 3
- cotangent: bfloat16 [4, 2048, 1152], P('batch', 'seq'), may hold values from -6 to 6
Outputs:
- output: bfloat16 [4, 2048, 1152], P('batch', 'seq')
- grad_tokens: float32 [4, 2048, 1152], P('batch', 'seq')
- grad_long_skip: float32 [4, 2048, 1152], P('batch', 'seq')
- grad_skip_weight: float32 [2304, 1152], P('batch', 'seq')
- grad_skip_bias: float32 [1152], replicated
- grad_attention_gain: float32 [1152], replicated
- grad_attention_shift: float32 [1152], replicated
- grad_qkv_weight: float32 [1152, 3456], P('batch', 'seq')
- grad_out_weight: float32 [1152, 1152], P('batch', 'seq')
- grad_out_bias: float32 [1152], replicated
- grad_mlp_gain: float32 [1152], replicated
- grad_mlp_shift: float32 [1152], replicated
- grad_hidden_weight: float32 [1152, 4608], P('batch', 'seq')
- grad_hidden_bias: float32 [4608], replicated
- grad_down_weight: float32 [4608, 1152], P('batch', 'seq')
- grad_down_bias: float32 [1152], replicated
Inputs may be any that keep to these rules, and one draw needn't show every extreme that they name: Row g lists the lengths of group g's items in the order in which they lie along the group's 2048 positions. Each entry is 258, 1026 or 0, every row has one or more entries 1026, zeros stand only after the last nonzero entry, and the row's total leaves fewer than 258 positions of padding at the end.
All inputs are finite; a program needn't handle non-finite values.
Results may differ from a plain program's by a relative error of at most 0.013.
Values may be sent and summed in bfloat16 or wider, within the bound.
A program may use at most 256 MiB of HBM per device.

v0:
```python
import math

import jax
import jax.numpy as jnp
from jax import lax
from jax.sharding import PartitionSpec as P

HD = 72


norm_eps = 1e-05


def product(left, right):
    return jnp.dot(left, right, preferred_element_type=jnp.float32)


def contract_rows(left, right):
    return lax.dot_general(
        left, right, (((0,), (0,)), ((), ())), preferred_element_type=jnp.float32
    )


def times_transposed(left, right):
    return lax.dot_general(
        left, right, (((1,), (1,)), ((), ())), preferred_element_type=jnp.float32
    )


def column_sums(values):
    return jnp.sum(values.astype(jnp.float32), axis=0)


def layer_norm(inputs, gain, shift):
    mean_row = jnp.mean(inputs, axis=-1, keepdims=True)
    centred = inputs - mean_row
    spread = jnp.mean(centred * centred, axis=-1, keepdims=True)
    return centred * lax.rsqrt(spread + norm_eps) * gain + shift


def exact_gelu(inputs):
    return jax.nn.gelu(inputs, approximate=False)


def segments(row_lengths, group_len):
    ends = jnp.cumsum(row_lengths)
    places = jnp.arange(group_len, dtype=jnp.int32)
    return jnp.sum((places[:, None] >= ends[None, :]).astype(jnp.int32), axis=1)


def score_block(query_block, key_heads, seg_block, segment):
    raw = jnp.einsum("bhd,khd->hbk", query_block, key_heads, preferred_element_type=jnp.float32)
    scores = raw * (1.0 / math.sqrt(HD))
    allowed = (seg_block[:, None] == segment[None, :])[None]
    return jnp.where(allowed, scores, -jnp.inf)


def attend_forward(query_heads, key_flat, value_flat, segment):
    length, head_cols = query_heads.shape
    head_count = head_cols // HD
    block_rows = min(512, length)
    block_count = length // block_rows
    key_heads = key_flat.reshape(length, head_count, HD)
    value_heads = value_flat.reshape(length, head_count, HD)

    def one_block(pieces):
        query_block, seg_block = pieces
        scores = score_block(query_block, key_heads, seg_block, segment)
        row_max = jnp.max(scores, axis=2, keepdims=True)
        log_total = row_max + jnp.log(jnp.sum(jnp.exp(scores - row_max), axis=2, keepdims=True))
        probs_low = jnp.exp(scores - log_total).astype(jnp.bfloat16)
        context = jnp.einsum(
            "hbk,khd->bhd", probs_low, value_heads, preferred_element_type=jnp.float32
        )
        return (context.astype(jnp.bfloat16).reshape(block_rows, head_cols), log_total)

    context, log_total = lax.map(
        one_block,
        (
            query_heads.reshape(block_count, block_rows, head_count, HD),
            segment.reshape(block_count, block_rows),
        ),
    )
    return (context.reshape(length, head_cols), log_total)


def attend_backward(query_heads, key_flat, value_flat, segment, grad_context, log_total):
    length, head_cols = query_heads.shape
    head_count = head_cols // HD
    block_rows = min(512, length)
    block_count = length // block_rows
    score_scale = 1.0 / math.sqrt(HD)
    key_heads = key_flat.reshape(length, head_count, HD)
    value_heads = value_flat.reshape(length, head_count, HD)

    def one_block(totals, pieces):
        grad_keys, grad_values = totals
        query_block, seg_block, grad_block, total_block = pieces
        scores = score_block(query_block, key_heads, seg_block, segment)
        prob_full = jnp.exp(scores - total_block)
        probs_low = prob_full.astype(jnp.bfloat16)
        grad_values = grad_values + jnp.einsum(
            "hbk,bhd->khd", probs_low, grad_block, preferred_element_type=jnp.float32
        )
        grad_probs = jnp.einsum(
            "bhd,khd->hbk", grad_block, value_heads, preferred_element_type=jnp.float32
        )
        row_delta = jnp.sum(prob_full * grad_probs, axis=2, keepdims=True)
        grad_scores = (prob_full * (grad_probs - row_delta)).astype(jnp.bfloat16)
        grad_query = (
            jnp.einsum("hbk,khd->bhd", grad_scores, key_heads, preferred_element_type=jnp.float32)
            * score_scale
        )
        grad_keys = grad_keys + jnp.einsum(
            "hbk,bhd->khd", grad_scores, query_block, preferred_element_type=jnp.float32
        )
        return (
            (grad_keys, grad_values),
            grad_query.astype(jnp.bfloat16).reshape(block_rows, head_cols),
        )

    empty_sum = jnp.zeros((length, head_count, HD), jnp.float32)
    (grad_keys, grad_values), grad_query = lax.scan(
        one_block,
        (empty_sum, empty_sum),
        (
            query_heads.reshape(block_count, block_rows, head_count, HD),
            segment.reshape(block_count, block_rows),
            grad_context.reshape(block_count, block_rows, head_count, HD),
            log_total,
        ),
    )
    grad_keys = (grad_keys * score_scale).astype(jnp.bfloat16).reshape(length, head_cols)
    grad_values = grad_values.astype(jnp.bfloat16).reshape(length, head_cols)
    return (grad_query.reshape(length, head_cols), grad_keys, grad_values)


def reduce_grads(weight_grads):
    partial_rows = (
        lax.psum_scatter(weight_grads[0], "batch", scatter_dimension=0, tiled=True),
        lax.psum_scatter(weight_grads[1], "batch", scatter_dimension=0, tiled=True),
        lax.psum_scatter(weight_grads[2], "batch", scatter_dimension=0, tiled=True),
        lax.psum_scatter(weight_grads[3], "batch", scatter_dimension=0, tiled=True),
        lax.psum_scatter(weight_grads[4], "batch", scatter_dimension=0, tiled=True),
    )
    return (
        lax.psum_scatter(partial_rows[0], "seq", scatter_dimension=1, tiled=True),
        lax.psum_scatter(partial_rows[1], "seq", scatter_dimension=1, tiled=True),
        lax.psum_scatter(partial_rows[2], "seq", scatter_dimension=1, tiled=True),
        lax.psum_scatter(partial_rows[3], "seq", scatter_dimension=1, tiled=True),
        lax.psum_scatter(partial_rows[4], "seq", scatter_dimension=1, tiled=True),
    )


def on_device(
    tokens,
    long_skip,
    lengths,
    skip_weight,
    skip_bias,
    attention_gain,
    attention_shift,
    qkv_weight,
    out_weight,
    out_bias,
    mlp_gain,
    mlp_shift,
    hidden_weight,
    hidden_bias,
    down_weight,
    down_bias,
    cotangent,
):
    local_rows = tokens.shape[1]
    feature_count = tokens.shape[2]
    group_len = local_rows * lax.axis_size("seq")
    joined = jnp.concatenate([tokens[0], long_skip[0]], axis=1)
    mixed = product(joined, skip_weight) + skip_bias.astype(jnp.float32)
    normed_full, first_pull = jax.vjp(
        layer_norm, mixed, attention_gain.astype(jnp.float32), attention_shift.astype(jnp.float32)
    )
    normed_one = normed_full.astype(jnp.bfloat16)
    packed = product(normed_one, qkv_weight).astype(jnp.bfloat16)
    query_tok = packed[:, :feature_count]
    key_tok = packed[:, feature_count : 2 * feature_count]
    value_tok = packed[:, 2 * feature_count :]
    query_heads, key_heads, value_heads = (
        lax.all_to_all(query_tok, "seq", split_axis=1, concat_axis=0, tiled=True),
        lax.all_to_all(key_tok, "seq", split_axis=1, concat_axis=0, tiled=True),
        lax.all_to_all(value_tok, "seq", split_axis=1, concat_axis=0, tiled=True),
    )
    segment = segments(lengths[0], group_len)
    context_heads, log_total = attend_forward(query_heads, key_heads, value_heads, segment)
    context_tok = lax.all_to_all(context_heads, "seq", split_axis=0, concat_axis=1, tiled=True)
    middle = mixed + product(context_tok, out_weight) + out_bias.astype(jnp.float32)
    second_full, second_pull = jax.vjp(
        layer_norm, middle, mlp_gain.astype(jnp.float32), mlp_shift.astype(jnp.float32)
    )
    normed_two = second_full.astype(jnp.bfloat16)
    hidden_pre = product(normed_two, hidden_weight) + hidden_bias.astype(jnp.float32)
    act_full, gelu_pull = jax.vjp(exact_gelu, hidden_pre)
    hidden_act = act_full.astype(jnp.bfloat16)
    output = (middle + product(hidden_act, down_weight) + down_bias.astype(jnp.float32)).astype(
        jnp.bfloat16
    )
    grad_out_rows = cotangent[0]
    grad_down_weight = contract_rows(hidden_act, grad_out_rows)
    grad_down_bias = column_sums(grad_out_rows)
    grad_act = times_transposed(grad_out_rows, down_weight)
    grad_pre = gelu_pull(grad_act)[0].astype(jnp.bfloat16)
    grad_hidden_weight = contract_rows(normed_two, grad_pre)
    grad_hidden_bias = column_sums(grad_pre)
    grad_normed_two = times_transposed(grad_pre, hidden_weight)
    grad_middle_norm, grad_mlp_gain, grad_mlp_shift = second_pull(grad_normed_two)
    grad_middle = grad_out_rows.astype(jnp.float32) + grad_middle_norm
    grad_attended = grad_middle.astype(jnp.bfloat16)
    grad_out_bias = column_sums(grad_attended)
    grad_out_weight = contract_rows(context_tok, grad_attended)
    grad_context = times_transposed(grad_attended, out_weight).astype(jnp.bfloat16)
    grad_context_heads = lax.all_to_all(
        grad_context, "seq", split_axis=1, concat_axis=0, tiled=True
    )
    grad_query, grad_key, grad_value = attend_backward(
        query_heads, key_heads, value_heads, segment, grad_context_heads, log_total
    )
    grad_query_tok, grad_key_tok, grad_value_tok = (
        lax.all_to_all(grad_query, "seq", split_axis=0, concat_axis=1, tiled=True),
        lax.all_to_all(grad_key, "seq", split_axis=0, concat_axis=1, tiled=True),
        lax.all_to_all(grad_value, "seq", split_axis=0, concat_axis=1, tiled=True),
    )
    grad_packed = jnp.concatenate([grad_query_tok, grad_key_tok, grad_value_tok], axis=1)
    grad_qkv_weight = contract_rows(normed_one, grad_packed)
    grad_normed_one = times_transposed(grad_packed, qkv_weight)
    grad_mixed_norm, grad_attention_gain, grad_attention_shift = first_pull(grad_normed_one)
    grad_mixed = (grad_middle + grad_mixed_norm).astype(jnp.bfloat16)
    grad_skip_bias = column_sums(grad_mixed)
    grad_skip_weight = contract_rows(joined, grad_mixed)
    grad_joined = times_transposed(grad_mixed, skip_weight)
    grad_tokens = grad_joined[:, :feature_count][None]
    grad_long_skip = grad_joined[:, feature_count:][None]
    summed_weights = reduce_grads(
        (grad_skip_weight, grad_qkv_weight, grad_out_weight, grad_hidden_weight, grad_down_weight)
    )
    summed_small = lax.psum(
        (
            grad_skip_bias,
            grad_attention_gain,
            grad_attention_shift,
            grad_out_bias,
            grad_mlp_gain,
            grad_mlp_shift,
            grad_hidden_bias,
            grad_down_bias,
        ),
        ("seq", "batch"),
    )
    return (
        output[None],
        grad_tokens,
        grad_long_skip,
        summed_weights[0],
        summed_small[0],
        summed_small[1],
        summed_small[2],
        summed_weights[1],
        summed_weights[2],
        summed_small[3],
        summed_small[4],
        summed_small[5],
        summed_weights[3],
        summed_small[6],
        summed_weights[4],
        summed_small[7],
    )


def solution(mesh):
    in_specs = (
        P("batch", "seq", None),
        P("batch", "seq", None),
        P("batch", None),
        P(),
        P(),
        P(),
        P(),
        P(),
        P(),
        P(),
        P(),
        P(),
        P(),
        P(),
        P(),
        P(),
        P("batch", "seq", None),
    )
    out_specs = (
        P("batch", "seq", None),
        P("batch", "seq", None),
        P("batch", "seq", None),
        P("batch", "seq"),
        P(),
        P(),
        P(),
        P("batch", "seq"),
        P("batch", "seq"),
        P(),
        P(),
        P(),
        P("batch", "seq"),
        P(),
        P("batch", "seq"),
        P(),
    )
    return jax.shard_map(
        on_device, mesh=mesh, in_specs=in_specs, out_specs=out_specs, check_vma=False
    )
```

profile of v0, /device:TPU:0, one launch (start us, length us, event | category | flops | bytes accessed | tf_op | source)
XLA Modules:
  0.0 1388.8 jit_solution(5655173782162970116)
XLA Ops:
  28.3 14.7 %all-to-all-done = bf16[256,8,144]{0,2,1:T(8,128)(2,1)} async-done(((bf16[256,8,144]{0,2,1:T(8,128)(2,1)}), bf16[256,8,144]{0,2,1:T(8,128)(2,1)}, u32[]{:S(2)}, u32[]{:S(2)}) %all-to-all-start) | async-done | bytes 589856 | tf_op jit(solution)/shard_map/all_to_all | solution.py:188
  48.3 15.7 %all-to-all-done.1 = bf16[256,8,144]{0,2,1:T(8,128)(2,1)} async-done(((bf16[256,8,144]{0,2,1:T(8,128)(2,1)}), bf16[256,8,144]{0,2,1:T(8,128)(2,1)}, u32[]{:S(2)}, u32[]{:S(2)}) %all-to-all-start.1) | async-done | bytes 589856 | tf_op jit(solution)/shard_map/all_to_all | solution.py:189
  90.2 36.5 %while.27 = (s32[]{:T(128)}, bf16[4,512,144]{1,2,0:T(8,128)(2,1)}, f32[4,2,512,1]{2,1,3,0:T(2,128)S(1)}, s32[4,512]{1,0:T(4,128)S(1)}, s32[2048]{0:T(1024)S(1)},...) while((s32[]{:T(128)}, bf16[4,512,144]{1,2,0:T(8,128)(2,1)}, ...), condition=%wide.region_7.8_spmd, body=%wide.region_4.7_spmd.sunk | while | flops 628169728 | bytes 33537152 | solution.py:77
  138.0 16.6 %all-to-all-done.3 = bf16[8,256,144]{1,2,0:T(8,128)(2,1)} async-done(((bf16[8,256,144]{1,2,0:T(8,128)(2,1)}), bf16[8,256,144]{1,2,0:T(8,128)(2,1)}, u32[]{:S(2)}, u32[]{:S(2)}) %all-to-all-start.3) | async-done | bytes 589856 | tf_op jit(solution)/shard_map/all_to_all | solution.py:194
  157.6 17.6 %multiply_convert_fusion.1 = (bf16[256,4608]{1,0:T(8,128)(2,1)}, f32[256,4608]{1,0:T(8,128)}, f32[256,4608]{1,0:T(8,128)}) fusion(f32[4608]{0:T(1024)S(1)} %convert_element_type.104, bf16[1152,4608]{1,0:T(8,128)(2,1)} %param.33, f32[256,1152]{1,0:T(8,128)S(1)} %get-tuple-element.392, f32[1152]{0:T(1024)S(1)} %convert_element_type.102, ...), kind=kOutput, calls=%fused_computation.56 | convolution fusion | flops 2797240320 | bytes 23622656 | tf_op jit(solution)/shard_map/dot_general | solution.py:15
  175.1 14.5 %convert_reduce_fusion = (f32[4608]{0:T(1024)}, bf16[256,4608]{1,0:T(8,128)(2,1)}) fusion(f32[256,4608]{1,0:T(8,128)} %get-tuple-element.378, f32[256,4608]{1,0:T(8,128)} %get-tuple-element.393, bf16[4608,1152]{1,0:T(8,128)(2,1)} %param.35, bf16[1,256,1152]{2,1,0:T(8,128)(2,1)S(1)} %copy-done.12), kind=kOutput, calls=%fused_computation.54 | convolution fusion | flops 2736778752 | bytes 23021568 | tf_op jit(solution)/shard_map/dot_general | solution.py:25
  209.3 16.6 %all-to-all-done.4 = bf16[256,8,144]{0,2,1:T(8,128)(2,1)S(1)} async-done(((bf16[256,8,144]{0,2,1:T(8,128)(2,1)}), bf16[256,8,144]{0,2,1:T(8,128)(2,1)S(1)}, u32[]{:S(2)}, u32[]{:S(2)}) %all-to-all-start.4) | async-done | bytes 589856 | tf_op jit(solution)/shard_map/all_to_all | solution.py:220
  228.2 96.4 %while.28 = (s32[]{:T(128)}, f32[2048,2,72]{0,2,1:T(8,128)S(1)}, f32[2048,2,72]{0,2,1:T(8,128)}, bf16[4,512,144]{1,2,0:T(8,128)(2,1)}, bf16[4,512,2,72]{1,3,2,0:...) while((s32[]{:T(128)}, f32[2048,2,72]{0,2,1:T(8,128)S(1)}, ...), condition=%wide.region_14.15_spmd.clone, body=%wide.region_12.14_spmd.clone.sunk | while | flops 1543781376 | bytes 144143088 | solution.py:123
  332.0 15.4 %all-to-all-done.5 = bf16[8,256,144]{1,2,0:T(8,128)(2,1)S(1)} async-done(((bf16[8,256,144]{1,2,0:T(8,128)(2,1)}), bf16[8,256,144]{1,2,0:T(8,128)(2,1)S(1)}, u32[]{:S(2)}, u32[]{:S(2)}) %all-to-all-start.5) | async-done | bytes 589856 | tf_op jit(solution)/shard_map/all_to_all | solution.py:227
  353.5 14.2 %all-to-all-done.6 = bf16[8,256,144]{1,2,0:T(8,128)(2,1)S(1)} async-done(((bf16[8,256,144]{1,2,0:T(8,128)(2,1)}), bf16[8,256,144]{1,2,0:T(8,128)(2,1)S(1)}, u32[]{:S(2)}, u32[]{:S(2)}) %all-to-all-start.6) | async-done | bytes 589856 | tf_op jit(solution)/shard_map/all_to_all | solution.py:228
  367.7 20.4 %all_to_all.140 = bf16[8,256,144]{1,2,0:T(8,128)(2,1)S(1)} all-to-all(bf16[8,256,144]{1,2,0:T(8,128)(2,1)} %copy.110), channel_id=1, replica_groups=mesh['seq'=8,'batch'=4] {'seq'}, dimensions={0} | all-to-all | bytes 1179648 | tf_op jit(solution)/shard_map/all_to_all | solution.py:229
  397.4 12.1 fusion.64
  429.7 12.9 fusion.52
  442.7 99.7 %reduce-scatter.23.cloned.1.call-done = f32[288,3456]{1,0:T(8,128)} async-done(((f32[1152,3456]{1,0:T(8,128)}), f32[288,3456]{1,0:T(8,128)}) %reduce-scatter.23.cloned.1.call-update) | async-done | bytes 3981328 | tf_op jit(solution)/shard_map/reduce_scatter | solution.py:141
  548.4 187.0 %reduce-scatter.27.cloned.1.call-done = f32[288,4608]{1,0:T(8,128)} async-done(((f32[1152,4608]{1,0:T(8,128)}), f32[288,4608]{1,0:T(8,128)}) %reduce-scatter.27.cloned.1.call-update) | async-done | bytes 5308432 | tf_op jit(solution)/shard_map/reduce_scatter | solution.py:143
  742.1 58.1 %reduce-scatter.25.cloned.1.call-done = f32[288,1152]{1,0:T(8,128)} async-done(((f32[1152,1152]{1,0:T(8,128)}), f32[288,1152]{1,0:T(8,128)}) %reduce-scatter.25.cloned.1.call-update) | async-done | bytes 1327120 | tf_op jit(solution)/shard_map/reduce_scatter | solution.py:142
  803.5 104.3 %reduce-scatter.21.cloned.1.call-done = f32[576,1152]{1,0:T(8,128)} async-done(((f32[2304,1152]{1,0:T(8,128)}), f32[576,1152]{1,0:T(8,128)}) %reduce-scatter.21.cloned.1.call-update) | async-done | bytes 2654224 | tf_op jit(solution)/shard_map/reduce_scatter | solution.py:140
  911.3 189.3 %reduce-scatter.29.cloned.1.call-done = f32[1152,1152]{1,0:T(8,128)} async-done(((f32[4608,1152]{1,0:T(8,128)}), f32[1152,1152]{1,0:T(8,128)}) %reduce-scatter.29.cloned.1.call-update) | async-done | bytes 5308432 | tf_op jit(solution)/shard_map/reduce_scatter | solution.py:144
  1108.2 9.1 fusion.47
  1117.3 43.5 %all-reduce = (f32[1152]{0:T(1024)}, f32[1152]{0:T(1024)}, f32[1152]{0:T(1024)}, f32[1152]{0:T(1024)}, f32[1152]{0:T(1024)}, /*index=5*/f32[1152]{0:T(1024)}, f32[4608]{0:T(1024)}, f32[1152]{0:T(1024)}) all-reduce(f32[1152]{0:T(1024)S(1)} %get-tuple-element.371, ...), channel_id=1, replica_groups=mesh['seq'=8,'batch'=4] {'seq','batch'}, use_global_device_ids=true, to_apply=%region_20.21 | all-reduce | flops 12672 | bytes 101376 | tf_op jit(solution)/shard_map/psum | solution.py:244
  1169.0 73.3 %reduce-scatter.37.cloned.1.call-done = f32[576,288]{1,0:T(8,128)} async-done(((f32[4608,288]{1,0:T(8,128)}), f32[576,288]{1,0:T(8,128)}) %reduce-scatter.37.cloned.1.call-update) | async-done | bytes 663568
  1244.6 34.2 %reduce-scatter.35.cloned.1.call-done = f32[144,288]{1,0:T(8,128)} async-done(((f32[1152,288]{1,0:T(8,128)}), f32[144,288]{1,0:T(8,128)}) %reduce-scatter.35.cloned.1.call-update) | async-done | bytes 165904
  1278.8 40.1 %reduce-scatter.31.cloned.1.call-done = f32[144,576]{1,0:T(8,128)} async-done(((f32[1152,576]{1,0:T(8,128)}), f32[144,576]{1,0:T(8,128)}) %reduce-scatter.31.cloned.1.call-update) | async-done | bytes 331792
  1318.9 62.6 %reduce-scatter.39.cloned.1.call-done = f32[144,1152]{1,0:T(8,128)} async-done(((f32[1152,1152]{1,0:T(8,128)}), f32[144,1152]{1,0:T(8,128)}) %reduce-scatter.39.cloned.1.call-update) | async-done | bytes 663568
  (288 shorter events, 301.1 us)
Async XLA Ops:
  7.2 147.5 %copy-start = (bf16[1152,1152]{1,0:T(8,128)(2,1)S(1)}, bf16[1152,1152]{1,0:T(8,128)(2,1)}, u32[]{:S(2)}) copy-start(bf16[1152,1152]{1,0:T(8,128)(2,1)} %param.29) | copy-start | bytes 7962628
  19.9 23.2 %all-to-all-start = ((bf16[256,8,144]{0,2,1:T(8,128)(2,1)}), bf16[256,8,144]{0,2,1:T(8,128)(2,1)}, u32[]{:S(2)}, u32[]{:S(2)}) async-start(bf16[256,8,144]{0,2,1:T(8,128)(2,1)} %bitcast.202), calls=%async_computation | async-start | bytes 1179648 | tf_op jit(solution)/shard_map/all_to_all | solution.py:188
  43.1 20.9 %all-to-all-start.1 = ((bf16[256,8,144]{0,2,1:T(8,128)(2,1)}), bf16[256,8,144]{0,2,1:T(8,128)(2,1)}, u32[]{:S(2)}, u32[]{:S(2)}) async-start(bf16[256,8,144]{0,2,1:T(8,128)(2,1)} %bitcast.200), calls=%async_computation.1 | async-start | bytes 1179648 | tf_op jit(solution)/shard_map/all_to_all | solution.py:189
  64.0 21.2 %all-to-all-start.2 = ((bf16[256,8,144]{0,2,1:T(8,128)(2,1)}), bf16[256,8,144]{0,2,1:T(8,128)(2,1)}, u32[]{:S(2)}, u32[]{:S(2)}) async-start(bf16[256,8,144]{0,2,1:T(8,128)(2,1)} %bitcast.199), calls=%async_computation.2 | async-start | bytes 1179648 | tf_op jit(solution)/shard_map/all_to_all | solution.py:190
  133.3 21.3 %all-to-all-start.3 = ((bf16[8,256,144]{1,2,0:T(8,128)(2,1)}), bf16[8,256,144]{1,2,0:T(8,128)(2,1)}, u32[]{:S(2)}, u32[]{:S(2)}) async-start(bf16[8,256,144]{1,2,0:T(8,128)(2,1)} %copy.102), calls=%async_computation.3 | async-start | bytes 1179648 | tf_op jit(solution)/shard_map/all_to_all | solution.py:194
  205.5 20.4 %all-to-all-start.4 = ((bf16[256,8,144]{0,2,1:T(8,128)(2,1)}), bf16[256,8,144]{0,2,1:T(8,128)(2,1)S(1)}, u32[]{:S(2)}, u32[]{:S(2)}) async-start(bf16[256,8,144]{0,2,1:T(8,128)(2,1)} %bitcast.19), calls=%async_computation.4 | async-start | bytes 1179648 | tf_op jit(solution)/shard_map/all_to_all | solution.py:220
  327.3 20.2 %all-to-all-start.5 = ((bf16[8,256,144]{1,2,0:T(8,128)(2,1)}), bf16[8,256,144]{1,2,0:T(8,128)(2,1)S(1)}, u32[]{:S(2)}, u32[]{:S(2)}) async-start(bf16[8,256,144]{1,2,0:T(8,128)(2,1)} %copy.108), calls=%async_computation.5 | async-start | bytes 1179648 | tf_op jit(solution)/shard_map/all_to_all | solution.py:227
  331.0 57.0 %copy-start.7 = (f32[256,1152]{1,0:T(8,128)S(1)}, f32[256,1152]{1,0:T(8,128)}, u32[]{:S(2)}) copy-start(f32[256,1152]{1,0:T(8,128)} %copy-done.6) | copy-start | bytes 3538948
  331.1 57.0 %copy-start.24 = (f32[1152]{0:T(1024)S(1)}, f32[1152]{0:T(1024)}, u32[]{:S(2)}) copy-start(f32[1152]{0:T(1024)} %copy-done.23) | copy-start | bytes 13828
  331.1 57.0 %copy-start.26 = (f32[1152]{0:T(1024)S(1)}, f32[1152]{0:T(1024)}, u32[]{:S(2)}) copy-start(f32[1152]{0:T(1024)} %copy-done.25) | copy-start | bytes 13828
  331.1 57.0 %copy-start.28 = (f32[256]{0:T(256)S(1)}, f32[256]{0:T(256)}, u32[]{:S(2)}) copy-start(f32[256]{0:T(256)} %copy-done.27) | copy-start | bytes 3076
  331.1 57.0 %copy-start.31 = (f32[256]{0:T(256)S(1)}, f32[256]{0:T(256)}, u32[]{:S(2)}) copy-start(f32[256]{0:T(256)} %copy-done.30) | copy-start | bytes 3076
  347.5 20.2 %all-to-all-start.6 = ((bf16[8,256,144]{1,2,0:T(8,128)(2,1)}), bf16[8,256,144]{1,2,0:T(8,128)(2,1)S(1)}, u32[]{:S(2)}, u32[]{:S(2)}) async-start(bf16[8,256,144]{1,2,0:T(8,128)(2,1)} %copy.109), calls=%async_computation.6 | async-start | bytes 1179648 | tf_op jit(solution)/shard_map/all_to_all | solution.py:228
  351.0 191.4 %reduce-scatter.23.cloned.1.call-start = ((), (), s32[]{:S(2)}) async-start(), calls=%async_computation.19 | async-start | bytes 19906560 | tf_op jit(solution)/shard_map/reduce_scatter | solution.py:141
  396.1 339.3 %reduce-scatter.27.cloned.1.call-start = ((), (), s32[]{:S(2)}) async-start(), calls=%async_computation.21 | async-start | bytes 26542080 | tf_op jit(solution)/shard_map/reduce_scatter | solution.py:143
  409.5 390.8 %reduce-scatter.25.cloned.1.call-start = ((), (), s32[]{:S(2)}) async-start(), calls=%async_computation.20 | async-start | bytes 6635520 | tf_op jit(solution)/shard_map/reduce_scatter | solution.py:142
  415.0 492.8 %reduce-scatter.21.cloned.1.call-start = ((), (), s32[]{:S(2)}) async-start(), calls=%async_computation.18 | async-start | bytes 13271040 | tf_op jit(solution)/shard_map/reduce_scatter | solution.py:140
  429.4 671.2 %reduce-scatter.29.cloned.1.call-start = ((), (), s32[]{:S(2)}) async-start(), calls=%async_computation.22 | async-start | bytes 26542080 | tf_op jit(solution)/shard_map/reduce_scatter | solution.py:144
  442.7 724.1 %reduce-scatter.33.cloned.1.call-start = ((), (), s32[]{:S(2)}) async-start(), calls=%async_computation.24 | async-start | bytes 5971968
  548.4 693.9 %reduce-scatter.37.cloned.1.call-start = ((), (), s32[]{:S(2)}) async-start(), calls=%async_computation.26 | async-start | bytes 7962624
  742.1 536.7 %reduce-scatter.35.cloned.1.call-start = ((), (), s32[]{:S(2)}) async-start(), calls=%async_computation.25 | async-start | bytes 1990656
  803.4 515.5 %reduce-scatter.31.cloned.1.call-start = ((), (), s32[]{:S(2)}) async-start(), calls=%async_computation.23 | async-start | bytes 3317760
  911.3 470.2 %reduce-scatter.39.cloned.1.call-start = ((), (), s32[]{:S(2)}) async-start(), calls=%async_computation.27 | async-start | bytes 5971968
  1160.8 220.7 %copy-start.1 = (bf16[1152,1152]{1,0:T(8,128)(2,1)S(1)}, bf16[1152,1152]{1,0:T(8,128)(2,1)}, u32[]{:S(2)}) copy-start(bf16[1152,1152]{1,0:T(8,128)(2,1)} %param.29) | copy-start | bytes 7962628
  (51 other events, 466.1 us)
Sparse Core Ops, SparseCore 0:
  396.2 146.1 reduce-scatter.22
  545.5 189.8 reduce-scatter.26
  738.4 61.8 reduce-scatter.24
  803.2 104.5 reduce-scatter.20
  910.7 189.8 reduce-scatter.28
  1102.8 61.4 reduce-scatter.32
  1166.6 75.6 reduce-scatter.36
  1245.2 33.5 reduce-scatter.34
  1281.7 37.1 reduce-scatter.30
  1321.6 59.8 reduce-scatter.38
where the time goes:
time: 1400 us; the launch traced here: 1390 us
  waiting for transfers between devices  951 us (68%)
  matrix products  212 us (15%)
  local copies, waits for them, and re-layouts  79 us (6%)
  blocking collectives  63.9 us (5%)
  other arithmetic  36.1 us (3%)
  starting transfers between devices  31 us (2%)
  between operations  15.2 us (1%)
    unnamed x15, waiting for transfers between devices  210 us
    reduce_scatter x1, waiting for transfers between devices, reduce_grads(): lax.psum_scatter(weight_grads[4], 'batch', scatter_dimension=0, tiled=True)  189 us
    reduce_scatter x1, waiting for transfers between devices, reduce_grads(): lax.psum_scatter(weight_grads[3], 'batch', scatter_dimension=0, tiled=True)  187 us
    reduce_scatter x1, waiting for transfers between devices, reduce_grads(): lax.psum_scatter(weight_grads[0], 'batch', scatter_dimension=0, tiled=True)  104 us
    reduce_scatter x1, waiting for transfers between devices, reduce_grads(): lax.psum_scatter(weight_grads[1], 'batch', scatter_dimension=0, tiled=True)  99.7 us
    reduce_scatter x1, waiting for transfers between devices, reduce_grads(): lax.psum_scatter(weight_grads[2], 'batch', scatter_dimension=0, tiled=True)  58.1 us
    psum x1, blocking collectives, on_device(): lax.psum((grad_skip_bias, grad_attention_gain, grad_attention_shift, grad...  43.5 us
    dot_general x5, matrix products, contract_rows(): lax.dot_general(left, right, (((0,), (0,)), ((), ())), preferred_element_...  43.1 us
  transfers between devices with their start and end apart: 17, of which 16 were waited for; matrix products, arithmetic and copies ran while one was open for 7% of the time, Pallas kernels for 0%

commit v1 on v0

--- a/solution.py
+++ b/solution.py
@@ -135,21 +135,27 @@
     return (grad_query.reshape(length, head_cols), grad_keys, grad_values)
 
 
-def reduce_grads(weight_grads):
-    partial_rows = (
-        lax.psum_scatter(weight_grads[0], "batch", scatter_dimension=0, tiled=True),
-        lax.psum_scatter(weight_grads[1], "batch", scatter_dimension=0, tiled=True),
-        lax.psum_scatter(weight_grads[2], "batch", scatter_dimension=0, tiled=True),
-        lax.psum_scatter(weight_grads[3], "batch", scatter_dimension=0, tiled=True),
-        lax.psum_scatter(weight_grads[4], "batch", scatter_dimension=0, tiled=True),
-    )
-    return (
-        lax.psum_scatter(partial_rows[0], "seq", scatter_dimension=1, tiled=True),
-        lax.psum_scatter(partial_rows[1], "seq", scatter_dimension=1, tiled=True),
-        lax.psum_scatter(partial_rows[2], "seq", scatter_dimension=1, tiled=True),
-        lax.psum_scatter(partial_rows[3], "seq", scatter_dimension=1, tiled=True),
-        lax.psum_scatter(partial_rows[4], "seq", scatter_dimension=1, tiled=True),
-    )
+def seq_gathered_grad(left, right):
+    left_all = lax.all_gather(left, "seq", axis=0, tiled=True)
+    right_cols = lax.all_to_all(right, "seq", split_axis=1, concat_axis=0, tiled=True)
+    partial = contract_rows(left_all, right_cols)
+    return lax.psum_scatter(partial, "batch", scatter_dimension=0, tiled=True)
+
+
+def batch_gathered_grad(left, right):
+    left_rows = lax.all_to_all(left, "batch", split_axis=1, concat_axis=0, tiled=True)
+    right_all = lax.all_gather(right, "batch", axis=0, tiled=True)
+    partial = contract_rows(left_rows, right_all)
+    return lax.psum_scatter(partial, "seq", scatter_dimension=1, tiled=True)
+
+
+GRAD_PLAN = {"skip": "batch", "qkv": "seq", "out": "batch", "hidden": "seq", "down": "batch"}
+
+
+def weight_grad(name, left, right):
+    if GRAD_PLAN[name] == "seq":
+        return seq_gathered_grad(left, right)
+    return batch_gathered_grad(left, right)
 
 
 def on_device(
@@ -204,18 +210,18 @@
         jnp.bfloat16
     )
     grad_out_rows = cotangent[0]
-    grad_down_weight = contract_rows(hidden_act, grad_out_rows)
+    grad_down_weight = weight_grad("down", hidden_act, grad_out_rows)
     grad_down_bias = column_sums(grad_out_rows)
     grad_act = times_transposed(grad_out_rows, down_weight)
     grad_pre = gelu_pull(grad_act)[0].astype(jnp.bfloat16)
-    grad_hidden_weight = contract_rows(normed_two, grad_pre)
+    grad_hidden_weight = weight_grad("hidden", normed_two, grad_pre)
     grad_hidden_bias = column_sums(grad_pre)
     grad_normed_two = times_transposed(grad_pre, hidden_weight)
     grad_middle_norm, grad_mlp_gain, grad_mlp_shift = second_pull(grad_normed_two)
     grad_middle = grad_out_rows.astype(jnp.float32) + grad_middle_norm
     grad_attended = grad_middle.astype(jnp.bfloat16)
     grad_out_bias = column_sums(grad_attended)
-    grad_out_weight = contract_rows(context_tok, grad_attended)
+    grad_out_weight = weight_grad("out", context_tok, grad_attended)
     grad_context = times_transposed(grad_attended, out_weight).astype(jnp.bfloat16)
     grad_context_heads = lax.all_to_all(
         grad_context, "seq", split_axis=1, concat_axis=0, tiled=True
@@ -229,18 +235,16 @@
         lax.all_to_all(grad_value, "seq", split_axis=0, concat_axis=1, tiled=True),
     )
     grad_packed = jnp.concatenate([grad_query_tok, grad_key_tok, grad_value_tok], axis=1)
-    grad_qkv_weight = contract_rows(normed_one, grad_packed)
+    grad_qkv_weight = weight_grad("qkv", normed_one, grad_packed)
     grad_normed_one = times_transposed(grad_packed, qkv_weight)
     grad_mixed_norm, grad_attention_gain, grad_attention_shift = first_pull(grad_normed_one)
     grad_mixed = (grad_middle + grad_mixed_norm).astype(jnp.bfloat16)
     grad_skip_bias = column_sums(grad_mixed)
-    grad_skip_weight = contract_rows(joined, grad_mixed)
+    grad_skip_weight = weight_grad("skip", joined, grad_mixed)
     grad_joined = times_transposed(grad_mixed, skip_weight)
     grad_tokens = grad_joined[:, :feature_count][None]
     grad_long_skip = grad_joined[:, feature_count:][None]
-    summed_weights = reduce_grads(
-        (grad_skip_weight, grad_qkv_weight, grad_out_weight, grad_hidden_weight, grad_down_weight)
-    )
+    summed_weights = (grad_skip_weight, grad_qkv_weight, grad_out_weight, grad_hidden_weight, grad_down_weight)
     summed_small = lax.psum(
         (
             grad_skip_bias,

time: 1400 us -> 791 us (0.56)
  waiting for transfers between devices: 951 us -> 279 us
  blocking collectives: 63.9 us -> 148 us
  local copies, waits for them, and re-layouts: 79 us -> 60.2 us
  matrix products: 212 us -> 197 us
    reduce_scatter x5, waiting for transfers between devices: 638 us -> 104 us  [the longest x3 59.5 us: batch_gathered_grad(): return lax.psum_scatter(partial, 'seq', scatter_dimension=1, tiled=True)]
    unnamed x15 -> x10, waiting for transfers between devices: 210 us -> 1.69 us
    all_to_all x1 -> x3, blocking collectives: 20.4 us -> 106 us  [the longest x1 69.1 us: seq_gathered_grad(): lax.all_to_all(right, 'seq', split_axis=1, concat_axis=0, tiled=True)]
    all_to_all x1 -> x4, waiting for transfers between devices: 15.4 us -> 90.3 us  [the longest x2 37.9 us: batch_gathered_grad(): lax.all_to_all(left, 'batch', split_axis=1, concat_axis=0, tiled=True)]
    unnamed x94 -> x85, local copies, waits for them, and re-layouts: 38 us -> 8.97 us
  transfers between devices with their start and end apart: 17 -> 20, of which waited for: 16 -> 12; matrix products, arithmetic and copies ran while one was open for 7% -> 23% of each run, Pallas kernels for 0% -> 0%
where the time goes in v1:
time: 791 us; the launch traced here: 784 us
  waiting for transfers between devices  279 us (35%)
  matrix products  197 us (25%)
  blocking collectives  148 us (19%)
  local copies, waits for them, and re-layouts  60.2 us (8%)
  other arithmetic  43.1 us (5%)
  starting transfers between devices  42 us (5%)
  between operations  15.3 us (2%)
    all_to_all x1, blocking collectives, seq_gathered_grad(): lax.all_to_all(right, 'seq', split_axis=1, concat_axis=0, tiled=True)  69.1 us
    reduce_scatter x3, waiting for transfers between devices, batch_gathered_grad(): return lax.psum_scatter(partial, 'seq', scatter_dimension=1, tiled=True)  59.5 us
    reduce_scatter x2, waiting for transfers between devices, seq_gathered_grad(): return lax.psum_scatter(partial, 'batch', scatter_dimension=0, tiled=True)  44.3 us
    psum x1, blocking collectives, on_device(): lax.psum((grad_skip_bias, grad_attention_gain, grad_attention_shift, grad...  41.3 us
    dot_general x5, matrix products, product(): return jnp.dot(left, right, preferred_element_type=jnp.float32)  39.3 us
    all_to_all x2, waiting for transfers between devices, batch_gathered_grad(): lax.all_to_all(left, 'batch', split_axis=1, concat_axis=0, tiled=True)  37.9 us
    dot_general x5, matrix products, times_transposed(): lax.dot_general(left, right, (((1,), (1,)), ((), ())), preferred_element_...  37 us
    all_to_all x1, waiting for transfers between devices, seq_gathered_grad(): lax.all_to_all(right, 'seq', split_axis=1, concat_axis=0, tiled=True)  37 us
  transfers between devices with their start and end apart: 20, of which 12 were waited for; matrix products, arithmetic and copies ran while one was open for 23% of the time, Pallas kernels for 0%

profile of v1, /device:TPU:0, one launch (start us, length us, event | category | flops | bytes accessed | tf_op | source)
XLA Modules:
  0.0 784.3 jit_solution(9298604926312819391)
XLA Ops:
  34.3 14.7 %all-to-all-done = bf16[256,8,144]{0,2,1:T(8,128)(2,1)} async-done(((bf16[256,8,144]{0,2,1:T(8,128)(2,1)}), bf16[256,8,144]{0,2,1:T(8,128)(2,1)}, u32[]{:S(2)}, u32[]{:S(2)}) %all-to-all-start) | async-done | bytes 589856 | tf_op jit(solution)/shard_map/all_to_all | solution.py:194
  54.3 15.7 %all-to-all-done.1 = bf16[256,8,144]{0,2,1:T(8,128)(2,1)} async-done(((bf16[256,8,144]{0,2,1:T(8,128)(2,1)}), bf16[256,8,144]{0,2,1:T(8,128)(2,1)}, u32[]{:S(2)}, u32[]{:S(2)}) %all-to-all-start.1) | async-done | bytes 589856 | tf_op jit(solution)/shard_map/all_to_all | solution.py:195
  82.5 8.6 %all-to-all-done.2 = bf16[256,8,144]{0,2,1:T(8,128)(2,1)} async-done(((bf16[256,8,144]{0,2,1:T(8,128)(2,1)}), bf16[256,8,144]{0,2,1:T(8,128)(2,1)}, u32[]{:S(2)}, u32[]{:S(2)}) %all-to-all-start.2) | async-done | bytes 589856 | tf_op jit(solution)/shard_map/all_to_all | solution.py:196
  96.1 36.5 %while.27 = (s32[]{:T(128)}, bf16[4,512,144]{1,2,0:T(8,128)(2,1)}, f32[4,2,512,1]{2,1,3,0:T(2,128)S(1)}, s32[4,512]{1,0:T(4,128)S(1)}, s32[2048]{0:T(1024)S(1)},...) while((s32[]{:T(128)}, bf16[4,512,144]{1,2,0:T(8,128)(2,1)}, ...), condition=%wide.region_7.8_spmd, body=%wide.region_4.7_spmd.sunk | while | flops 628169728 | bytes 33536144 | solution.py:77
  144.0 16.2 %all-to-all-done.3 = bf16[8,256,144]{1,2,0:T(8,128)(2,1)} async-done(((bf16[8,256,144]{1,2,0:T(8,128)(2,1)}), bf16[8,256,144]{1,2,0:T(8,128)(2,1)}, u32[]{:S(2)}, u32[]{:S(2)}) %all-to-all-start.3) | async-done | bytes 589856 | tf_op jit(solution)/shard_map/all_to_all | solution.py:200
  164.9 17.1 %multiply_convert_fusion.1 = (bf16[256,4608]{1,0:T(8,128)(2,1)}, f32[256,4608]{1,0:T(8,128)}, f32[256,4608]{1,0:T(8,128)}) fusion(f32[4608]{0:T(1024)S(1)} %convert_element_type.104, bf16[256,1152]{1,0:T(8,128)(2,1)} %add_convert_fusion.2, bf16[1152,4608]{1,0:T(8,128)(2,1)} %param.33), kind=kOutput, calls=%fused_computation.56 | convolution fusion | flops 2795765760 | bytes 23021568 | tf_op jit(solution)/shard_map/dot_general | solution.py:15
  182.1 14.6 %convert_reduce_fusion = (f32[4608]{0:T(1024)}, bf16[256,4608]{1,0:T(8,128)(2,1)}) fusion(f32[256,4608]{1,0:T(8,128)} %get-tuple-element.298, f32[256,4608]{1,0:T(8,128)} %get-tuple-element.313, bf16[4608,1152]{1,0:T(8,128)(2,1)} %param.35, bf16[1,256,1152]{2,1,0:T(8,128)(2,1)S(1)} %copy-done.13), kind=kOutput, calls=%fused_computation.54 | convolution fusion | flops 2736778752 | bytes 23021568 | tf_op jit(solution)/shard_map/dot_general | solution.py:25
  196.7 8.7 %multiply_reduce_fusion.1 = (f32[1152]{0:T(1024)}, f32[256]{0:T(256)S(1)}, f32[1152]{0:T(1024)}, f32[256,1152]{1,0:T(8,128)S(1)}) fusion(f32[256,1152]{1,0:T(8,128)S(1)} %copy-done.7, f32[256]{0:T(256)S(1)} %fusion.59, f32[256]{0:T(256)S(1)} %broadcast_multiply_fusion, f32[1152]{0:T(1024)S(1)} %convert_element_type.101, ...), kind=kOutput, calls=%fused_computation.92 | convolution fusion | flops 2720265728 | bytes 15352320 | tf_op jit(solution)/shard_map/dot_general | solution.py:25
  217.9 15.9 %all-to-all-done.4 = bf16[256,8,144]{0,2,1:T(8,128)(2,1)S(1)} async-done(((bf16[256,8,144]{0,2,1:T(8,128)(2,1)}), bf16[256,8,144]{0,2,1:T(8,128)(2,1)S(1)}, u32[]{:S(2)}, u32[]{:S(2)}) %all-to-all-start.4) | async-done | bytes 589856 | tf_op jit(solution)/shard_map/all_to_all | solution.py:226
  236.2 87.6 %while.28 = (s32[]{:T(128)}, f32[2048,2,72]{0,2,1:T(8,128)S(1)}, f32[2048,2,72]{0,2,1:T(8,128)}, bf16[4,512,144]{1,2,0:T(8,128)(2,1)}, bf16[4,512,2,72]{1,3,2,0:...) while((s32[]{:T(128)}, f32[2048,2,72]{0,2,1:T(8,128)S(1)}, ...), condition=%wide.region_14.15_spmd.clone, body=%wide.region_12.14_spmd.clone.sunk | while | flops 1543781376 | bytes 136800560 | solution.py:123
  331.2 15.4 %all-to-all-done.7 = bf16[8,256,144]{1,2,0:T(8,128)(2,1)S(1)} async-done(((bf16[8,256,144]{1,2,0:T(8,128)(2,1)}), bf16[8,256,144]{1,2,0:T(8,128)(2,1)S(1)}, u32[]{:S(2)}, u32[]{:S(2)}) %all-to-all-start.7) | async-done | bytes 589856 | tf_op jit(solution)/shard_map/all_to_all | solution.py:235
  354.9 11.9 %all-to-all-done.6 = bf16[8,256,144]{1,2,0:T(8,128)(2,1)S(1)} async-done(((bf16[8,256,144]{1,2,0:T(8,128)(2,1)}), bf16[8,256,144]{1,2,0:T(8,128)(2,1)S(1)}, u32[]{:S(2)}, u32[]{:S(2)}) %all-to-all-start.6) | async-done | bytes 589856 | tf_op jit(solution)/shard_map/all_to_all | solution.py:234
  366.8 19.3 %all_to_all.232 = bf16[8,256,144]{1,2,0:T(8,128)(2,1)S(1)} all-to-all(bf16[8,256,144]{1,2,0:T(8,128)(2,1)S(1)} %copy.122), channel_id=1, replica_groups=mesh['seq'=8,'batch'=4] {'seq'}, dimensions={0} | all-to-all | bytes 1179648 | tf_op jit(solution)/shard_map/all_to_all | solution.py:233
  402.3 12.0 %all-to-all-done.10 = bf16[256,4,288]{0,2,1:T(8,128)(2,1)S(1)} async-done(((bf16[256,4,288]{0,2,1:T(8,128)(2,1)}), bf16[256,4,288]{0,2,1:T(8,128)(2,1)S(1)}, u32[]{:S(2)}, u32[]{:S(2)}) %all-to-all-start.10) | async-done | bytes 589856 | tf_op jit(solution)/shard_map/all_to_all | solution.py:146
  422.9 37.0 %all-to-all-done.9 = bf16[256,8,432]{0,2,1:T(8,128)(2,1)S(1)} async-done(((bf16[256,8,432]{0,2,1:T(8,128)(2,1)}), bf16[256,8,432]{0,2,1:T(8,128)(2,1)S(1)}, u32[]{:S(2)}, u32[]{:S(2)}) %all-to-all-start.9) | async-done | bytes 1769504 | tf_op jit(solution)/shard_map/all_to_all | solution.py:140
  469.9 18.0 %all_to_all.233 = bf16[256,4,576]{0,2,1:T(8,128)(2,1)S(1)} all-to-all(bf16[256,4,576]{0,2,1:T(8,128)(2,1)S(1)} %pad_maximum_fusion.1), channel_id=1, replica_groups=mesh['seq'=8,'batch'=4] {'batch'}, dimensions={1} | all-to-all | bytes 2359296 | tf_op jit(solution)/shard_map/all_to_all | solution.py:146
  500.8 25.9 %all-to-all-done.12 = bf16[256,4,1152]{2,0,1:T(8,128)(2,1)S(1)} async-done(((bf16[256,4,1152]{2,0,1:T(8,128)(2,1)}), bf16[256,4,1152]{2,0,1:T(8,128)(2,1)S(1)}, u32[]{:S(2)}, u32[]{:S(2)}) %all-to-all-start.12) | async-done | bytes 2359328 | tf_op jit(solution)/shard_map/all_to_all | solution.py:146
  526.7 7.3 fusion.48
  537.0 69.1 %all_to_all.234 = bf16[256,8,576]{0,2,1:T(8,128)(2,1)S(1)} all-to-all(bf16[256,8,576]{0,2,1:T(8,128)(2,1)S(1)} %bitcast.207), channel_id=1, replica_groups=mesh['seq'=8,'batch'=4] {'seq'}, dimensions={1} | all-to-all | bytes 4718592 | tf_op jit(solution)/shard_map/all_to_all | solution.py:140
  607.9 8.8 %fusion.73 = f32[1152,576]{1,0:T(8,128)} fusion(bf16[2048,1152]{1,0:T(8,128)(2,1)} %all-gather.13.cloned.1.call-done, bf16[2048,576]{0,1:T(8,128)(2,1)} %bitcast.222), kind=kOutput, calls=%fused_computation.130 | convolution fusion | flops 2717908992 | bytes 9732096 | tf_op jit(solution)/shard_map/dot_general | solution.py:19
  616.8 9.1 %fusion.47 = bf16[1,256,1152]{2,1,0:T(8,128)(2,1)} fusion(f32[256,1152]{1,0:T(8,128)S(1)} %copy-done.8, bf16[256,4608]{1,0:T(8,128)(2,1)} %get-tuple-element.297, bf16[4608,1152]{1,0:T(8,128)(2,1)} %param.35, f32[1152]{0:T(1024)S(1)} %convert_element_type.106), kind=kOutput, calls=%fused_computation.77 | convolution fusion | flops 2718793728 | bytes 14750208 | tf_op jit(solution)/shard_map/dot_general | solution.py:15
  626.0 41.3 %all-reduce = (f32[1152]{0:T(1024)}, f32[1152]{0:T(1024)}, f32[1152]{0:T(1024)}, f32[1152]{0:T(1024)}, f32[1152]{0:T(1024)}, /*index=5*/f32[1152]{0:T(1024)}, f32[4608]{0:T(1024)}, f32[1152]{0:T(1024)}) all-reduce(f32[1152]{0:T(1024)S(1)} %get-tuple-element.291, ...), channel_id=1, replica_groups=mesh['seq'=8,'batch'=4] {'seq','batch'}, use_global_device_ids=true, to_apply=%region_19.20 | all-reduce | flops 12672 | bytes 101376 | tf_op jit(solution)/shard_map/psum | solution.py:248
  673.2 59.5 %reduce-scatter.14.cloned.1.call-done = f32[1152,144]{0,1:T(8,128)} async-done(((f32[1152,1152]{0,1:T(8,128)}), f32[1152,144]{0,1:T(8,128)}) %reduce-scatter.14.cloned.1.call-update) | async-done | bytes 663568 | tf_op jit(solution)/shard_map/reduce_scatter | solution.py:149
  732.7 44.3 %reduce-scatter.12.cloned.1.call-done = f32[288,576]{1,0:T(8,128)} async-done(((f32[1152,576]{1,0:T(8,128)}), f32[288,576]{1,0:T(8,128)}) %reduce-scatter.12.cloned.1.call-update) | async-done | bytes 663568 | tf_op jit(solution)/shard_map/reduce_scatter | solution.py:142
  (313 shorter events, 278.0 us)
Async XLA Ops:
  7.2 153.1 %copy-start = (bf16[1152,1152]{1,0:T(8,128)(2,1)S(1)}, bf16[1152,1152]{1,0:T(8,128)(2,1)}, u32[]{:S(2)}) copy-start(bf16[1152,1152]{1,0:T(8,128)(2,1)} %param.29) | copy-start | bytes 7962628
  25.8 23.2 %all-to-all-start = ((bf16[256,8,144]{0,2,1:T(8,128)(2,1)}), bf16[256,8,144]{0,2,1:T(8,128)(2,1)}, u32[]{:S(2)}, u32[]{:S(2)}) async-start(bf16[256,8,144]{0,2,1:T(8,128)(2,1)} %bitcast.227), calls=%async_computation | async-start | bytes 1179648 | tf_op jit(solution)/shard_map/all_to_all | solution.py:194
  49.0 20.9 %all-to-all-start.1 = ((bf16[256,8,144]{0,2,1:T(8,128)(2,1)}), bf16[256,8,144]{0,2,1:T(8,128)(2,1)}, u32[]{:S(2)}, u32[]{:S(2)}) async-start(bf16[256,8,144]{0,2,1:T(8,128)(2,1)} %bitcast.226), calls=%async_computation.1 | async-start | bytes 1179648 | tf_op jit(solution)/shard_map/all_to_all | solution.py:195
  70.0 21.2 %all-to-all-start.2 = ((bf16[256,8,144]{0,2,1:T(8,128)(2,1)}), bf16[256,8,144]{0,2,1:T(8,128)(2,1)}, u32[]{:S(2)}, u32[]{:S(2)}) async-start(bf16[256,8,144]{0,2,1:T(8,128)(2,1)} %bitcast.223), calls=%async_computation.2 | async-start | bytes 1179648 | tf_op jit(solution)/shard_map/all_to_all | solution.py:196
  139.3 20.9 %all-to-all-start.3 = ((bf16[8,256,144]{1,2,0:T(8,128)(2,1)}), bf16[8,256,144]{1,2,0:T(8,128)(2,1)}, u32[]{:S(2)}, u32[]{:S(2)}) async-start(bf16[8,256,144]{1,2,0:T(8,128)(2,1)} %copy.116), calls=%async_computation.3 | async-start | bytes 1179648 | tf_op jit(solution)/shard_map/all_to_all | solution.py:200
  143.5 274.6 %all-gather.11.cloned.1.call-start = ((), (), s32[]{:S(2)}) async-start(), calls=%async_computation.22 | async-start | bytes 2949120 | tf_op jit(solution)/shard_map/all_gather | solution.py:147
  213.6 20.2 %all-to-all-start.4 = ((bf16[256,8,144]{0,2,1:T(8,128)(2,1)}), bf16[256,8,144]{0,2,1:T(8,128)(2,1)S(1)}, u32[]{:S(2)}, u32[]{:S(2)}) async-start(bf16[256,8,144]{0,2,1:T(8,128)(2,1)} %bitcast.19), calls=%async_computation.4 | async-start | bytes 1179648 | tf_op jit(solution)/shard_map/all_to_all | solution.py:226
  217.2 244.2 %all-gather.9.cloned.1.call-start = ((), (), s32[]{:S(2)}) async-start(), calls=%async_computation.20 | async-start | bytes 5308416 | tf_op jit(solution)/shard_map/all_gather | solution.py:139
  326.3 20.3 %all-to-all-start.7 = ((bf16[8,256,144]{1,2,0:T(8,128)(2,1)}), bf16[8,256,144]{1,2,0:T(8,128)(2,1)S(1)}, u32[]{:S(2)}, u32[]{:S(2)}) async-start(bf16[8,256,144]{1,2,0:T(8,128)(2,1)} %copy.124), calls=%async_computation.7 | async-start | bytes 1179648 | tf_op jit(solution)/shard_map/all_to_all | solution.py:235
  330.2 55.9 %copy-start.10 = (f32[256,1152]{1,0:T(8,128)S(1)}, f32[256,1152]{1,0:T(8,128)}, u32[]{:S(2)}) copy-start(f32[256,1152]{1,0:T(8,128)} %copy-done.9) | copy-start | bytes 3538948
  330.2 55.9 %copy-start.29 = (f32[1152]{0:T(1024)S(1)}, f32[1152]{0:T(1024)}, u32[]{:S(2)}) copy-start(f32[1152]{0:T(1024)} %copy-done.28) | copy-start | bytes 13828
  346.6 20.2 %all-to-all-start.6 = ((bf16[8,256,144]{1,2,0:T(8,128)(2,1)}), bf16[8,256,144]{1,2,0:T(8,128)(2,1)S(1)}, u32[]{:S(2)}, u32[]{:S(2)}) async-start(bf16[8,256,144]{1,2,0:T(8,128)(2,1)} %copy.123), calls=%async_computation.6 | async-start | bytes 1179648 | tf_op jit(solution)/shard_map/all_to_all | solution.py:234
  350.1 137.9 %all-gather.7.cloned.1.call-start = ((), (), s32[]{:S(2)}) async-start(), calls=%async_computation.18 | async-start | bytes 2949120 | tf_op jit(solution)/shard_map/all_gather | solution.py:147
  395.1 105.7 %all-gather.15.cloned.1.call-start = ((), (), s32[]{:S(2)}) async-start(), calls=%async_computation.27 | async-start | bytes 2949120 | tf_op jit(solution)/shard_map/all_gather | solution.py:147
  395.7 212.2 %all-gather.13.cloned.1.call-start = ((), (), s32[]{:S(2)}) async-start(), calls=%async_computation.24 | async-start | bytes 5308416 | tf_op jit(solution)/shard_map/all_gather | solution.py:139
  396.3 18.0 %all-to-all-start.10 = ((bf16[256,4,288]{0,2,1:T(8,128)(2,1)}), bf16[256,4,288]{0,2,1:T(8,128)(2,1)S(1)}, u32[]{:S(2)}, u32[]{:S(2)}) async-start(bf16[256,4,288]{0,2,1:T(8,128)(2,1)} %bitcast.34), calls=%async_computation.12 | async-start | bytes 1179648 | tf_op jit(solution)/shard_map/all_to_all | solution.py:146
  414.3 45.5 %all-to-all-start.9 = ((bf16[256,8,432]{0,2,1:T(8,128)(2,1)}), bf16[256,8,432]{0,2,1:T(8,128)(2,1)S(1)}, u32[]{:S(2)}, u32[]{:S(2)}) async-start(bf16[256,8,432]{0,2,1:T(8,128)(2,1)} %bitcast.32), calls=%async_computation.10 | async-start | bytes 3538944 | tf_op jit(solution)/shard_map/all_to_all | solution.py:140
  417.9 255.3 %reduce-scatter.10.cloned.1.call-start = ((), (), s32[]{:S(2)}) async-start(), calls=%async_computation.23 | async-start | bytes 1990656 | tf_op jit(solution)/shard_map/reduce_scatter | solution.py:149
  422.8 250.4 %reduce-scatter.8.cloned.1.call-start = ((), (), s32[]{:S(2)}) async-start(), calls=%async_computation.21 | async-start | bytes 2949120 | tf_op jit(solution)/shard_map/reduce_scatter | solution.py:142
  468.5 204.7 %reduce-scatter.6.cloned.1.call-start = ((), (), s32[]{:S(2)}) async-start(), calls=%async_computation.19 | async-start | bytes 3317760 | tf_op jit(solution)/shard_map/reduce_scatter | solution.py:149
  496.9 29.9 %all-to-all-start.12 = ((bf16[256,4,1152]{2,0,1:T(8,128)(2,1)}), bf16[256,4,1152]{2,0,1:T(8,128)(2,1)S(1)}, u32[]{:S(2)}, u32[]{:S(2)}) async-start(bf16[256,4,1152]{2,0,1:T(8,128)(2,1)} %bitcast.165), calls=%async_computation.16 | async-start | bytes 4718592 | tf_op jit(solution)/shard_map/all_to_all | solution.py:146
  500.5 232.2 %reduce-scatter.14.cloned.1.call-start = ((), (), s32[]{:S(2)}) async-start(), calls=%async_computation.26 | async-start | bytes 5971968 | tf_op jit(solution)/shard_map/reduce_scatter | solution.py:149
  534.1 242.8 %reduce-scatter.12.cloned.1.call-start = ((), (), s32[]{:S(2)}) async-start(), calls=%async_computation.25 | async-start | bytes 3686400 | tf_op jit(solution)/shard_map/reduce_scatter | solution.py:142
  667.2 109.7 %copy-start.1 = (bf16[1152,1152]{1,0:T(8,128)(2,1)S(1)}, bf16[1152,1152]{1,0:T(8,128)(2,1)}, u32[]{:S(2)}) copy-start(bf16[1152,1152]{1,0:T(8,128)(2,1)} %param.29) | copy-start | bytes 7962628
  (60 other events, 563.2 us)
Sparse Core Ops, SparseCore 0:
  208.7 36.2 all-gather.10
  246.6 51.1 all-gather.8
  395.2 38.5 all-gather.6
  435.5 37.3 all-gather.14
  474.9 51.1 all-gather.12
  528.9 41.3 reduce-scatter.9
  573.9 53.2 reduce-scatter.7
  630.1 40.1 reduce-scatter.5
  673.1 59.5 reduce-scatter.13
  736.2 40.7 reduce-scatter.11

commit v2 on v1

--- a/solution.py
+++ b/solution.py
@@ -135,15 +135,34 @@
     return (grad_query.reshape(length, head_cols), grad_keys, grad_values)
 
 
+def exchange(blocks, axis):
+    count = blocks.shape[0]
+    me = lax.axis_index(axis)
+    got = [lax.dynamic_index_in_dim(blocks, me, axis=0, keepdims=False)]
+    for step in range(1, count):
+        piece = lax.dynamic_index_in_dim(blocks, (me + step) % count, axis=0, keepdims=False)
+        pairs = [(source, (source + step) % count) for source in range(count)]
+        got.append(lax.ppermute(piece, axis, pairs))
+    order = (me - jnp.arange(count)) % count
+    return jnp.take(jnp.stack(got), order, axis=0)
+
+
+def split_columns(values, axis):
+    count = lax.axis_size(axis)
+    rows, cols = values.shape
+    blocks = values.reshape(rows, count, cols // count).transpose(1, 0, 2)
+    return exchange(blocks, axis).reshape(count * rows, cols // count)
+
+
 def seq_gathered_grad(left, right):
     left_all = lax.all_gather(left, "seq", axis=0, tiled=True)
-    right_cols = lax.all_to_all(right, "seq", split_axis=1, concat_axis=0, tiled=True)
+    right_cols = split_columns(right, "seq")
     partial = contract_rows(left_all, right_cols)
     return lax.psum_scatter(partial, "batch", scatter_dimension=0, tiled=True)
 
 
 def batch_gathered_grad(left, right):
-    left_rows = lax.all_to_all(left, "batch", split_axis=1, concat_axis=0, tiled=True)
+    left_rows = split_columns(left, "batch")
     right_all = lax.all_gather(right, "batch", axis=0, tiled=True)
     partial = contract_rows(left_rows, right_all)
     return lax.psum_scatter(partial, "seq", scatter_dimension=1, tiled=True)
@@ -187,14 +206,17 @@
     )
     normed_one = normed_full.astype(jnp.bfloat16)
     packed = product(normed_one, qkv_weight).astype(jnp.bfloat16)
-    query_tok = packed[:, :feature_count]
-    key_tok = packed[:, feature_count : 2 * feature_count]
-    value_tok = packed[:, 2 * feature_count :]
-    query_heads, key_heads, value_heads = (
-        lax.all_to_all(query_tok, "seq", split_axis=1, concat_axis=0, tiled=True),
-        lax.all_to_all(key_tok, "seq", split_axis=1, concat_axis=0, tiled=True),
-        lax.all_to_all(value_tok, "seq", split_axis=1, concat_axis=0, tiled=True),
-    )
+    seq_count = lax.axis_size("seq")
+    packed_heads = lax.all_to_all(
+        packed.reshape(local_rows, 3, seq_count, feature_count // seq_count),
+        "seq",
+        split_axis=2,
+        concat_axis=0,
+        tiled=True,
+    ).reshape(group_len, 3, feature_count // seq_count)
+    query_heads = packed_heads[:, 0]
+    key_heads = packed_heads[:, 1]
+    value_heads = packed_heads[:, 2]
     segment = segments(lengths[0], group_len)
     context_heads, log_total = attend_forward(query_heads, key_heads, value_heads, segment)
     context_tok = lax.all_to_all(context_heads, "seq", split_axis=0, concat_axis=1, tiled=True)
@@ -229,12 +251,13 @@
     grad_query, grad_key, grad_value = attend_backward(
         query_heads, key_heads, value_heads, segment, grad_context_heads, log_total
     )
-    grad_query_tok, grad_key_tok, grad_value_tok = (
-        lax.all_to_all(grad_query, "seq", split_axis=0, concat_axis=1, tiled=True),
-        lax.all_to_all(grad_key, "seq", split_axis=0, concat_axis=1, tiled=True),
-        lax.all_to_all(grad_value, "seq", split_axis=0, concat_axis=1, tiled=True),
-    )
-    grad_packed = jnp.concatenate([grad_query_tok, grad_key_tok, grad_value_tok], axis=1)
+    grad_packed = lax.all_to_all(
+        jnp.stack([grad_query, grad_key, grad_value], axis=1)[:, :, None],
+        "seq",
+        split_axis=0,
+        concat_axis=2,
+        tiled=True,
+    ).reshape(local_rows, 3 * feature_count)
     grad_qkv_weight = weight_grad("qkv", normed_one, grad_packed)
     grad_normed_one = times_transposed(grad_packed, qkv_weight)
     grad_mixed_norm, grad_attention_gain, grad_attention_shift = first_pull(grad_normed_one)
@@ -245,19 +268,23 @@
     grad_tokens = grad_joined[:, :feature_count][None]
     grad_long_skip = grad_joined[:, feature_count:][None]
     summed_weights = (grad_skip_weight, grad_qkv_weight, grad_out_weight, grad_hidden_weight, grad_down_weight)
-    summed_small = lax.psum(
-        (
-            grad_skip_bias,
-            grad_attention_gain,
-            grad_attention_shift,
-            grad_out_bias,
-            grad_mlp_gain,
-            grad_mlp_shift,
-            grad_hidden_bias,
-            grad_down_bias,
-        ),
-        ("seq", "batch"),
-    )
+    small_grads = (
+        grad_skip_bias,
+        grad_attention_gain,
+        grad_attention_shift,
+        grad_out_bias,
+        grad_mlp_gain,
+        grad_mlp_shift,
+        grad_hidden_bias,
+        grad_down_bias,
+    )
+    small_sizes = [piece.shape[0] for piece in small_grads]
+    small_total = lax.psum(jnp.concatenate(small_grads), ("seq", "batch"))
+    summed_small = []
+    offset = 0
+    for size in small_sizes:
+        summed_small.append(small_total[offset : offset + size])
+        offset += size
     return (
         output[None],
         grad_tokens,

time: 791 us -> 820 us (1.037)
  blocking collectives: 148 us -> 64.8 us
  starting transfers between devices: 42 us -> 115 us
  local copies, waits for them, and re-layouts: 60.2 us -> 120 us
  waiting for transfers between devices: 279 us -> 246 us
  matrix products: 197 us -> 208 us
    all_to_all x3 -> x0, blocking collectives: 106 us -> none  [the longest x1 69.1 us: seq_gathered_grad(): lax.all_to_all(right, 'seq', split_axis=1, concat_axis=0, tiled=True)]
    ppermute x0 -> x23, waiting for transfers between devices: none -> 97.9 us  [exchange(): got.append(lax.ppermute(piece, axis, pairs))]
    ppermute x0 -> x23, starting transfers between devices: none -> 94.7 us  [exchange(): got.append(lax.ppermute(piece, axis, pairs))]
    reduce_scatter x3, waiting for transfers between devices: 59.5 us -> 0.02 us  [batch_gathered_grad(): return lax.psum_scatter(partial, 'seq', scatter_dimension=1, tiled=True)]
    all_to_all x8 -> x2, waiting for transfers between devices: 141 us -> 82.9 us  [the longest x1 41.7 us: on_device(): lax.all_to_all(packed.reshape(local_rows, 3, seq_count, feature_count //...]
    unnamed x85 -> x100, local copies, waits for them, and re-layouts: 8.97 us -> 33.6 us
    psum x1, blocking collectives: 41.3 us -> 64.8 us  [on_device(): small_total = lax.psum(jnp.concatenate(small_grads), ('seq', 'batch'))]
    all_to_all x8 -> x2, starting transfers between devices: 33 us -> 10.6 us  [the longest x1 6.83 us: on_device(): lax.all_to_all(packed.reshape(local_rows, 3, seq_count, feature_count //...]
  transfers between devices with their start and end apart: 20 -> 37, of which waited for: 12 -> 19; matrix products, arithmetic and copies ran while one was open for 23% -> 30% of each run, Pallas kernels for 0% -> 0%
where the time goes in v2:
time: 820 us; the launch traced here: 814 us
  waiting for transfers between devices  246 us (30%)
  matrix products  208 us (25%)
  local copies, waits for them, and re-layouts  120 us (15%)
  starting transfers between devices  115 us (14%)
  blocking collectives  64.8 us (8%)
  other arithmetic  43.7 us (5%)
  between operations  15.3 us (2%)
    ppermute x23, waiting for transfers between devices, exchange(): got.append(lax.ppermute(piece, axis, pairs))  97.9 us
    ppermute x23, starting transfers between devices, exchange(): got.append(lax.ppermute(piece, axis, pairs))  94.7 us
    psum x1, blocking collectives, on_device(): small_total = lax.psum(jnp.concatenate(small_grads), ('seq', 'batch'))  64.8 us
    all_to_all x1, waiting for transfers between devices, on_device(): lax.all_to_all(packed.reshape(local_rows, 3, seq_count, feature_count //...  41.7 us
    all_to_all x1, waiting for transfers between devices, on_device(): lax.all_to_all(jnp.stack([grad_query, grad_key, grad_value], axis=1)[:, :...  41.1 us
    dot_general x5, matrix products, product(): return jnp.dot(left, right, preferred_element_type=jnp.float32)  40.5 us
    dot_general x5, matrix products, times_transposed(): lax.dot_general(left, right, (((1,), (1,)), ((), ())), preferred_element_...  37.6 us
    unnamed x100, local copies, waits for them, and re-layouts  33.6 us
  transfers between devices with their start and end apart: 37, of which 19 were waited for; matrix products, arithmetic and copies ran while one was open for 30% of the time, Pallas kernels for 0%

profile of v2, /device:TPU:0, one launch (start us, length us, event | category | flops | bytes accessed | tf_op | source)
XLA Modules:
  0.0 813.6 jit_solution(7529825776939285861)
XLA Ops:
  14.6 7.2 convolution_convert_fusion
  35.6 41.7 %all-to-all-done = bf16[256,3,8,144]{0,3,1,2:T(8,128)(2,1)} async-done(((bf16[256,3,8,144]{0,3,1,2:T(8,128)(2,1)}), bf16[256,3,8,144]{0,3,1,2:T(8,128)(2,1)}, u32[]{:S(2)}, u32[]{:S(2)}) %all-to-all-start) | async-done | bytes 1769504 | tf_op jit(solution)/shard_map/all_to_all | solution.py:210
  92.6 36.5 %while.27 = (s32[]{:T(128)}, bf16[4,512,144]{1,2,0:T(8,128)(2,1)}, f32[4,2,512,1]{2,1,3,0:T(2,128)S(1)}, s32[4,512]{1,0:T(4,128)S(1)}, s32[2048]{0:T(1024)S(1)},...) while((s32[]{:T(128)}, bf16[4,512,144]{1,2,0:T(8,128)(2,1)}, ...), condition=%wide.region_7.8_spmd, body=%wide.region_4.7_spmd.sunk | while | flops 628169728 | bytes 33537152 | solution.py:77
  140.6 16.1 %all-to-all-done.1 = bf16[8,256,144]{1,2,0:T(8,128)(2,1)} async-done(((bf16[8,256,144]{1,2,0:T(8,128)(2,1)}), bf16[8,256,144]{1,2,0:T(8,128)(2,1)}, u32[]{:S(2)}, u32[]{:S(2)}) %all-to-all-start.1) | async-done | bytes 589856 | tf_op jit(solution)/shard_map/all_to_all | solution.py:222
  161.4 17.1 %multiply_convert_fusion.1 = (bf16[256,4608]{1,0:T(8,128)(2,1)}, f32[256,4608]{1,0:T(8,128)}, f32[256,4608]{1,0:T(8,128)}) fusion(f32[4608]{0:T(1024)S(1)} %convert_element_type.104, bf16[256,1152]{1,0:T(8,128)(2,1)} %add_convert_fusion.2, bf16[1152,4608]{1,0:T(8,128)(2,1)} %param.33), kind=kOutput, calls=%fused_computation.61 | convolution fusion | flops 2795765760 | bytes 23021568 | tf_op jit(solution)/shard_map/dot_general | solution.py:15
  178.5 14.6 %convert_reduce_fusion = (f32[4608]{0:T(1024)}, bf16[256,4608]{1,0:T(8,128)(2,1)}) fusion(f32[256,4608]{1,0:T(8,128)} %get-tuple-element.309, f32[256,4608]{1,0:T(8,128)} %get-tuple-element.357, bf16[4608,1152]{1,0:T(8,128)(2,1)} %param.35, bf16[1,256,1152]{2,1,0:T(8,128)(2,1)S(1)} %copy-done.13), kind=kOutput, calls=%fused_computation.59 | convolution fusion | flops 2736778752 | bytes 23021568 | tf_op jit(solution)/shard_map/dot_general | solution.py:25
  193.2 8.7 %multiply_reduce_fusion.1 = (f32[1152]{0:T(1024)}, f32[256]{0:T(256)S(1)}, f32[1152]{0:T(1024)}, f32[256,1152]{1,0:T(8,128)S(1)}) fusion(f32[256,1152]{1,0:T(8,128)S(1)} %copy-done.7, f32[256]{0:T(256)S(1)} %fusion.83, f32[256]{0:T(256)S(1)} %broadcast_multiply_fusion, f32[1152]{0:T(1024)S(1)} %convert_element_type.101, ...), kind=kOutput, calls=%fused_computation.113 | convolution fusion | flops 2720265728 | bytes 15352320 | tf_op jit(solution)/shard_map/dot_general | solution.py:25
  214.5 15.9 %all-to-all-done.2 = bf16[256,8,144]{0,2,1:T(8,128)(2,1)S(1)} async-done(((bf16[256,8,144]{0,2,1:T(8,128)(2,1)}), bf16[256,8,144]{0,2,1:T(8,128)(2,1)S(1)}, u32[]{:S(2)}, u32[]{:S(2)}) %all-to-all-start.2) | async-done | bytes 589856 | tf_op jit(solution)/shard_map/all_to_all | solution.py:248
  232.7 96.8 %while.28 = (s32[]{:T(128)}, f32[2048,2,72]{0,2,1:T(8,128)S(1)}, f32[2048,2,72]{0,2,1:T(8,128)}, bf16[4,512,144]{1,2,0:T(8,128)(2,1)}, bf16[4,512,2,72]{1,3,2,0:...) while((s32[]{:T(128)}, f32[2048,2,72]{0,2,1:T(8,128)S(1)}, ...), condition=%wide.region_14.15_spmd.clone, body=%wide.region_12.14_spmd.clone.sunk | while | flops 1543781376 | bytes 144143088 | solution.py:123
  337.9 8.6 %reshape.483 = bf16[8,2,55296]{2,1,0:T(2,128)(2,1)} reshape(bf16[2048,1,3,144]{3,2,1,0:T(4,128)(2,1)} %bitcast.291) | data formatting | bytes 3538944
  351.0 41.1 %all-to-all-done.3 = bf16[8,2,55296]{2,1,0:T(2,128)(2,1)S(1)} async-done(((bf16[8,2,55296]{2,1,0:T(2,128)(2,1)}), bf16[8,2,55296]{2,1,0:T(2,128)(2,1)S(1)}, u32[]{:S(2)}, u32[]{:S(2)}) %all-to-all-start.3) | async-done | bytes 1769504 | tf_op jit(solution)/shard_map/all_to_all | solution.py:254
  457.0 22.1 %collective-permute-done.5 = bf16[256,432]{0,1:T(8,128)(2,1)S(1)} collective-permute-done((bf16[256,432]{0,1:T(8,128)(2,1)S(1)}, bf16[256,432]{0,1:T(8,128)(2,1)S(1)}, u32[]{:S(2)}, u32[]{:S(2)}) %collective-permute-start.5) | collective-permute-done | bytes 221216 | tf_op jit(solution)/shard_map/ppermute | solution.py:145
  525.0 8.0 fusion.48
  555.5 13.3 %collective-permute-start.13 = (bf16[256,576]{0,1:T(8,128)(2,1)S(1)}, bf16[256,576]{0,1:T(8,128)(2,1)S(1)}, u32[]{:S(2)}, u32[]{:S(2)}) collective-permute-start(bf16[256,576]{0,1:T(8,128)(2,1)S(1)} %get-tuple-element.324), channel_id=1, source_target_pairs={{0,4},{4,8},{8,12},{12,16},{16,20},{20,24},{24,28},{28,0},{1,5},{5... | collective-permute-start | bytes 884744 | tf_op jit(solution)/shard_map/ppermute | solution.py:145
  568.8 37.8 %collective-permute-start.14 = (bf16[256,576]{0,1:T(8,128)(2,1)S(1)}, bf16[256,576]{0,1:T(8,128)(2,1)S(1)}, u32[]{:S(2)}, u32[]{:S(2)}) collective-permute-start(bf16[256,576]{0,1:T(8,128)(2,1)S(1)} %get-tuple-element.323), channel_id=1, source_target_pairs={{0,8},{4,12},{8,16},{12,20},{16,24},{20,28},{24,0},{28,4},{1,9},{5... | collective-permute-start | bytes 884744 | tf_op jit(solution)/shard_map/ppermute | solution.py:145
  607.4 9.8 %collective-permute-start.15 = (bf16[256,576]{0,1:T(8,128)(2,1)S(1)}, bf16[256,576]{0,1:T(8,128)(2,1)S(1)}, u32[]{:S(2)}, u32[]{:S(2)}) collective-permute-start(bf16[256,576]{0,1:T(8,128)(2,1)S(1)} %get-tuple-element.322), channel_id=1, source_target_pairs={{0,12},{4,16},{8,20},{12,24},{16,28},{20,0},{24,4},{28,8},{1,13},{... | collective-permute-start | bytes 884744 | tf_op jit(solution)/shard_map/ppermute | solution.py:145
  623.0 9.8 %collective-permute-start.19 = (bf16[256,576]{0,1:T(8,128)(2,1)S(1)}, bf16[256,576]{0,1:T(8,128)(2,1)S(1)}, u32[]{:S(2)}, u32[]{:S(2)}) collective-permute-start(bf16[256,576]{0,1:T(8,128)(2,1)S(1)} %get-tuple-element.318), channel_id=1, source_target_pairs={{0,28},{4,0},{8,4},{12,8},{16,12},{20,16},{24,20},{28,24},{1,29},{... | collective-permute-start | bytes 884744 | tf_op jit(solution)/shard_map/ppermute | solution.py:145
  634.2 17.3 %collective-permute-done.16 = bf16[256,576]{0,1:T(8,128)(2,1)S(1)} collective-permute-done((bf16[256,576]{0,1:T(8,128)(2,1)S(1)}, bf16[256,576]{0,1:T(8,128)(2,1)S(1)}, u32[]{:S(2)}, u32[]{:S(2)}) %collective-permute-start.16) | collective-permute-done | bytes 294944 | tf_op jit(solution)/shard_map/ppermute | solution.py:145
  655.5 11.4 %collective-permute-done.18 = bf16[256,576]{0,1:T(8,128)(2,1)S(1)} collective-permute-done((bf16[256,576]{0,1:T(8,128)(2,1)S(1)}, bf16[256,576]{0,1:T(8,128)(2,1)S(1)}, u32[]{:S(2)}, u32[]{:S(2)}) %collective-permute-start.18) | collective-permute-done | bytes 294944 | tf_op jit(solution)/shard_map/ppermute | solution.py:145
  667.7 10.9 %collective-permute-done.19 = bf16[256,576]{0,1:T(8,128)(2,1)S(1)} collective-permute-done((bf16[256,576]{0,1:T(8,128)(2,1)S(1)}, bf16[256,576]{0,1:T(8,128)(2,1)S(1)}, u32[]{:S(2)}, u32[]{:S(2)}) %collective-permute-start.19) | collective-permute-done | bytes 294944 | tf_op jit(solution)/shard_map/ppermute | solution.py:145
  683.5 8.6 %fusion.50 = f32[1152,576]{1,0:T(8,128)} fusion(bf16[2048,1152]{1,0:T(8,128)(2,1)} %all-gather.13.cloned.1.call-done, bf16[2048,576]{0,1:T(8,128)(2,1)} %bitcast.307, pred[2048]{0:T(1024)(128)(4,1)S(1)} %broadcast_in_dim.155), kind=kOutput, calls=%fused_computation.87 | convolution fusion | flops 2719088640 | bytes 9734144 | tf_op jit(solution)/shard_map/dot_general | solution.py:19
  693.4 8.9 %fusion.47 = bf16[1,256,1152]{2,1,0:T(8,128)(2,1)} fusion(f32[256,1152]{1,0:T(8,128)S(1)} %copy-done.8, bf16[256,4608]{1,0:T(8,128)(2,1)} %get-tuple-element.308, bf16[4608,1152]{1,0:T(8,128)(2,1)} %param.35, f32[1152]{0:T(1024)S(1)} %convert_element_type.106), kind=kOutput, calls=%fused_computation.82 | convolution fusion | flops 2718793728 | bytes 14750208 | tf_op jit(solution)/shard_map/dot_general | solution.py:15
  702.5 64.8 %psum.7 = f32[12672]{0:T(1024)S(1)} all-reduce(f32[12672]{0:T(1024)S(1)} %constant_dynamic-update-slice_fusion.1), channel_id=1, replica_groups=mesh['seq'=8,'batch'=4] {'seq','batch'}, use_global_device_ids=true, to_apply=%region_26.27 | all-reduce | flops 12672 | bytes 101376 | tf_op jit(solution)/shard_map/psum | solution.py:282
  774.8 31.7 %reduce-scatter.12.cloned.1.call-done = f32[288,576]{1,0:T(8,128)} async-done(((f32[1152,576]{1,0:T(8,128)}), f32[288,576]{1,0:T(8,128)}) %reduce-scatter.12.cloned.1.call-update) | async-done | bytes 663568 | tf_op jit(solution)/shard_map/reduce_scatter | solution.py:161
  (369 shorter events, 372.3 us)
Async XLA Ops:
  28.5 48.9 %all-to-all-start = ((bf16[256,3,8,144]{0,3,1,2:T(8,128)(2,1)}), bf16[256,3,8,144]{0,3,1,2:T(8,128)(2,1)}, u32[]{:S(2)}, u32[]{:S(2)}) async-start(bf16[256,3,8,144]{0,3,1,2:T(8,128)(2,1)} %copy.125), calls=%async_computation | async-start | bytes 3538944 | tf_op jit(solution)/shard_map/all_to_all | solution.py:210
  140.0 290.8 %all-gather.11.cloned.1.call-start = ((), (), s32[]{:S(2)}) async-start(), calls=%async_computation.13 | async-start | bytes 2949120 | tf_op jit(solution)/shard_map/all_gather | solution.py:166
  213.7 272.6 %all-gather.9.cloned.1.call-start = ((), (), s32[]{:S(2)}) async-start(), calls=%async_computation.11 | async-start | bytes 5308416 | tf_op jit(solution)/shard_map/all_gather | solution.py:158
  346.4 45.7 %all-to-all-start.3 = ((bf16[8,2,55296]{2,1,0:T(2,128)(2,1)}), bf16[8,2,55296]{2,1,0:T(2,128)(2,1)S(1)}, u32[]{:S(2)}, u32[]{:S(2)}) async-start(bf16[8,2,55296]{2,1,0:T(2,128)(2,1)} %reshape.483), calls=%async_computation.3 | async-start | bytes 3538944 | tf_op jit(solution)/shard_map/all_to_all | solution.py:254
  350.3 174.7 %all-gather.15.cloned.1.call-start = ((), (), s32[]{:S(2)}) async-start(), calls=%async_computation.18 | async-start | bytes 2949120 | tf_op jit(solution)/shard_map/all_gather | solution.py:166
  351.0 195.8 %all-gather.7.cloned.1.call-start = ((), (), s32[]{:S(2)}) async-start(), calls=%async_computation.9 | async-start | bytes 2949120 | tf_op jit(solution)/shard_map/all_gather | solution.py:166
  415.2 268.3 %all-gather.13.cloned.1.call-start = ((), (), s32[]{:S(2)}) async-start(), calls=%async_computation.15 | async-start | bytes 5308416 | tf_op jit(solution)/shard_map/all_gather | solution.py:158
  415.8 359.0 %reduce-scatter.10.cloned.1.call-start = ((), (), s32[]{:S(2)}) async-start(), calls=%async_computation.14 | async-start | bytes 1990656 | tf_op jit(solution)/shard_map/reduce_scatter | solution.py:168
  435.3 339.6 %reduce-scatter.8.cloned.1.call-start = ((), (), s32[]{:S(2)}) async-start(), calls=%async_computation.12 | async-start | bytes 2949120 | tf_op jit(solution)/shard_map/reduce_scatter | solution.py:161
  442.7 36.4 %collective-permute-start.5 = (bf16[256,432]{0,1:T(8,128)(2,1)S(1)}, bf16[256,432]{0,1:T(8,128)(2,1)S(1)}, u32[]{:S(2)}, u32[]{:S(2)}) collective-permute-start(bf16[256,432]{0,1:T(8,128)(2,1)S(1)} %get-tuple-element.331), channel_id=1, source_target_pairs={{0,12},{4,16},{8,20},{12,24},{16,28},{20,0},{24,4},{28,8},{1,13},{... | collective-permute-start | bytes 663560 | tf_op jit(solution)/shard_map/ppermute | solution.py:145
  443.1 36.8 %collective-permute-start.6 = (bf16[256,432]{0,1:T(8,128)(2,1)S(1)}, bf16[256,432]{0,1:T(8,128)(2,1)S(1)}, u32[]{:S(2)}, u32[]{:S(2)}) collective-permute-start(bf16[256,432]{0,1:T(8,128)(2,1)S(1)} %get-tuple-element.330), channel_id=1, source_target_pairs={{0,16},{4,20},{8,24},{12,28},{16,0},{20,4},{24,8},{28,12},{1,17},{... | collective-permute-start | bytes 663560 | tf_op jit(solution)/shard_map/ppermute | solution.py:145
  446.8 33.7 %collective-permute-start.7 = (bf16[256,432]{0,1:T(8,128)(2,1)S(1)}, bf16[256,432]{0,1:T(8,128)(2,1)S(1)}, u32[]{:S(2)}, u32[]{:S(2)}) collective-permute-start(bf16[256,432]{0,1:T(8,128)(2,1)S(1)} %get-tuple-element.329), channel_id=1, source_target_pairs={{0,20},{4,24},{8,28},{12,0},{16,4},{20,8},{24,12},{28,16},{1,21},{... | collective-permute-start | bytes 663560 | tf_op jit(solution)/shard_map/ppermute | solution.py:145
  451.7 29.5 %collective-permute-start.8 = (bf16[256,432]{0,1:T(8,128)(2,1)S(1)}, bf16[256,432]{0,1:T(8,128)(2,1)S(1)}, u32[]{:S(2)}, u32[]{:S(2)}) collective-permute-start(bf16[256,432]{0,1:T(8,128)(2,1)S(1)} %get-tuple-element.328), channel_id=1, source_target_pairs={{0,24},{4,28},{8,0},{12,4},{16,8},{20,12},{24,16},{28,20},{1,25},{... | collective-permute-start | bytes 663560 | tf_op jit(solution)/shard_map/ppermute | solution.py:145
  453.0 28.9 %collective-permute-start.9 = (bf16[256,432]{0,1:T(8,128)(2,1)S(1)}, bf16[256,432]{0,1:T(8,128)(2,1)S(1)}, u32[]{:S(2)}, u32[]{:S(2)}) collective-permute-start(bf16[256,432]{0,1:T(8,128)(2,1)S(1)} %get-tuple-element.327), channel_id=1, source_target_pairs={{0,28},{4,0},{8,4},{12,8},{16,12},{20,16},{24,20},{28,24},{1,29},{... | collective-permute-start | bytes 663560 | tf_op jit(solution)/shard_map/ppermute | solution.py:145
  493.3 281.5 %reduce-scatter.14.cloned.1.call-start = ((), (), s32[]{:S(2)}) async-start(), calls=%async_computation.17 | async-start | bytes 5971968 | tf_op jit(solution)/shard_map/reduce_scatter | solution.py:168
  533.0 241.8 %reduce-scatter.6.cloned.1.call-start = ((), (), s32[]{:S(2)}) async-start(), calls=%async_computation.10 | async-start | bytes 3317760 | tf_op jit(solution)/shard_map/reduce_scatter | solution.py:168
  552.3 254.2 %reduce-scatter.12.cloned.1.call-start = ((), (), s32[]{:S(2)}) async-start(), calls=%async_computation.16 | async-start | bytes 3686400 | tf_op jit(solution)/shard_map/reduce_scatter | solution.py:161
  555.5 64.0 %collective-permute-start.13 = (bf16[256,576]{0,1:T(8,128)(2,1)S(1)}, bf16[256,576]{0,1:T(8,128)(2,1)S(1)}, u32[]{:S(2)}, u32[]{:S(2)}) collective-permute-start(bf16[256,576]{0,1:T(8,128)(2,1)S(1)} %get-tuple-element.324), channel_id=1, source_target_pairs={{0,4},{4,8},{8,12},{12,16},{16,20},{20,24},{24,28},{28,0},{1,5},{5... | collective-permute-start | bytes 884744 | tf_op jit(solution)/shard_map/ppermute | solution.py:145
  568.8 54.2 %collective-permute-start.14 = (bf16[256,576]{0,1:T(8,128)(2,1)S(1)}, bf16[256,576]{0,1:T(8,128)(2,1)S(1)}, u32[]{:S(2)}, u32[]{:S(2)}) collective-permute-start(bf16[256,576]{0,1:T(8,128)(2,1)S(1)} %get-tuple-element.323), channel_id=1, source_target_pairs={{0,8},{4,12},{8,16},{12,20},{16,24},{20,28},{24,0},{28,4},{1,9},{5... | collective-permute-start | bytes 884744 | tf_op jit(solution)/shard_map/ppermute | solution.py:145
  607.4 26.1 %collective-permute-start.15 = (bf16[256,576]{0,1:T(8,128)(2,1)S(1)}, bf16[256,576]{0,1:T(8,128)(2,1)S(1)}, u32[]{:S(2)}, u32[]{:S(2)}) collective-permute-start(bf16[256,576]{0,1:T(8,128)(2,1)S(1)} %get-tuple-element.322), channel_id=1, source_target_pairs={{0,12},{4,16},{8,20},{12,24},{16,28},{20,0},{24,4},{28,8},{1,13},{... | collective-permute-start | bytes 884744 | tf_op jit(solution)/shard_map/ppermute | solution.py:145
  617.2 34.4 %collective-permute-start.16 = (bf16[256,576]{0,1:T(8,128)(2,1)S(1)}, bf16[256,576]{0,1:T(8,128)(2,1)S(1)}, u32[]{:S(2)}, u32[]{:S(2)}) collective-permute-start(bf16[256,576]{0,1:T(8,128)(2,1)S(1)} %get-tuple-element.321), channel_id=1, source_target_pairs={{0,16},{4,20},{8,24},{12,28},{16,0},{20,4},{24,8},{28,12},{1,17},{... | collective-permute-start | bytes 884744 | tf_op jit(solution)/shard_map/ppermute | solution.py:145
  617.2 37.6 %collective-permute-start.17 = (bf16[256,576]{0,1:T(8,128)(2,1)S(1)}, bf16[256,576]{0,1:T(8,128)(2,1)S(1)}, u32[]{:S(2)}, u32[]{:S(2)}) collective-permute-start(bf16[256,576]{0,1:T(8,128)(2,1)S(1)} %get-tuple-element.320), channel_id=1, source_target_pairs={{0,20},{4,24},{8,28},{12,0},{16,4},{20,8},{24,12},{28,16},{1,21},{... | collective-permute-start | bytes 884744 | tf_op jit(solution)/shard_map/ppermute | solution.py:145
  619.5 47.4 %collective-permute-start.18 = (bf16[256,576]{0,1:T(8,128)(2,1)S(1)}, bf16[256,576]{0,1:T(8,128)(2,1)S(1)}, u32[]{:S(2)}, u32[]{:S(2)}) collective-permute-start(bf16[256,576]{0,1:T(8,128)(2,1)S(1)} %get-tuple-element.319), channel_id=1, source_target_pairs={{0,24},{4,28},{8,0},{12,4},{16,8},{20,12},{24,16},{28,20},{1,25},{... | collective-permute-start | bytes 884744 | tf_op jit(solution)/shard_map/ppermute | solution.py:145
  623.0 55.6 %collective-permute-start.19 = (bf16[256,576]{0,1:T(8,128)(2,1)S(1)}, bf16[256,576]{0,1:T(8,128)(2,1)S(1)}, u32[]{:S(2)}, u32[]{:S(2)}) collective-permute-start(bf16[256,576]{0,1:T(8,128)(2,1)S(1)} %get-tuple-element.318), channel_id=1, source_target_pairs={{0,28},{4,0},{8,4},{12,8},{16,12},{20,16},{24,20},{28,24},{1,29},{... | collective-permute-start | bytes 884744 | tf_op jit(solution)/shard_map/ppermute | solution.py:145
  (64 other events, 677.8 us)
Sparse Core Ops, SparseCore 0:
  205.2 36.2 all-gather.10
  243.1 51.1 all-gather.8
  352.9 38.6 all-gather.14
  415.3 36.7 all-gather.6
  453.6 71.3 all-gather.12
  527.7 32.4 reduce-scatter.9
  563.9 43.4 reduce-scatter.7
  610.2 103.6 reduce-scatter.13
  716.8 44.0 reduce-scatter.5
  764.4 42.0 reduce-scatter.11

commit v3 on v2

--- a/solution.py
+++ b/solution.py
@@ -135,37 +135,20 @@
     return (grad_query.reshape(length, head_cols), grad_keys, grad_values)
 
 
-def exchange(blocks, axis):
-    count = blocks.shape[0]
-    me = lax.axis_index(axis)
-    got = [lax.dynamic_index_in_dim(blocks, me, axis=0, keepdims=False)]
-    for step in range(1, count):
-        piece = lax.dynamic_index_in_dim(blocks, (me + step) % count, axis=0, keepdims=False)
-        pairs = [(source, (source + step) % count) for source in range(count)]
-        got.append(lax.ppermute(piece, axis, pairs))
-    order = (me - jnp.arange(count)) % count
-    return jnp.take(jnp.stack(got), order, axis=0)
-
-
-def split_columns(values, axis):
-    count = lax.axis_size(axis)
-    rows, cols = values.shape
-    blocks = values.reshape(rows, count, cols // count).transpose(1, 0, 2)
-    return exchange(blocks, axis).reshape(count * rows, cols // count)
-
-
 def seq_gathered_grad(left, right):
     left_all = lax.all_gather(left, "seq", axis=0, tiled=True)
-    right_cols = split_columns(right, "seq")
-    partial = contract_rows(left_all, right_cols)
-    return lax.psum_scatter(partial, "batch", scatter_dimension=0, tiled=True)
+    right_cols = lax.all_to_all(right, "seq", split_axis=1, concat_axis=0, tiled=True)
+    partial = contract_rows(left_all, right_cols).astype(jnp.bfloat16)
+    summed = lax.psum_scatter(partial, "batch", scatter_dimension=0, tiled=True)
+    return summed.astype(jnp.float32)
 
 
 def batch_gathered_grad(left, right):
-    left_rows = split_columns(left, "batch")
+    left_rows = lax.all_to_all(left, "batch", split_axis=1, concat_axis=0, tiled=True)
     right_all = lax.all_gather(right, "batch", axis=0, tiled=True)
-    partial = contract_rows(left_rows, right_all)
-    return lax.psum_scatter(partial, "seq", scatter_dimension=1, tiled=True)
+    partial = contract_rows(left_rows, right_all).astype(jnp.bfloat16)
+    summed = lax.psum_scatter(partial, "seq", scatter_dimension=1, tiled=True)
+    return summed.astype(jnp.float32)
 
 
 GRAD_PLAN = {"skip": "batch", "qkv": "seq", "out": "batch", "hidden": "seq", "down": "batch"}

time: 820 us -> 774 us (0.944)
  starting transfers between devices: 115 us -> 35.1 us
  waiting for transfers between devices: 246 us -> 290 us
  local copies, waits for them, and re-layouts: 120 us -> 96.2 us
  blocking collectives: 64.8 us -> 83.9 us
  matrix products: 208 us -> 196 us
    all_to_all x1 -> x5, waiting for transfers between devices: 41.1 us -> 183 us  [the longest x2 131 us: seq_gathered_grad(): lax.all_to_all(right, 'seq', split_axis=1, concat_axis=0, tiled=True)]
    ppermute x23 -> x0, waiting for transfers between devices: 97.9 us -> none  [exchange(): got.append(lax.ppermute(piece, axis, pairs))]
    ppermute x23 -> x0, starting transfers between devices: 94.7 us -> none  [exchange(): got.append(lax.ppermute(piece, axis, pairs))]
    all_to_all x0 -> x1, blocking collectives: none -> 45.4 us  [on_device(): lax.all_to_all(jnp.stack([grad_query, grad_key, grad_value], axis=1)[:, :...]
    psum x1, blocking collectives: 64.8 us -> 38.5 us  [on_device(): small_total = lax.psum(jnp.concatenate(small_grads), ('seq', 'batch'))]
    all_to_all x1 -> x5, starting transfers between devices: 3.8 us -> 19.5 us  [the longest x3 12.1 us: batch_gathered_grad(): lax.all_to_all(left, 'batch', split_axis=1, concat_axis=0, tiled=True)]
    gather x9 -> x0, local copies, waits for them, and re-layouts: 11.8 us -> none  [exchange(): return jnp.take(jnp.stack(got), order, axis=0)]
    unnamed x100 -> x78, local copies, waits for them, and re-layouts: 33.6 us -> 23 us
  transfers between devices with their start and end apart: 37 -> 18, of which waited for: 19 -> 10; matrix products, arithmetic and copies ran while one was open for 30% -> 27% of each run, Pallas kernels for 0% -> 0%
where the time goes in v3:
time: 774 us; the launch traced here: 767 us
  waiting for transfers between devices  290 us (37%)
  matrix products  196 us (25%)
  local copies, waits for them, and re-layouts  96.2 us (12%)
  blocking collectives  83.9 us (11%)
  other arithmetic  50.7 us (7%)
  starting transfers between devices  35.1 us (5%)
  between operations  15 us (2%)
    all_to_all x2, waiting for transfers between devices, seq_gathered_grad(): lax.all_to_all(right, 'seq', split_axis=1, concat_axis=0, tiled=True)  131 us
    all_to_all x3, waiting for transfers between devices, batch_gathered_grad(): lax.all_to_all(left, 'batch', split_axis=1, concat_axis=0, tiled=True)  52.3 us
    all_to_all x1, blocking collectives, on_device(): lax.all_to_all(jnp.stack([grad_query, grad_key, grad_value], axis=1)[:, :...  45.4 us
    all_to_all x1, waiting for transfers between devices, on_device(): lax.all_to_all(packed.reshape(local_rows, 3, seq_count, feature_count //...  41.7 us
    dot_general x5, matrix products, product(): return jnp.dot(left, right, preferred_element_type=jnp.float32)  40.6 us
    psum x1, blocking collectives, on_device(): small_total = lax.psum(jnp.concatenate(small_grads), ('seq', 'batch'))  38.5 us
    dot_general x5, matrix products, times_transposed(): lax.dot_general(left, right, (((1,), (1,)), ((), ())), preferred_element_...  37.1 us
    dot_general x5, matrix products, contract_rows(): lax.dot_general(left, right, (((0,), (0,)), ((), ())), preferred_element_...  31 us
  transfers between devices with their start and end apart: 18, of which 10 were waited for; matrix products, arithmetic and copies ran while one was open for 27% of the time, Pallas kernels for 0%

profile of v3, /device:TPU:0, one launch (start us, length us, event | category | flops | bytes accessed | tf_op | source)
XLA Modules:
  0.0 767.2 jit_solution(8733200593062052870)
XLA Ops:
  16.0 7.2 convolution_convert_fusion.1
  29.9 6.8 all-to-all-start
  37.0 41.7 %all-to-all-done = bf16[256,3,8,144]{0,3,1,2:T(8,128)(2,1)} async-done(((bf16[256,3,8,144]{0,3,1,2:T(8,128)(2,1)}), bf16[256,3,8,144]{0,3,1,2:T(8,128)(2,1)}, u32[]{:S(2)}, u32[]{:S(2)}) %all-to-all-start) | async-done | bytes 1769504 | tf_op jit(solution)/shard_map/all_to_all | solution.py:193
  94.0 36.5 %while.27 = (s32[]{:T(128)}, bf16[4,512,144]{1,2,0:T(8,128)(2,1)}, f32[4,2,512,1]{2,1,3,0:T(2,128)S(1)}, s32[4,512]{1,0:T(4,128)S(1)}, s32[2048]{0:T(1024)S(1)},...) while((s32[]{:T(128)}, bf16[4,512,144]{1,2,0:T(8,128)(2,1)}, ...), condition=%wide.region_7.8_spmd, body=%wide.region_4.7_spmd.sunk | while | flops 628169728 | bytes 33536144 | solution.py:77
  142.0 16.1 %all-to-all-done.1 = bf16[8,256,144]{1,2,0:T(8,128)(2,1)} async-done(((bf16[8,256,144]{1,2,0:T(8,128)(2,1)}), bf16[8,256,144]{1,2,0:T(8,128)(2,1)}, u32[]{:S(2)}, u32[]{:S(2)}) %all-to-all-start.1) | async-done | bytes 589856 | tf_op jit(solution)/shard_map/all_to_all | solution.py:205
  162.8 17.1 %multiply_convert_fusion.1 = (bf16[256,4608]{1,0:T(8,128)(2,1)}, f32[256,4608]{1,0:T(8,128)}, f32[256,4608]{1,0:T(8,128)}) fusion(f32[4608]{0:T(1024)S(1)} %convert_element_type.134, bf16[256,1152]{1,0:T(8,128)(2,1)} %add_convert_fusion.2, bf16[1152,4608]{1,0:T(8,128)(2,1)} %param.33), kind=kOutput, calls=%fused_computation.57 | convolution fusion | flops 2795765760 | bytes 23021568 | tf_op jit(solution)/shard_map/dot_general | solution.py:15
  179.9 14.6 %convert_reduce_fusion = (f32[4608]{0:T(1024)}, bf16[256,4608]{1,0:T(8,128)(2,1)}) fusion(f32[256,4608]{1,0:T(8,128)} %get-tuple-element.290, f32[256,4608]{1,0:T(8,128)} %get-tuple-element.312, bf16[4608,1152]{1,0:T(8,128)(2,1)} %param.35, bf16[1,256,1152]{2,1,0:T(8,128)(2,1)S(1)} %copy-done.13), kind=kOutput, calls=%fused_computation.55 | convolution fusion | flops 2736778752 | bytes 23021568 | tf_op jit(solution)/shard_map/dot_general | solution.py:25
  194.5 8.7 %multiply_reduce_fusion.1 = (f32[1152]{0:T(1024)}, f32[256]{0:T(256)S(1)}, f32[1152]{0:T(1024)}, f32[256,1152]{1,0:T(8,128)S(1)}) fusion(f32[256,1152]{1,0:T(8,128)S(1)} %copy-done.7, f32[256]{0:T(256)S(1)} %fusion.58, f32[256]{0:T(256)S(1)} %broadcast_multiply_fusion, f32[1152]{0:T(1024)S(1)} %convert_element_type.131, ...), kind=kOutput, calls=%fused_computation.96 | convolution fusion | flops 2720265728 | bytes 15352320 | tf_op jit(solution)/shard_map/dot_general | solution.py:25
  216.7 15.7 %all-to-all-done.2 = bf16[256,8,144]{0,2,1:T(8,128)(2,1)S(1)} async-done(((bf16[256,8,144]{0,2,1:T(8,128)(2,1)}), bf16[256,8,144]{0,2,1:T(8,128)(2,1)S(1)}, u32[]{:S(2)}, u32[]{:S(2)}) %all-to-all-start.2) | async-done | bytes 589856 | tf_op jit(solution)/shard_map/all_to_all | solution.py:231
  234.7 88.0 %while.28 = (s32[]{:T(128)}, f32[2048,2,72]{0,2,1:T(8,128)S(1)}, f32[2048,2,72]{0,2,1:T(8,128)}, bf16[4,512,144]{1,2,0:T(8,128)(2,1)}, bf16[4,512,2,72]{1,3,2,0:...) while((s32[]{:T(128)}, f32[2048,2,72]{0,2,1:T(8,128)S(1)}, ...), condition=%wide.region_14.15_spmd.clone, body=%wide.region_12.14_spmd.clone.sunk | while | flops 1543781376 | bytes 136800560 | solution.py:123
  331.0 7.6 reshape.271
  338.6 45.4 %all_to_all.157 = bf16[8,2,55296]{2,1,0:T(2,128)(2,1)} all-to-all(bf16[8,2,55296]{2,1,0:T(2,128)(2,1)S(1)} %reshape.271), channel_id=1, replica_groups=mesh['seq'=8,'batch'=4] {'seq'}, dimensions={0} | all-to-all | bytes 3538944 | tf_op jit(solution)/shard_map/all_to_all | solution.py:237
  384.0 8.8 %reshape.272 = bf16[2048,1,3,144]{3,2,1,0:T(4,128)(2,1)} reshape(bf16[8,2,55296]{2,1,0:T(2,128)(2,1)} %all_to_all.157) | data formatting | bytes 3538944
  392.8 6.9 copy.120
  415.2 12.0 %all-to-all-done.6 = bf16[256,4,288]{0,2,1:T(8,128)(2,1)S(1)} async-done(((bf16[256,4,288]{0,2,1:T(8,128)(2,1)}), bf16[256,4,288]{0,2,1:T(8,128)(2,1)S(1)}, u32[]{:S(2)}, u32[]{:S(2)}) %all-to-all-start.6) | async-done | bytes 589856 | tf_op jit(solution)/shard_map/all_to_all | solution.py:147
  436.3 30.6 %all-to-all-done.8 = bf16[256,4,1152]{2,0,1:T(8,128)(2,1)S(1)} async-done(((bf16[256,4,1152]{2,0,1:T(8,128)(2,1)}), bf16[256,4,1152]{2,0,1:T(8,128)(2,1)S(1)}, u32[]{:S(2)}, u32[]{:S(2)}) %all-to-all-start.8) | async-done | bytes 2359328 | tf_op jit(solution)/shard_map/all_to_all | solution.py:147
  486.3 68.4 %all-to-all-done.5 = bf16[256,8,432]{0,2,1:T(8,128)(2,1)S(1)} async-done(((bf16[256,8,432]{0,2,1:T(8,128)(2,1)}), bf16[256,8,432]{0,2,1:T(8,128)(2,1)S(1)}, u32[]{:S(2)}, u32[]{:S(2)}) %all-to-all-start.5) | async-done | bytes 1769504 | tf_op jit(solution)/shard_map/all_to_all | solution.py:140
  565.1 9.8 %all-to-all-done.4 = bf16[256,4,576]{0,2,1:T(8,128)(2,1)} async-done(((bf16[256,4,576]{0,2,1:T(8,128)(2,1)}), bf16[256,4,576]{0,2,1:T(8,128)(2,1)}, u32[]{:S(2)}, u32[]{:S(2)}) %all-to-all-start.4) | async-done | bytes 1179680 | tf_op jit(solution)/shard_map/all_to_all | solution.py:147
  578.6 6.7 convolution_convert_fusion.4
  593.1 62.4 %all-to-all-done.7 = bf16[256,8,576]{0,2,1:T(8,128)(2,1)S(1)} async-done(((bf16[256,8,576]{0,2,1:T(8,128)(2,1)}), bf16[256,8,576]{0,2,1:T(8,128)(2,1)S(1)}, u32[]{:S(2)}, u32[]{:S(2)}) %all-to-all-start.7) | async-done | bytes 2359328 | tf_op jit(solution)/shard_map/all_to_all | solution.py:140
  657.3 8.2 %convolution_convert_fusion.2 = bf16[1152,576]{1,0:T(8,128)(2,1)} fusion(bf16[2048,1152]{1,0:T(8,128)(2,1)} %all-gather.13.cloned.1.call-done, bf16[2048,576]{0,1:T(8,128)(2,1)} %bitcast.215), kind=kOutput, calls=%fused_computation.71 | convolution fusion | flops 2718572544 | bytes 8404992 | tf_op jit(solution)/shard_map/dot_general | solution.py:19
  665.6 9.0 %fusion.47 = bf16[1,256,1152]{2,1,0:T(8,128)(2,1)} fusion(f32[256,1152]{1,0:T(8,128)S(1)} %copy-done.8, bf16[256,4608]{1,0:T(8,128)(2,1)} %get-tuple-element.289, bf16[4608,1152]{1,0:T(8,128)(2,1)} %param.35, f32[1152]{0:T(1024)S(1)} %convert_element_type.136), kind=kOutput, calls=%fused_computation.82 | convolution fusion | flops 2718793728 | bytes 14750208 | tf_op jit(solution)/shard_map/dot_general | solution.py:15
  674.7 38.5 %psum.7 = f32[12672]{0:T(1024)S(1)} all-reduce(f32[12672]{0:T(1024)S(1)} %constant_dynamic-update-slice_fusion), channel_id=1, replica_groups=mesh['seq'=8,'batch'=4] {'seq','batch'}, use_global_device_ids=true, to_apply=%region_26.27 | all-reduce | flops 12672 | bytes 101376 | tf_op jit(solution)/shard_map/psum | solution.py:265
  728.2 30.1 %reduce-scatter.12.cloned.1.call-done = bf16[288,576]{1,0:T(8,128)(2,1)} async-done(((bf16[1152,576]{1,0:T(8,128)(2,1)}), bf16[288,576]{1,0:T(8,128)(2,1)}) %reduce-scatter.12.cloned.1.call-update) | async-done | bytes 331792 | tf_op jit(solution)/shard_map/reduce_scatter | solution.py:142
  (306 shorter events, 279.4 us)
Async XLA Ops:
  7.2 150.9 %copy-start = (bf16[1152,1152]{1,0:T(8,128)(2,1)S(1)}, bf16[1152,1152]{1,0:T(8,128)(2,1)}, u32[]{:S(2)}) copy-start(bf16[1152,1152]{1,0:T(8,128)(2,1)} %param.29) | copy-start | bytes 7962628
  29.9 48.9 %all-to-all-start = ((bf16[256,3,8,144]{0,3,1,2:T(8,128)(2,1)}), bf16[256,3,8,144]{0,3,1,2:T(8,128)(2,1)}, u32[]{:S(2)}, u32[]{:S(2)}) async-start(bf16[256,3,8,144]{0,3,1,2:T(8,128)(2,1)} %copy.97), calls=%async_computation | async-start | bytes 3538944 | tf_op jit(solution)/shard_map/all_to_all | solution.py:193
  130.6 11.5 %copy-start.36 = (bf16[1152]{0:T(1024)(128)(2,1)S(1)}, bf16[1152]{0:T(1024)(128)(2,1)}, u32[]{:S(2)}) copy-start(bf16[1152]{0:T(1024)(128)(2,1)} %param.31) | copy-start | bytes 6916
  137.2 20.9 %all-to-all-start.1 = ((bf16[8,256,144]{1,2,0:T(8,128)(2,1)}), bf16[8,256,144]{1,2,0:T(8,128)(2,1)}, u32[]{:S(2)}, u32[]{:S(2)}) async-start(bf16[8,256,144]{1,2,0:T(8,128)(2,1)} %copy.101), calls=%async_computation.1 | async-start | bytes 1179648 | tf_op jit(solution)/shard_map/all_to_all | solution.py:205
  141.4 290.3 %all-gather.11.cloned.1.call-start = ((), (), s32[]{:S(2)}) async-start(), calls=%async_computation.18 | async-start | bytes 2949120 | tf_op jit(solution)/shard_map/all_gather | solution.py:148
  162.8 17.1 %copy-start.13 = (bf16[1,256,1152]{2,1,0:T(8,128)(2,1)S(1)}, bf16[1,256,1152]{2,1,0:T(8,128)(2,1)}, u32[]{:S(2)}) copy-start(bf16[1,256,1152]{2,1,0:T(8,128)(2,1)} %param.37) | copy-start | bytes 1769476
  179.9 14.6 %copy-start.7 = (f32[256,1152]{1,0:T(8,128)S(1)}, f32[256,1152]{1,0:T(8,128)}, u32[]{:S(2)}) copy-start(f32[256,1152]{1,0:T(8,128)} %copy-done.6) | copy-start | bytes 3538948
  206.4 229.9 %all-gather.15.cloned.1.call-start = ((), (), s32[]{:S(2)}) async-start(), calls=%async_computation.23 | async-start | bytes 2949120 | tf_op jit(solution)/shard_map/all_gather | solution.py:148
  212.2 20.2 %all-to-all-start.2 = ((bf16[256,8,144]{0,2,1:T(8,128)(2,1)}), bf16[256,8,144]{0,2,1:T(8,128)(2,1)S(1)}, u32[]{:S(2)}, u32[]{:S(2)}) async-start(bf16[256,8,144]{0,2,1:T(8,128)(2,1)} %bitcast.18), calls=%async_computation.2 | async-start | bytes 1179648 | tf_op jit(solution)/shard_map/all_to_all | solution.py:231
  215.7 362.9 %all-gather.9.cloned.1.call-start = ((), (), s32[]{:S(2)}) async-start(), calls=%async_computation.16 | async-start | bytes 5308416 | tf_op jit(solution)/shard_map/all_gather | solution.py:139
  216.4 371.3 %all-gather.7.cloned.1.call-start = ((), (), s32[]{:S(2)}) async-start(), calls=%async_computation.14 | async-start | bytes 2949120 | tf_op jit(solution)/shard_map/all_gather | solution.py:148
  409.0 248.3 %all-gather.13.cloned.1.call-start = ((), (), s32[]{:S(2)}) async-start(), calls=%async_computation.20 | async-start | bytes 5308416 | tf_op jit(solution)/shard_map/all_gather | solution.py:139
  409.6 17.5 %all-to-all-start.6 = ((bf16[256,4,288]{0,2,1:T(8,128)(2,1)}), bf16[256,4,288]{0,2,1:T(8,128)(2,1)S(1)}, u32[]{:S(2)}, u32[]{:S(2)}) async-start(bf16[256,4,288]{0,2,1:T(8,128)(2,1)} %bitcast.34), calls=%async_computation.8 | async-start | bytes 1179648 | tf_op jit(solution)/shard_map/all_to_all | solution.py:147
  427.1 39.8 %all-to-all-start.8 = ((bf16[256,4,1152]{2,0,1:T(8,128)(2,1)}), bf16[256,4,1152]{2,0,1:T(8,128)(2,1)S(1)}, u32[]{:S(2)}, u32[]{:S(2)}) async-start(bf16[256,4,1152]{2,0,1:T(8,128)(2,1)} %bitcast.158), calls=%async_computation.12 | async-start | bytes 4718592 | tf_op jit(solution)/shard_map/all_to_all | solution.py:147
  430.8 289.5 %reduce-scatter.10.cloned.1.call-start = ((), (), s32[]{:S(2)}) async-start(), calls=%async_computation.19 | async-start | bytes 995328 | tf_op jit(solution)/shard_map/reduce_scatter | solution.py:150
  436.3 285.7 %reduce-scatter.14.cloned.1.call-start = ((), (), s32[]{:S(2)}) async-start(), calls=%async_computation.22 | async-start | bytes 2985984 | tf_op jit(solution)/shard_map/reduce_scatter | solution.py:150
  479.9 74.8 %all-to-all-start.5 = ((bf16[256,8,432]{0,2,1:T(8,128)(2,1)}), bf16[256,8,432]{0,2,1:T(8,128)(2,1)S(1)}, u32[]{:S(2)}, u32[]{:S(2)}) async-start(bf16[256,8,432]{0,2,1:T(8,128)(2,1)} %bitcast.207), calls=%async_computation.6 | async-start | bytes 3538944 | tf_op jit(solution)/shard_map/all_to_all | solution.py:140
  554.7 20.2 %all-to-all-start.4 = ((bf16[256,4,576]{0,2,1:T(8,128)(2,1)}), bf16[256,4,576]{0,2,1:T(8,128)(2,1)}, u32[]{:S(2)}, u32[]{:S(2)}) async-start(bf16[256,4,576]{0,2,1:T(8,128)(2,1)} %pad_maximum_fusion), calls=%async_computation.4 | async-start | bytes 2359296 | tf_op jit(solution)/shard_map/all_to_all | solution.py:147
  574.9 80.6 %all-to-all-start.7 = ((bf16[256,8,576]{0,2,1:T(8,128)(2,1)}), bf16[256,8,576]{0,2,1:T(8,128)(2,1)S(1)}, u32[]{:S(2)}, u32[]{:S(2)}) async-start(bf16[256,8,576]{0,2,1:T(8,128)(2,1)} %bitcast.36), calls=%async_computation.10 | async-start | bytes 4718592 | tf_op jit(solution)/shard_map/all_to_all | solution.py:140
  578.5 145.3 %reduce-scatter.8.cloned.1.call-start = ((), (), s32[]{:S(2)}) async-start(), calls=%async_computation.17 | async-start | bytes 1474560 | tf_op jit(solution)/shard_map/reduce_scatter | solution.py:142
  585.3 141.2 %reduce-scatter.6.cloned.1.call-start = ((), (), s32[]{:S(2)}) async-start(), calls=%async_computation.15 | async-start | bytes 1658880 | tf_op jit(solution)/shard_map/reduce_scatter | solution.py:150
  593.0 165.2 %reduce-scatter.12.cloned.1.call-start = ((), (), s32[]{:S(2)}) async-start(), calls=%async_computation.21 | async-start | bytes 1843200 | tf_op jit(solution)/shard_map/reduce_scatter | solution.py:142
  665.5 48.9 %copy-start.17 = (bf16[256,1152]{1,0:T(8,128)(2,1)S(1)}, bf16[256,1152]{1,0:T(8,128)(2,1)}, u32[]{:S(2)}) copy-start(bf16[256,1152]{1,0:T(8,128)(2,1)} %get-tuple-element.284) | copy-start | bytes 1769476
  718.7 41.5 %copy-start.1 = (bf16[1152,1152]{1,0:T(8,128)(2,1)S(1)}, bf16[1152,1152]{1,0:T(8,128)(2,1)}, u32[]{:S(2)}) copy-start(bf16[1152,1152]{1,0:T(8,128)(2,1)} %param.29) | copy-start | bytes 7962628
  (51 other events, 240.2 us)
Sparse Core Ops, SparseCore 0:
  206.5 36.2 all-gather.10
  244.6 37.3 all-gather.14
  283.6 51.2 all-gather.8
  409.1 57.9 all-gather.6
  469.2 82.9 all-gather.12
  554.4 31.9 reduce-scatter.9
  588.6 67.7 reduce-scatter.13
  659.4 30.9 reduce-scatter.7
  692.6 33.8 reduce-scatter.5
  729.3 28.8 reduce-scatter.11

commit v4 on v3

--- a/solution.py
+++ b/solution.py
@@ -149,6 +149,27 @@
     partial = contract_rows(left_rows, right_all).astype(jnp.bfloat16)
     summed = lax.psum_scatter(partial, "seq", scatter_dimension=1, tiled=True)
     return summed.astype(jnp.float32)
+
+
+def qkv_grad_from_heads(left, grad_heads):
+    seq_count = lax.axis_size("seq")
+    me = lax.axis_index("seq")
+    piece = grad_heads.shape[1] // 3
+    left_all = lax.all_gather(left, "seq", axis=0, tiled=True)
+    partial = contract_rows(left_all, grad_heads).astype(jnp.bfloat16)
+    summed = lax.psum_scatter(partial, "batch", scatter_dimension=0, tiled=True)
+    summed = summed.astype(jnp.float32)
+    inverse = pow(3, -1, seq_count)
+    slots = []
+    for slot in range(3):
+        target = ((me - slot) * inverse) % seq_count
+        chunk = (3 * target + slot) // seq_count
+        sent = lax.dynamic_slice_in_dim(summed, chunk * piece, piece, axis=1)
+        pairs = []
+        for source in range(seq_count):
+            pairs.append((source, ((source - slot) * inverse) % seq_count))
+        slots.append(lax.ppermute(sent, "seq", pairs))
+    return jnp.concatenate(slots, axis=1)
 
 
 GRAD_PLAN = {"skip": "batch", "qkv": "seq", "out": "batch", "hidden": "seq", "down": "batch"}
@@ -234,14 +255,17 @@
     grad_query, grad_key, grad_value = attend_backward(
         query_heads, key_heads, value_heads, segment, grad_context_heads, log_total
     )
-    grad_packed = lax.all_to_all(
-        jnp.stack([grad_query, grad_key, grad_value], axis=1)[:, :, None],
-        "seq",
-        split_axis=0,
-        concat_axis=2,
-        tiled=True,
-    ).reshape(local_rows, 3 * feature_count)
-    grad_qkv_weight = weight_grad("qkv", normed_one, grad_packed)
+    grad_packed = jnp.concatenate(
+        [
+            lax.all_to_all(grad_query, "seq", split_axis=0, concat_axis=1, tiled=True),
+            lax.all_to_all(grad_key, "seq", split_axis=0, concat_axis=1, tiled=True),
+            lax.all_to_all(grad_value, "seq", split_axis=0, concat_axis=1, tiled=True),
+        ],
+        axis=1,
+    )
+    grad_qkv_weight = qkv_grad_from_heads(
+        normed_one, jnp.concatenate([grad_query, grad_key, grad_value], axis=1)
+    )
     grad_normed_one = times_transposed(grad_packed, qkv_weight)
     grad_mixed_norm, grad_attention_gain, grad_attention_shift = first_pull(grad_normed_one)
     grad_mixed = (grad_middle + grad_mixed_norm).astype(jnp.bfloat16)

time: 774 us -> 729 us (0.942)
  local copies, waits for them, and re-layouts: 96.2 us -> 64.7 us
  blocking collectives: 83.9 us -> 58.1 us
  starting transfers between devices: 35.1 us -> 46.1 us
    all_to_all x2 -> x1, waiting for transfers between devices: 131 us -> 61.5 us  [seq_gathered_grad(): lax.all_to_all(right, 'seq', split_axis=1, concat_axis=0, tiled=True)]
    all_to_all x0 -> x2, waiting for transfers between devices: none -> 28.9 us  [the longest x1 15.5 us: on_device(): lax.all_to_all(grad_value, 'seq', split_axis=0, concat_axis=1, tiled=True)]
    all_to_all x1, blocking collectives: 45.4 us -> 19.3 us  [on_device(): lax.all_to_all(grad_query, 'seq', split_axis=0, concat_axis=1, tiled=True)]
    reduce_scatter x3, waiting for transfers between devices: 0.86 us -> 23.6 us  [batch_gathered_grad(): summed = lax.psum_scatter(partial, 'seq', scatter_dimension=1, tiled=True)]
    unnamed x78 -> x92, local copies, waits for them, and re-layouts: 23 us -> 7.59 us
    ppermute x0 -> x3, waiting for transfers between devices: none -> 10.9 us  [qkv_grad_from_heads(): slots.append(lax.ppermute(sent, 'seq', pairs))]
    all_to_all x3 -> x4, local copies, waits for them, and re-layouts: 13.5 us -> 3.98 us  [the longest x2 2.13 us: on_device(): lax.all_to_all(grad_query, 'seq', split_axis=0, concat_axis=1, tiled=True)]
    all_to_all x0 -> x2, starting transfers between devices: none -> 8.53 us  [the longest x1 4.33 us: on_device(): lax.all_to_all(grad_value, 'seq', split_axis=0, concat_axis=1, tiled=True)]
  transfers between devices with their start and end apart: 18 -> 22, of which waited for: 10 -> 12; matrix products, arithmetic and copies ran while one was open for 27% -> 31% of each run, Pallas kernels for 0% -> 0%
where the time goes in v4:
time: 729 us; the launch traced here: 722 us
  waiting for transfers between devices  290 us (40%)
  matrix products  195 us (27%)
  local copies, waits for them, and re-layouts  64.7 us (9%)
  blocking collectives  58.1 us (8%)
  other arithmetic  52 us (7%)
  starting transfers between devices  46.1 us (6%)
  between operations  15.3 us (2%)
    all_to_all x1, waiting for transfers between devices, seq_gathered_grad(): lax.all_to_all(right, 'seq', split_axis=1, concat_axis=0, tiled=True)  61.5 us
    all_to_all x3, waiting for transfers between devices, batch_gathered_grad(): lax.all_to_all(left, 'batch', split_axis=1, concat_axis=0, tiled=True)  54.5 us
    all_to_all x1, waiting for transfers between devices, on_device(): lax.all_to_all(packed.reshape(local_rows, 3, seq_count, feature_count //...  41.7 us
    dot_general x5, matrix products, product(): return jnp.dot(left, right, preferred_element_type=jnp.float32)  40.6 us
    psum x1, blocking collectives, on_device(): small_total = lax.psum(jnp.concatenate(small_grads), ('seq', 'batch'))  38.9 us
    dot_general x5, matrix products, times_transposed(): lax.dot_general(left, right, (((1,), (1,)), ((), ())), preferred_element_...  37.2 us
    dot_general x5, matrix products, contract_rows(): lax.dot_general(left, right, (((0,), (0,)), ((), ())), preferred_element_...  30.8 us
    reduce_scatter x1, waiting for transfers between devices, seq_gathered_grad(): summed = lax.psum_scatter(partial, 'batch', scatter_dimension=0, tiled=True)  29.8 us
  transfers between devices with their start and end apart: 22, of which 12 were waited for; matrix products, arithmetic and copies ran while one was open for 31% of the time, Pallas kernels for 0%

profile of v4, /device:TPU:0, one launch (start us, length us, event | category | flops | bytes accessed | tf_op | source)
XLA Modules:
  0.0 722.0 jit_solution(6150779179004533748)
XLA Ops:
  16.0 7.2 %convolution_convert_fusion.1 = bf16[256,3456]{1,0:T(8,128)(2,1)} fusion(bf16[256,1152]{1,0:T(8,128)(2,1)S(1)} %add_convert_fusion.3, bf16[1152,3456]{1,0:T(8,128)(2,1)} %param.28), kind=kOutput, calls=%fused_computation.53 | convolution fusion | flops 2039316480 | bytes 10321920 | tf_op jit(solution)/shard_map/dot_general | solution.py:15
  29.9 6.6 all-to-all-start
  36.8 41.7 %all-to-all-done = bf16[256,3,8,144]{0,3,1,2:T(8,128)(2,1)} async-done(((bf16[256,3,8,144]{0,3,1,2:T(8,128)(2,1)}), bf16[256,3,8,144]{0,3,1,2:T(8,128)(2,1)}, u32[]{:S(2)}, u32[]{:S(2)}) %all-to-all-start) | async-done | bytes 1769504 | tf_op jit(solution)/shard_map/all_to_all | solution.py:214
  93.8 36.5 %while.27 = (s32[]{:T(128)}, bf16[4,512,144]{1,2,0:T(8,128)(2,1)}, f32[4,2,512,1]{2,1,3,0:T(2,128)S(1)}, s32[4,512]{1,0:T(4,128)S(1)}, s32[2048]{0:T(1024)S(1)},...) while((s32[]{:T(128)}, bf16[4,512,144]{1,2,0:T(8,128)(2,1)}, ...), condition=%wide.region_7.8_spmd, body=%wide.region_4.7_spmd.sunk | while | flops 628169728 | bytes 33536144 | solution.py:77
  142.0 20.8 %all-to-all-done.1 = bf16[8,256,144]{1,2,0:T(8,128)(2,1)} async-done(((bf16[8,256,144]{1,2,0:T(8,128)(2,1)}), bf16[8,256,144]{1,2,0:T(8,128)(2,1)}, u32[]{:S(2)}, u32[]{:S(2)}) %all-to-all-start.1) | async-done | bytes 589856 | tf_op jit(solution)/shard_map/all_to_all | solution.py:226
  167.6 17.2 %multiply_convert_fusion.1 = (bf16[256,4608]{1,0:T(8,128)(2,1)}, f32[256,4608]{1,0:T(8,128)}, f32[256,4608]{1,0:T(8,128)}) fusion(f32[4608]{0:T(1024)S(1)} %convert_element_type.134, bf16[256,1152]{1,0:T(8,128)(2,1)} %add_convert_fusion.2, bf16[1152,4608]{1,0:T(8,128)(2,1)} %param.33), kind=kOutput, calls=%fused_computation.57 | convolution fusion | flops 2795765760 | bytes 23021568 | tf_op jit(solution)/shard_map/dot_general | solution.py:15
  184.8 14.7 %convert_reduce_fusion = (f32[4608]{0:T(1024)}, bf16[256,4608]{1,0:T(8,128)(2,1)}) fusion(f32[256,4608]{1,0:T(8,128)} %get-tuple-element.290, f32[256,4608]{1,0:T(8,128)} %get-tuple-element.315, bf16[4608,1152]{1,0:T(8,128)(2,1)} %param.35, bf16[1,256,1152]{2,1,0:T(8,128)(2,1)S(1)} %copy-done.14), kind=kOutput, calls=%fused_computation.55 | convolution fusion | flops 2736778752 | bytes 23021568 | tf_op jit(solution)/shard_map/dot_general | solution.py:25
  199.5 8.7 %multiply_reduce_fusion.1 = (f32[1152]{0:T(1024)}, f32[256]{0:T(256)S(1)}, f32[1152]{0:T(1024)}, f32[256,1152]{1,0:T(8,128)S(1)}) fusion(f32[256,1152]{1,0:T(8,128)S(1)} %copy-done.7, f32[256]{0:T(256)S(1)} %fusion.69, f32[256]{0:T(256)S(1)} %broadcast_multiply_fusion, f32[1152]{0:T(1024)S(1)} %convert_element_type.131, ...), kind=kOutput, calls=%fused_computation.106 | convolution fusion | flops 2720265728 | bytes 15352320 | tf_op jit(solution)/shard_map/dot_general | solution.py:25
  220.7 15.9 %all-to-all-done.2 = bf16[256,8,144]{0,2,1:T(8,128)(2,1)S(1)} async-done(((bf16[256,8,144]{0,2,1:T(8,128)(2,1)}), bf16[256,8,144]{0,2,1:T(8,128)(2,1)S(1)}, u32[]{:S(2)}, u32[]{:S(2)}) %all-to-all-start.2) | async-done | bytes 589856 | tf_op jit(solution)/shard_map/all_to_all | solution.py:252
  239.0 87.2 %while.28 = (s32[]{:T(128)}, f32[2048,2,72]{0,2,1:T(8,128)S(1)}, f32[2048,2,72]{0,2,1:T(8,128)}, bf16[4,512,144]{1,2,0:T(8,128)(2,1)}, bf16[4,512,2,72]{1,3,2,0:...) while((s32[]{:T(128)}, f32[2048,2,72]{0,2,1:T(8,128)S(1)}, ...), condition=%wide.region_14.15_spmd.clone, body=%wide.region_12.14_spmd.clone.sunk | while | flops 1543781376 | bytes 136800560 | solution.py:123
  334.1 15.5 %all-to-all-done.5 = bf16[8,256,144]{1,2,0:T(8,128)(2,1)} async-done(((bf16[8,256,144]{1,2,0:T(8,128)(2,1)}), bf16[8,256,144]{1,2,0:T(8,128)(2,1)}, u32[]{:S(2)}, u32[]{:S(2)}) %all-to-all-start.5) | async-done | bytes 589856 | tf_op jit(solution)/shard_map/all_to_all | solution.py:262
  357.3 13.3 %all-to-all-done.4 = bf16[8,256,144]{1,2,0:T(8,128)(2,1)} async-done(((bf16[8,256,144]{1,2,0:T(8,128)(2,1)}), bf16[8,256,144]{1,2,0:T(8,128)(2,1)}, u32[]{:S(2)}, u32[]{:S(2)}) %all-to-all-start.4) | async-done | bytes 589856 | tf_op jit(solution)/shard_map/all_to_all | solution.py:261
  370.6 19.3 %all_to_all.180 = bf16[8,256,144]{1,2,0:T(8,128)(2,1)S(1)} all-to-all(bf16[8,256,144]{1,2,0:T(8,128)(2,1)S(1)} %copy.108), channel_id=1, replica_groups=mesh['seq'=8,'batch'=4] {'seq'}, dimensions={0} | all-to-all | bytes 1179648 | tf_op jit(solution)/shard_map/all_to_all | solution.py:260
  411.6 9.8 %all-to-all-done.7 = bf16[256,4,288]{0,2,1:T(8,128)(2,1)S(1)} async-done(((bf16[256,4,288]{0,2,1:T(8,128)(2,1)}), bf16[256,4,288]{0,2,1:T(8,128)(2,1)S(1)}, u32[]{:S(2)}, u32[]{:S(2)}) %all-to-all-start.7) | async-done | bytes 589856 | tf_op jit(solution)/shard_map/all_to_all | solution.py:147
  430.9 34.5 %all-to-all-done.9 = bf16[256,4,1152]{2,0,1:T(8,128)(2,1)S(1)} async-done(((bf16[256,4,1152]{2,0,1:T(8,128)(2,1)}), bf16[256,4,1152]{2,0,1:T(8,128)(2,1)S(1)}, u32[]{:S(2)}, u32[]{:S(2)}) %all-to-all-start.9) | async-done | bytes 2359328 | tf_op jit(solution)/shard_map/all_to_all | solution.py:147
  465.5 6.5 convolution_convert_fusion
  482.2 10.3 %all-to-all-done.6 = bf16[256,4,576]{0,2,1:T(8,128)(2,1)S(1)} async-done(((bf16[256,4,576]{0,2,1:T(8,128)(2,1)}), bf16[256,4,576]{0,2,1:T(8,128)(2,1)S(1)}, u32[]{:S(2)}, u32[]{:S(2)}) %all-to-all-start.6) | async-done | bytes 1179680 | tf_op jit(solution)/shard_map/all_to_all | solution.py:147
  506.3 61.5 %all-to-all-done.8 = bf16[256,8,576]{0,2,1:T(8,128)(2,1)S(1)} async-done(((bf16[256,8,576]{0,2,1:T(8,128)(2,1)}), bf16[256,8,576]{0,2,1:T(8,128)(2,1)S(1)}, u32[]{:S(2)}, u32[]{:S(2)}) %all-to-all-start.8) | async-done | bytes 2359328 | tf_op jit(solution)/shard_map/all_to_all | solution.py:140
  569.6 8.2 %convolution_convert_fusion.2 = bf16[1152,576]{1,0:T(8,128)(2,1)} fusion(bf16[2048,1152]{1,0:T(8,128)(2,1)} %all-gather.13.cloned.1.call-done, bf16[2048,576]{0,1:T(8,128)(2,1)} %bitcast.219), kind=kOutput, calls=%fused_computation.71 | convolution fusion | flops 2718572544 | bytes 8404992 | tf_op jit(solution)/shard_map/dot_general | solution.py:19
  578.0 8.9 %fusion.47 = bf16[1,256,1152]{2,1,0:T(8,128)(2,1)} fusion(f32[256,1152]{1,0:T(8,128)S(1)} %copy-done.8, bf16[256,4608]{1,0:T(8,128)(2,1)} %get-tuple-element.289, bf16[4608,1152]{1,0:T(8,128)(2,1)} %param.35, f32[1152]{0:T(1024)S(1)} %convert_element_type.136), kind=kOutput, calls=%fused_computation.82 | convolution fusion | flops 2718793728 | bytes 14750208 | tf_op jit(solution)/shard_map/dot_general | solution.py:15
  587.0 38.9 %psum.7 = f32[12672]{0:T(1024)S(1)} all-reduce(f32[12672]{0:T(1024)S(1)} %constant_dynamic-update-slice_fusion), channel_id=1, replica_groups=mesh['seq'=8,'batch'=4] {'seq','batch'}, use_global_device_ids=true, to_apply=%region_26.27 | all-reduce | flops 12672 | bytes 101376 | tf_op jit(solution)/shard_map/psum | solution.py:289
  642.9 10.9 %collective-permute-done.2 = f32[288,144]{1,0:T(8,128)} collective-permute-done((f32[288,144]{1,0:T(8,128)}, f32[288,144]{1,0:T(8,128)}, u32[]{:S(2)}, u32[]{:S(2)}) %collective-permute-start.2) | collective-permute-done | bytes 165920 | tf_op jit(solution)/shard_map/ppermute | solution.py:171
  657.9 23.6 %reduce-scatter.6.cloned.1.call-done = bf16[576,144]{0,1:T(8,128)(2,1)} async-done(((bf16[576,1152]{0,1:T(8,128)(2,1)}), bf16[576,144]{0,1:T(8,128)(2,1)}) %reduce-scatter.6.cloned.1.call-update) | async-done | bytes 165904 | tf_op jit(solution)/shard_map/reduce_scatter | solution.py:150
  683.2 29.8 %reduce-scatter.12.cloned.1.call-done = bf16[288,576]{1,0:T(8,128)(2,1)} async-done(((bf16[1152,576]{1,0:T(8,128)(2,1)}), bf16[288,576]{1,0:T(8,128)(2,1)}) %reduce-scatter.12.cloned.1.call-update) | async-done | bytes 331792 | tf_op jit(solution)/shard_map/reduce_scatter | solution.py:142
  (328 shorter events, 282.1 us)
Async XLA Ops:
  7.2 155.6 %copy-start = (bf16[1152,1152]{1,0:T(8,128)(2,1)S(1)}, bf16[1152,1152]{1,0:T(8,128)(2,1)}, u32[]{:S(2)}) copy-start(bf16[1152,1152]{1,0:T(8,128)(2,1)} %param.29) | copy-start | bytes 7962628
  29.9 48.6 %all-to-all-start = ((bf16[256,3,8,144]{0,3,1,2:T(8,128)(2,1)}), bf16[256,3,8,144]{0,3,1,2:T(8,128)(2,1)}, u32[]{:S(2)}, u32[]{:S(2)}) async-start(bf16[256,3,8,144]{0,3,1,2:T(8,128)(2,1)} %copy.98), calls=%async_computation | async-start | bytes 3538944 | tf_op jit(solution)/shard_map/all_to_all | solution.py:214
  137.0 25.9 %all-to-all-start.1 = ((bf16[8,256,144]{1,2,0:T(8,128)(2,1)}), bf16[8,256,144]{1,2,0:T(8,128)(2,1)}, u32[]{:S(2)}, u32[]{:S(2)}) async-start(bf16[8,256,144]{1,2,0:T(8,128)(2,1)} %copy.102), calls=%async_computation.1 | async-start | bytes 1179648 | tf_op jit(solution)/shard_map/all_to_all | solution.py:226
  141.2 258.6 %all-gather.9.cloned.1.call-start = ((), (), s32[]{:S(2)}) async-start(), calls=%async_computation.17 | async-start | bytes 5308416 | tf_op jit(solution)/shard_map/all_gather | solution.py:158
  216.4 20.2 %all-to-all-start.2 = ((bf16[256,8,144]{0,2,1:T(8,128)(2,1)}), bf16[256,8,144]{0,2,1:T(8,128)(2,1)S(1)}, u32[]{:S(2)}, u32[]{:S(2)}) async-start(bf16[256,8,144]{0,2,1:T(8,128)(2,1)} %bitcast.18), calls=%async_computation.2 | async-start | bytes 1179648 | tf_op jit(solution)/shard_map/all_to_all | solution.py:252
  220.0 206.0 %all-gather.11.cloned.1.call-start = ((), (), s32[]{:S(2)}) async-start(), calls=%async_computation.19 | async-start | bytes 2949120 | tf_op jit(solution)/shard_map/all_gather | solution.py:148
  328.6 21.1 %all-to-all-start.5 = ((bf16[8,256,144]{1,2,0:T(8,128)(2,1)}), bf16[8,256,144]{1,2,0:T(8,128)(2,1)}, u32[]{:S(2)}, u32[]{:S(2)}) async-start(bf16[8,256,144]{1,2,0:T(8,128)(2,1)} %copy.110), calls=%async_computation.5 | async-start | bytes 1179648 | tf_op jit(solution)/shard_map/all_to_all | solution.py:262
  349.7 20.9 %all-to-all-start.4 = ((bf16[8,256,144]{1,2,0:T(8,128)(2,1)}), bf16[8,256,144]{1,2,0:T(8,128)(2,1)}, u32[]{:S(2)}, u32[]{:S(2)}) async-start(bf16[8,256,144]{1,2,0:T(8,128)(2,1)} %copy.109), calls=%async_computation.4 | async-start | bytes 1179648 | tf_op jit(solution)/shard_map/all_to_all | solution.py:261
  353.9 77.1 %all-gather.15.cloned.1.call-start = ((), (), s32[]{:S(2)}) async-start(), calls=%async_computation.24 | async-start | bytes 2949120 | tf_op jit(solution)/shard_map/all_gather | solution.py:148
  354.6 145.9 %all-gather.7.cloned.1.call-start = ((), (), s32[]{:S(2)}) async-start(), calls=%async_computation.15 | async-start | bytes 2949120 | tf_op jit(solution)/shard_map/all_gather | solution.py:148
  399.0 170.6 %all-gather.13.cloned.1.call-start = ((), (), s32[]{:S(2)}) async-start(), calls=%async_computation.21 | async-start | bytes 5308416 | tf_op jit(solution)/shard_map/all_gather | solution.py:139
  399.6 232.7 %reduce-scatter.8.cloned.1.call-start = ((), (), s32[]{:S(2)}) async-start(), calls=%async_computation.18 | async-start | bytes 1474560 | tf_op jit(solution)/shard_map/reduce_scatter | solution.py:160
  405.9 15.5 %all-to-all-start.7 = ((bf16[256,4,288]{0,2,1:T(8,128)(2,1)}), bf16[256,4,288]{0,2,1:T(8,128)(2,1)S(1)}, u32[]{:S(2)}, u32[]{:S(2)}) async-start(bf16[256,4,288]{0,2,1:T(8,128)(2,1)} %bitcast.33), calls=%async_computation.9 | async-start | bytes 1179648 | tf_op jit(solution)/shard_map/all_to_all | solution.py:147
  421.3 44.1 %all-to-all-start.9 = ((bf16[256,4,1152]{2,0,1:T(8,128)(2,1)}), bf16[256,4,1152]{2,0,1:T(8,128)(2,1)S(1)}, u32[]{:S(2)}, u32[]{:S(2)}) async-start(bf16[256,4,1152]{2,0,1:T(8,128)(2,1)} %bitcast.164), calls=%async_computation.13 | async-start | bytes 4718592 | tf_op jit(solution)/shard_map/all_to_all | solution.py:147
  425.0 216.3 %reduce-scatter.10.cloned.1.call-start = ((), (), s32[]{:S(2)}) async-start(), calls=%async_computation.20 | async-start | bytes 995328 | tf_op jit(solution)/shard_map/reduce_scatter | solution.py:150
  430.7 225.3 %reduce-scatter.14.cloned.1.call-start = ((), (), s32[]{:S(2)}) async-start(), calls=%async_computation.23 | async-start | bytes 2985984 | tf_op jit(solution)/shard_map/reduce_scatter | solution.py:150
  474.4 18.1 %all-to-all-start.6 = ((bf16[256,4,576]{0,2,1:T(8,128)(2,1)}), bf16[256,4,576]{0,2,1:T(8,128)(2,1)S(1)}, u32[]{:S(2)}, u32[]{:S(2)}) async-start(bf16[256,4,576]{0,2,1:T(8,128)(2,1)} %pad_maximum_fusion), calls=%async_computation.6 | async-start | bytes 2359296 | tf_op jit(solution)/shard_map/all_to_all | solution.py:147
  493.5 74.3 %all-to-all-start.8 = ((bf16[256,8,576]{0,2,1:T(8,128)(2,1)}), bf16[256,8,576]{0,2,1:T(8,128)(2,1)S(1)}, u32[]{:S(2)}, u32[]{:S(2)}) async-start(bf16[256,8,576]{0,2,1:T(8,128)(2,1)} %bitcast.35), calls=%async_computation.11 | async-start | bytes 4718592 | tf_op jit(solution)/shard_map/all_to_all | solution.py:140
  498.0 183.5 %reduce-scatter.6.cloned.1.call-start = ((), (), s32[]{:S(2)}) async-start(), calls=%async_computation.16 | async-start | bytes 1658880 | tf_op jit(solution)/shard_map/reduce_scatter | solution.py:150
  505.8 207.2 %reduce-scatter.12.cloned.1.call-start = ((), (), s32[]{:S(2)}) async-start(), calls=%async_computation.22 | async-start | bytes 1843200 | tf_op jit(solution)/shard_map/reduce_scatter | solution.py:142
  630.8 84.1 %copy-start.1 = (bf16[1152,1152]{1,0:T(8,128)(2,1)S(1)}, bf16[1152,1152]{1,0:T(8,128)(2,1)}, u32[]{:S(2)}) copy-start(bf16[1152,1152]{1,0:T(8,128)(2,1)} %param.29) | copy-start | bytes 7962628
  634.5 19.3 %collective-permute-start.2 = (f32[288,144]{1,0:T(8,128)}, f32[288,144]{1,0:T(8,128)}, u32[]{:S(2)}, u32[]{:S(2)}) collective-permute-start(f32[288,144]{1,0:T(8,128)} %get-tuple-element.301), channel_id=1, source_target_pairs={{0,8},{4,20},{8,0},{12,12},{16,24},{20,4},{24,16},{28,28},{1,9},{5... | collective-permute-start | bytes 497672 | tf_op jit(solution)/shard_map/ppermute | solution.py:171
  639.2 14.6 %collective-permute-start.1 = (f32[288,144]{1,0:T(8,128)S(1)}, f32[288,144]{1,0:T(8,128)}, u32[]{:S(2)}, u32[]{:S(2)}) collective-permute-start(f32[288,144]{1,0:T(8,128)S(1)} %get-tuple-element.302), channel_id=1, source_target_pairs={{0,20},{4,0},{8,12},{12,24},{16,4},{20,16},{24,28},{28,8},{1,21},{... | collective-permute-start | bytes 497672 | tf_op jit(solution)/shard_map/ppermute | solution.py:171
  639.3 14.5 %collective-permute-start = (f32[288,144]{1,0:T(8,128)S(1)}, f32[288,144]{1,0:T(8,128)}, u32[]{:S(2)}, u32[]{:S(2)}) collective-permute-start(f32[288,144]{1,0:T(8,128)S(1)} %get-tuple-element.300), channel_id=1, source_target_pairs={{0,0},{4,12},{8,24},{12,4},{16,16},{20,28},{24,8},{28,20},{1,1},{5... | collective-permute-start | bytes 497672 | tf_op jit(solution)/shard_map/ppermute | solution.py:171
  (62 other events, 596.9 us)
Sparse Core Ops, SparseCore 0:
  143.6 53.6 all-gather.8
  222.6 38.7 all-gather.10
  356.5 38.7 all-gather.14
  399.2 66.5 all-gather.6
  467.8 65.8 all-gather.12
  536.5 34.6 reduce-scatter.7
  573.5 32.1 reduce-scatter.9
  608.0 37.3 reduce-scatter.13
  647.7 33.7 reduce-scatter.5
  684.3 28.6 reduce-scatter.11

commit v5 on v4

--- a/solution.py
+++ b/solution.py
@@ -4,6 +4,7 @@
 import jax.numpy as jnp
 from jax import lax
 from jax.sharding import PartitionSpec as P
+
 
 HD = 72
 
@@ -135,18 +136,33 @@
     return (grad_query.reshape(length, head_cols), grad_keys, grad_values)
 
 
-def seq_gathered_grad(left, right):
+def scatter_sum(partial, axis, dim):
+    count = lax.axis_size(axis)
+    shape = partial.shape
+    pieces = partial.reshape(shape[:dim] + (count, shape[dim] // count) + shape[dim + 1 :])
+    swapped = lax.all_to_all(pieces, axis, split_axis=dim, concat_axis=dim, tiled=True)
+    return jnp.sum(swapped.astype(jnp.float32), axis=dim)
+
+
+EXCHANGE_SUM = ("hidden", "skip")
+
+
+def seq_gathered_grad(left, right, by_exchange):
     left_all = lax.all_gather(left, "seq", axis=0, tiled=True)
     right_cols = lax.all_to_all(right, "seq", split_axis=1, concat_axis=0, tiled=True)
     partial = contract_rows(left_all, right_cols).astype(jnp.bfloat16)
+    if by_exchange:
+        return scatter_sum(partial, "batch", 0)
     summed = lax.psum_scatter(partial, "batch", scatter_dimension=0, tiled=True)
     return summed.astype(jnp.float32)
 
 
-def batch_gathered_grad(left, right):
+def batch_gathered_grad(left, right, by_exchange):
     left_rows = lax.all_to_all(left, "batch", split_axis=1, concat_axis=0, tiled=True)
     right_all = lax.all_gather(right, "batch", axis=0, tiled=True)
     partial = contract_rows(left_rows, right_all).astype(jnp.bfloat16)
+    if by_exchange:
+        return scatter_sum(partial, "seq", 1)
     summed = lax.psum_scatter(partial, "seq", scatter_dimension=1, tiled=True)
     return summed.astype(jnp.float32)
 
@@ -177,11 +193,11 @@
 
 def weight_grad(name, left, right):
     if GRAD_PLAN[name] == "seq":
-        return seq_gathered_grad(left, right)
-    return batch_gathered_grad(left, right)
-
-
-def on_device(
+        return seq_gathered_grad(left, right, name in EXCHANGE_SUM)
+    return batch_gathered_grad(left, right, name in EXCHANGE_SUM)
+
+
+def block(
     tokens,
     long_skip,
     lengths,
@@ -350,6 +366,4 @@
         P("batch", "seq"),
         P(),
     )
-    return jax.shard_map(
-        on_device, mesh=mesh, in_specs=in_specs, out_specs=out_specs, check_vma=False
-    )
+    return jax.shard_map(block, mesh=mesh, in_specs=in_specs, out_specs=out_specs, check_vma=False)

time: 729 us -> 696 us (0.955)
  waiting for transfers between devices: 290 us -> 210 us
  blocking collectives: 58.1 us -> 95.2 us
  local copies, waits for them, and re-layouts: 64.7 us -> 72 us
    reduce_scatter x1 -> x0, waiting for transfers between devices: 29.8 us -> none  [seq_gathered_grad(): summed = lax.psum_scatter(partial, 'batch', scatter_dimension=0, tiled=True)]
    all_to_all x3 -> x2, waiting for transfers between devices: 54.5 us -> 25.4 us  [batch_gathered_grad(): lax.all_to_all(left, 'batch', split_axis=1, concat_axis=0, tiled=True)]
    all_to_all x1 -> x2, blocking collectives: 19.3 us -> 44.7 us  [the longest x1 25.4 us: batch_gathered_grad(): lax.all_to_all(left, 'batch', split_axis=1, concat_axis=0, tiled=True)]
    reduce_scatter x3 -> x2, waiting for transfers between devices: 23.6 us -> 0.01 us  [batch_gathered_grad(): summed = lax.psum_scatter(partial, 'seq', scatter_dimension=1, tiled=True)]
    psum x1, blocking collectives: 38.9 us -> 50.5 us  [block(): small_total = lax.psum(jnp.concatenate(small_grads), ('seq', 'batch'))]
    all_to_all x5 -> x7, starting transfers between devices: 22.8 us -> 30.7 us  [the longest x2 7.95 us: scatter_sum(): lax.all_to_all(pieces, axis, split_axis=dim, concat_axis=dim, tiled=True)]
    all_to_all x5 -> x7, waiting for transfers between devices: 107 us -> 107 us  [the longest x1 41.7 us: block(): lax.all_to_all(packed.reshape(local_rows, 3, seq_count, feature_count //...]
  transfers between devices with their start and end apart: 22 -> 21, of which waited for: 12 -> 9; matrix products, arithmetic and copies ran while one was open for 31% -> 34% of each run, Pallas kernels for 0% -> 0%
where the time goes in v5:
time: 696 us; the launch traced here: 689 us
  waiting for transfers between devices  210 us (30%)
  matrix products  195 us (28%)
  blocking collectives  95.2 us (14%)
  local copies, waits for them, and re-layouts  72 us (10%)
  other arithmetic  52.3 us (8%)
  starting transfers between devices  49.2 us (7%)
  between operations  15.3 us (2%)
    all_to_all x1, waiting for transfers between devices, seq_gathered_grad(): lax.all_to_all(right, 'seq', split_axis=1, concat_axis=0, tiled=True)  66 us
    psum x1, blocking collectives, block(): small_total = lax.psum(jnp.concatenate(small_grads), ('seq', 'batch'))  50.5 us
    all_to_all x1, waiting for transfers between devices, block(): lax.all_to_all(packed.reshape(local_rows, 3, seq_count, feature_count //...  41.7 us
    dot_general x5, matrix products, product(): return jnp.dot(left, right, preferred_element_type=jnp.float32)  40.9 us
    dot_general x5, matrix products, times_transposed(): lax.dot_general(left, right, (((1,), (1,)), ((), ())), preferred_element_...  38.6 us
    dot_general x5, matrix products, contract_rows(): lax.dot_general(left, right, (((0,), (0,)), ((), ())), preferred_element_...  28.6 us
    all_to_all x1, blocking collectives, batch_gathered_grad(): lax.all_to_all(left, 'batch', split_axis=1, concat_axis=0, tiled=True)  25.4 us
    all_to_all x2, waiting for transfers between devices, batch_gathered_grad(): lax.all_to_all(left, 'batch', split_axis=1, concat_axis=0, tiled=True)  25.4 us
  transfers between devices with their start and end apart: 21, of which 9 were waited for; matrix products, arithmetic and copies ran while one was open for 34% of the time, Pallas kernels for 0%

profile of v5, /device:TPU:0, one launch (start us, length us, event | category | flops | bytes accessed | tf_op | source)
XLA Modules:
  0.0 689.4 jit_solution(17010732412714007584)
XLA Ops:
  16.0 7.2 %convolution_convert_fusion.1 = bf16[256,3456]{1,0:T(8,128)(2,1)} fusion(bf16[256,1152]{1,0:T(8,128)(2,1)S(1)} %add_convert_fusion.3, bf16[1152,3456]{1,0:T(8,128)(2,1)} %param.28), kind=kOutput, calls=%fused_computation.53 | convolution fusion | flops 2039316480 | bytes 10321920 | tf_op jit(solution)/shard_map/dot_general | solution.py:16
  29.8 6.6 all-to-all-start
  36.7 41.7 %all-to-all-done = bf16[256,3,8,144]{0,3,1,2:T(8,128)(2,1)} async-done(((bf16[256,3,8,144]{0,3,1,2:T(8,128)(2,1)}), bf16[256,3,8,144]{0,3,1,2:T(8,128)(2,1)}, u32[]{:S(2)}, u32[]{:S(2)}) %all-to-all-start) | async-done | bytes 1769504 | tf_op jit(solution)/shard_map/all_to_all | solution.py:230
  93.7 36.5 %while.27 = (s32[]{:T(128)}, bf16[4,512,144]{1,2,0:T(8,128)(2,1)}, f32[4,2,512,1]{2,1,3,0:T(2,128)S(1)}, s32[4,512]{1,0:T(4,128)S(1)}, s32[2048]{0:T(1024)S(1)},...) while((s32[]{:T(128)}, bf16[4,512,144]{1,2,0:T(8,128)(2,1)}, ...), condition=%wide.region_7.8_spmd, body=%wide.region_4.7_spmd.sunk | while | flops 628169728 | bytes 33536144 | solution.py:78
  141.9 20.8 %all-to-all-done.1 = bf16[8,256,144]{1,2,0:T(8,128)(2,1)} async-done(((bf16[8,256,144]{1,2,0:T(8,128)(2,1)}), bf16[8,256,144]{1,2,0:T(8,128)(2,1)}, u32[]{:S(2)}, u32[]{:S(2)}) %all-to-all-start.1) | async-done | bytes 589856 | tf_op jit(solution)/shard_map/all_to_all | solution.py:242
  167.5 17.3 %multiply_convert_fusion.1 = (bf16[256,4608]{1,0:T(8,128)(2,1)}, f32[256,4608]{1,0:T(8,128)}, f32[256,4608]{1,0:T(8,128)}) fusion(f32[4608]{0:T(1024)S(1)} %convert_element_type.134, bf16[256,1152]{1,0:T(8,128)(2,1)} %add_convert_fusion.2, bf16[1152,4608]{1,0:T(8,128)(2,1)} %param.33), kind=kOutput, calls=%fused_computation.57 | convolution fusion | flops 2795765760 | bytes 23021568 | tf_op jit(solution)/shard_map/dot_general | solution.py:16
  184.8 14.7 %convert_reduce_fusion = (f32[4608]{0:T(1024)}, bf16[256,4608]{1,0:T(8,128)(2,1)}) fusion(f32[256,4608]{1,0:T(8,128)} %get-tuple-element.290, f32[256,4608]{1,0:T(8,128)} %get-tuple-element.315, bf16[4608,1152]{1,0:T(8,128)(2,1)} %param.35, bf16[1,256,1152]{2,1,0:T(8,128)(2,1)S(1)} %copy-done.15), kind=kOutput, calls=%fused_computation.55 | convolution fusion | flops 2736778752 | bytes 23021568 | tf_op jit(solution)/shard_map/dot_general | solution.py:26
  199.5 8.7 %multiply_reduce_fusion.1 = (f32[1152]{0:T(1024)}, f32[256]{0:T(256)S(1)}, f32[1152]{0:T(1024)}, f32[256,1152]{1,0:T(8,128)S(1)}) fusion(f32[256,1152]{1,0:T(8,128)S(1)} %copy-done.7, f32[256]{0:T(256)S(1)} %fusion.69, f32[256]{0:T(256)S(1)} %broadcast_multiply_fusion, f32[1152]{0:T(1024)S(1)} %convert_element_type.131, ...), kind=kOutput, calls=%fused_computation.108 | convolution fusion | flops 2720265728 | bytes 15352320 | tf_op jit(solution)/shard_map/dot_general | solution.py:26
  220.7 15.9 %all-to-all-done.2 = bf16[256,8,144]{0,2,1:T(8,128)(2,1)S(1)} async-done(((bf16[256,8,144]{0,2,1:T(8,128)(2,1)}), bf16[256,8,144]{0,2,1:T(8,128)(2,1)S(1)}, u32[]{:S(2)}, u32[]{:S(2)}) %all-to-all-start.2) | async-done | bytes 589856 | tf_op jit(solution)/shard_map/all_to_all | solution.py:268
  239.0 87.1 %while.28 = (s32[]{:T(128)}, f32[2048,2,72]{0,2,1:T(8,128)S(1)}, f32[2048,2,72]{0,2,1:T(8,128)}, bf16[4,512,144]{1,2,0:T(8,128)(2,1)}, bf16[4,512,2,72]{1,3,2,0:...) while((s32[]{:T(128)}, f32[2048,2,72]{0,2,1:T(8,128)S(1)}, ...), condition=%wide.region_14.15_spmd.clone, body=%wide.region_12.14_spmd.clone.sunk | while | flops 1543781376 | bytes 136800560 | solution.py:124
  334.0 15.5 %all-to-all-done.5 = bf16[8,256,144]{1,2,0:T(8,128)(2,1)} async-done(((bf16[8,256,144]{1,2,0:T(8,128)(2,1)}), bf16[8,256,144]{1,2,0:T(8,128)(2,1)}, u32[]{:S(2)}, u32[]{:S(2)}) %all-to-all-start.5) | async-done | bytes 589856 | tf_op jit(solution)/shard_map/all_to_all | solution.py:278
  357.2 13.3 %all-to-all-done.4 = bf16[8,256,144]{1,2,0:T(8,128)(2,1)} async-done(((bf16[8,256,144]{1,2,0:T(8,128)(2,1)}), bf16[8,256,144]{1,2,0:T(8,128)(2,1)}, u32[]{:S(2)}, u32[]{:S(2)}) %all-to-all-start.4) | async-done | bytes 589856 | tf_op jit(solution)/shard_map/all_to_all | solution.py:277
  370.5 19.3 %all_to_all.190 = bf16[8,256,144]{1,2,0:T(8,128)(2,1)S(1)} all-to-all(bf16[8,256,144]{1,2,0:T(8,128)(2,1)S(1)} %copy.114), channel_id=1, replica_groups=mesh['seq'=8,'batch'=4] {'seq'}, dimensions={0} | all-to-all | bytes 1179648 | tf_op jit(solution)/shard_map/all_to_all | solution.py:276
  389.8 6.5 multiply_reduce_fusion.2
  401.2 25.4 %all_to_all.191 = bf16[256,4,576]{0,2,1:T(8,128)(2,1)S(1)} all-to-all(bf16[256,4,576]{0,2,1:T(8,128)(2,1)S(1)} %pad_maximum_fusion), channel_id=1, replica_groups=mesh['seq'=8,'batch'=4] {'batch'}, dimensions={1} | all-to-all | bytes 2359296 | tf_op jit(solution)/shard_map/all_to_all | solution.py:161
  433.3 11.8 %all-to-all-done.8 = bf16[256,4,288]{0,2,1:T(8,128)(2,1)S(1)} async-done(((bf16[256,4,288]{0,2,1:T(8,128)(2,1)}), bf16[256,4,288]{0,2,1:T(8,128)(2,1)S(1)}, u32[]{:S(2)}, u32[]{:S(2)}) %all-to-all-start.8) | async-done | bytes 589856 | tf_op jit(solution)/shard_map/all_to_all | solution.py:161
  451.6 6.2 convolution_convert_fusion.4
  462.1 13.6 %all-to-all-done.11 = bf16[256,4,1152]{2,0,1:T(8,128)(2,1)} async-done(((bf16[256,4,1152]{2,0,1:T(8,128)(2,1)}), bf16[256,4,1152]{2,0,1:T(8,128)(2,1)}, u32[]{:S(2)}, u32[]{:S(2)}) %all-to-all-start.11) | async-done | bytes 2359328 | tf_op jit(solution)/shard_map/all_to_all | solution.py:161
  484.6 7.2 %convolution_convert_fusion = bf16[1152,1152]{0,1:T(8,128)(2,1)} fusion(bf16[1024,1152]{1,0:T(8,128)(2,1)} %bitcast.40, bf16[1,1024,1152]{2,1,0:T(8,128)(2,1)} %all-gather.15.cloned.1.call-done), kind=kOutput, calls=%fused_computation.50 | convolution fusion | flops 2719236096 | bytes 7372800 | tf_op jit(solution)/shard_map/dot_general | solution.py:20
  498.6 66.0 %all-to-all-done.9 = bf16[256,8,576]{0,2,1:T(8,128)(2,1)} async-done(((bf16[256,8,576]{0,2,1:T(8,128)(2,1)}), bf16[256,8,576]{0,2,1:T(8,128)(2,1)}, u32[]{:S(2)}, u32[]{:S(2)}) %all-to-all-start.9) | async-done | bytes 2359328 | tf_op jit(solution)/shard_map/all_to_all | solution.py:152
  568.2 9.1 %fusion.47 = bf16[1,256,1152]{2,1,0:T(8,128)(2,1)} fusion(f32[256,1152]{1,0:T(8,128)S(1)} %copy-done.8, bf16[256,4608]{1,0:T(8,128)(2,1)} %get-tuple-element.289, bf16[4608,1152]{1,0:T(8,128)(2,1)} %param.35, f32[1152]{0:T(1024)S(1)} %convert_element_type.136), kind=kOutput, calls=%fused_computation.84 | convolution fusion | flops 2718793728 | bytes 14750208 | tf_op jit(solution)/shard_map/dot_general | solution.py:16
  577.4 50.5 %psum.7 = f32[12672]{0:T(1024)S(1)} all-reduce(f32[12672]{0:T(1024)S(1)} %constant_dynamic-update-slice_fusion), channel_id=1, replica_groups=mesh['seq'=8,'batch'=4] {'seq','batch'}, use_global_device_ids=true, to_apply=%region_26.27 | all-reduce | flops 12672 | bytes 101376 | tf_op jit(solution)/shard_map/psum | solution.py:305
  637.7 7.4 %convolution_convert_fusion.3 = bf16[1152,576]{0,1:T(8,128)(2,1)} fusion(bf16[2048,576]{0,1:T(8,128)(2,1)} %bitcast.221, bf16[2048,1152]{1,0:T(8,128)(2,1)} %all-gather.13.cloned.1.call-done), kind=kOutput, calls=%fused_computation.72 | convolution fusion | flops 2718572544 | bytes 8404992 | tf_op jit(solution)/shard_map/dot_general | solution.py:20
  663.9 9.4 %collective-permute-done.2 = f32[288,144]{1,0:T(8,128)} collective-permute-done((f32[288,144]{1,0:T(8,128)S(1)}, f32[288,144]{1,0:T(8,128)}, u32[]{:S(2)}, u32[]{:S(2)}) %collective-permute-start.2) | collective-permute-done | bytes 165920 | tf_op jit(solution)/shard_map/ppermute | solution.py:187
  (327 shorter events, 279.4 us)
Async XLA Ops:
  7.2 155.5 %copy-start = (bf16[1152,1152]{1,0:T(8,128)(2,1)S(1)}, bf16[1152,1152]{1,0:T(8,128)(2,1)}, u32[]{:S(2)}) copy-start(bf16[1152,1152]{1,0:T(8,128)(2,1)} %param.29) | copy-start | bytes 7962628
  29.8 48.6 %all-to-all-start = ((bf16[256,3,8,144]{0,3,1,2:T(8,128)(2,1)}), bf16[256,3,8,144]{0,3,1,2:T(8,128)(2,1)}, u32[]{:S(2)}, u32[]{:S(2)}) async-start(bf16[256,3,8,144]{0,3,1,2:T(8,128)(2,1)} %copy.104), calls=%async_computation | async-start | bytes 3538944 | tf_op jit(solution)/shard_map/all_to_all | solution.py:230
  136.9 25.9 %all-to-all-start.1 = ((bf16[8,256,144]{1,2,0:T(8,128)(2,1)}), bf16[8,256,144]{1,2,0:T(8,128)(2,1)}, u32[]{:S(2)}, u32[]{:S(2)}) async-start(bf16[8,256,144]{1,2,0:T(8,128)(2,1)} %copy.108), calls=%async_computation.1 | async-start | bytes 1179648 | tf_op jit(solution)/shard_map/all_to_all | solution.py:242
  141.1 310.5 %all-gather.9.cloned.1.call-start = ((), (), s32[]{:S(2)}) async-start(), calls=%async_computation.16 | async-start | bytes 5308416 | tf_op jit(solution)/shard_map/all_gather | solution.py:174
  216.4 20.2 %all-to-all-start.2 = ((bf16[256,8,144]{0,2,1:T(8,128)(2,1)}), bf16[256,8,144]{0,2,1:T(8,128)(2,1)S(1)}, u32[]{:S(2)}, u32[]{:S(2)}) async-start(bf16[256,8,144]{0,2,1:T(8,128)(2,1)} %bitcast.18), calls=%async_computation.2 | async-start | bytes 1179648 | tf_op jit(solution)/shard_map/all_to_all | solution.py:268
  220.0 260.2 %all-gather.11.cloned.1.call-start = ((), (), s32[]{:S(2)}) async-start(), calls=%async_computation.18 | async-start | bytes 2949120 | tf_op jit(solution)/shard_map/all_gather | solution.py:162
  328.6 20.9 %all-to-all-start.5 = ((bf16[8,256,144]{1,2,0:T(8,128)(2,1)}), bf16[8,256,144]{1,2,0:T(8,128)(2,1)}, u32[]{:S(2)}, u32[]{:S(2)}) async-start(bf16[8,256,144]{1,2,0:T(8,128)(2,1)} %copy.116), calls=%async_computation.5 | async-start | bytes 1179648 | tf_op jit(solution)/shard_map/all_to_all | solution.py:278
  349.5 20.9 %all-to-all-start.4 = ((bf16[8,256,144]{1,2,0:T(8,128)(2,1)}), bf16[8,256,144]{1,2,0:T(8,128)(2,1)}, u32[]{:S(2)}, u32[]{:S(2)}) async-start(bf16[8,256,144]{1,2,0:T(8,128)(2,1)} %copy.115), calls=%async_computation.4 | async-start | bytes 1179648 | tf_op jit(solution)/shard_map/all_to_all | solution.py:277
  353.8 130.8 %all-gather.15.cloned.1.call-start = ((), (), s32[]{:S(2)}) async-start(), calls=%async_computation.22 | async-start | bytes 2949120 | tf_op jit(solution)/shard_map/all_gather | solution.py:162
  354.5 138.6 %all-gather.7.cloned.1.call-start = ((), (), s32[]{:S(2)}) async-start(), calls=%async_computation.15 | async-start | bytes 2949120 | tf_op jit(solution)/shard_map/all_gather | solution.py:162
  398.9 238.8 %all-gather.13.cloned.1.call-start = ((), (), s32[]{:S(2)}) async-start(), calls=%async_computation.20 | async-start | bytes 5308416 | tf_op jit(solution)/shard_map/all_gather | solution.py:151
  426.6 18.6 %all-to-all-start.8 = ((bf16[256,4,288]{0,2,1:T(8,128)(2,1)}), bf16[256,4,288]{0,2,1:T(8,128)(2,1)S(1)}, u32[]{:S(2)}, u32[]{:S(2)}) async-start(bf16[256,4,288]{0,2,1:T(8,128)(2,1)} %bitcast.34), calls=%async_computation.9 | async-start | bytes 1179648 | tf_op jit(solution)/shard_map/all_to_all | solution.py:161
  446.0 29.7 %all-to-all-start.11 = ((bf16[256,4,1152]{2,0,1:T(8,128)(2,1)}), bf16[256,4,1152]{2,0,1:T(8,128)(2,1)}, u32[]{:S(2)}, u32[]{:S(2)}) async-start(bf16[256,4,1152]{2,0,1:T(8,128)(2,1)} %bitcast.166), calls=%async_computation.13 | async-start | bytes 4718592 | tf_op jit(solution)/shard_map/all_to_all | solution.py:161
  450.7 204.7 %reduce-scatter.4.cloned.1.call-start = ((), (), s32[]{:S(2)}) async-start(), calls=%async_computation.17 | async-start | bytes 1474560 | tf_op jit(solution)/shard_map/reduce_scatter | solution.py:176
  475.6 88.9 %all-to-all-start.9 = ((bf16[256,8,576]{0,2,1:T(8,128)(2,1)}), bf16[256,8,576]{0,2,1:T(8,128)(2,1)}, u32[]{:S(2)}, u32[]{:S(2)}) async-start(bf16[256,8,576]{0,2,1:T(8,128)(2,1)} %bitcast.36), calls=%async_computation.11 | async-start | bytes 4718592 | tf_op jit(solution)/shard_map/all_to_all | solution.py:152
  480.0 182.2 %reduce-scatter.6.cloned.1.call-start = ((), (), s32[]{:S(2)}) async-start(), calls=%async_computation.19 | async-start | bytes 995328 | tf_op jit(solution)/shard_map/reduce_scatter | solution.py:166
  484.3 191.3 %reduce-scatter.8.cloned.1.call-start = ((), (), s32[]{:S(2)}) async-start(), calls=%async_computation.21 | async-start | bytes 2985984 | tf_op jit(solution)/shard_map/reduce_scatter | solution.py:166
  496.9 71.2 %copy-start.8 = (f32[256,1152]{1,0:T(8,128)S(1)}, f32[256,1152]{1,0:T(8,128)}, u32[]{:S(2)}) copy-start(f32[256,1152]{1,0:T(8,128)} %copy-done.6) | copy-start | bytes 3538948
  564.5 83.2 %all-to-all-start.7 = ((bf16[576,8,144]{0,2,1:T(8,128)(2,1)}), bf16[576,8,144]{0,2,1:T(8,128)(2,1)S(1)}, u32[]{:S(2)}, u32[]{:S(2)}) async-start(bf16[576,8,144]{0,2,1:T(8,128)(2,1)} %bitcast.212), calls=%async_computation.7 | async-start | bytes 2949120 | tf_op jit(solution)/shard_map/all_to_all | solution.py:143
  568.2 60.4 %copy-start.24 = (bf16[256,1152]{1,0:T(8,128)(2,1)S(1)}, bf16[256,1152]{1,0:T(8,128)(2,1)}, u32[]{:S(2)}) copy-start(bf16[256,1152]{1,0:T(8,128)(2,1)} %get-tuple-element.284) | copy-start | bytes 1769476
  647.8 32.0 %all-to-all-start.10 = ((bf16[4,288,576]{2,1,0:T(8,128)(2,1)}), bf16[4,288,576]{2,1,0:T(8,128)(2,1)}, u32[]{:S(2)}, u32[]{:S(2)}) async-start(bf16[4,288,576]{2,1,0:T(8,128)(2,1)} %bitcast.211), calls=%async_computation.12 | async-start | bytes 2949120 | tf_op jit(solution)/shard_map/all_to_all | solution.py:143
  656.7 16.6 %collective-permute-start.2 = (f32[288,144]{1,0:T(8,128)S(1)}, f32[288,144]{1,0:T(8,128)}, u32[]{:S(2)}, u32[]{:S(2)}) collective-permute-start(f32[288,144]{1,0:T(8,128)S(1)} %get-tuple-element.301), channel_id=1, source_target_pairs={{0,8},{4,20},{8,0},{12,12},{16,24},{20,4},{24,16},{28,28},{1,9},{5... | collective-permute-start | bytes 497672 | tf_op jit(solution)/shard_map/ppermute | solution.py:187
  658.7 14.6 %collective-permute-start.1 = (f32[288,144]{1,0:T(8,128)S(1)}, f32[288,144]{1,0:T(8,128)}, u32[]{:S(2)}, u32[]{:S(2)}) collective-permute-start(f32[288,144]{1,0:T(8,128)S(1)} %get-tuple-element.302), channel_id=1, source_target_pairs={{0,20},{4,0},{8,12},{12,24},{16,4},{20,16},{24,28},{28,8},{1,21},{... | collective-permute-start | bytes 497672 | tf_op jit(solution)/shard_map/ppermute | solution.py:187
  660.2 13.2 %collective-permute-start = (f32[288,144]{1,0:T(8,128)S(1)}, f32[288,144]{1,0:T(8,128)}, u32[]{:S(2)}, u32[]{:S(2)}) collective-permute-start(f32[288,144]{1,0:T(8,128)S(1)} %get-tuple-element.300), channel_id=1, source_target_pairs={{0,0},{4,12},{8,24},{12,4},{16,16},{20,28},{24,8},{28,20},{1,1},{5... | collective-permute-start | bytes 497672 | tf_op jit(solution)/shard_map/ppermute | solution.py:187
  (61 other events, 499.0 us)
Sparse Core Ops, SparseCore 0:
  143.5 53.6 all-gather.8
  222.6 38.7 all-gather.10
  356.4 38.7 all-gather.14
  399.0 51.6 all-gather.6
  452.7 103.2 all-gather.12
  558.8 27.8 reduce-scatter.3
  588.9 33.0 reduce-scatter.5
  624.2 36.1 reduce-scatter.7

commit v6 on v4

--- a/solution.py
+++ b/solution.py
@@ -5,7 +5,9 @@
 from jax import lax
 from jax.sharding import PartitionSpec as P
 
+
 HD = 72
+ATTENTION_BLOCK = 256
 
 
 norm_eps = 1e-05
@@ -58,7 +60,7 @@
 def attend_forward(query_heads, key_flat, value_flat, segment):
     length, head_cols = query_heads.shape
     head_count = head_cols // HD
-    block_rows = min(512, length)
+    block_rows = min(ATTENTION_BLOCK, length)
     block_count = length // block_rows
     key_heads = key_flat.reshape(length, head_count, HD)
     value_heads = value_flat.reshape(length, head_count, HD)
@@ -87,7 +89,7 @@
 def attend_backward(query_heads, key_flat, value_flat, segment, grad_context, log_total):
     length, head_cols = query_heads.shape
     head_count = head_cols // HD
-    block_rows = min(512, length)
+    block_rows = min(ATTENTION_BLOCK, length)
     block_count = length // block_rows
     score_scale = 1.0 / math.sqrt(HD)
     key_heads = key_flat.reshape(length, head_count, HD)
@@ -181,7 +183,7 @@
     return batch_gathered_grad(left, right)
 
 
-def on_device(
+def block(
     tokens,
     long_skip,
     lengths,
@@ -350,6 +352,4 @@
         P("batch", "seq"),
         P(),
     )
-    return jax.shard_map(
-        on_device, mesh=mesh, in_specs=in_specs, out_specs=out_specs, check_vma=False
-    )
+    return jax.shard_map(block, mesh=mesh, in_specs=in_specs, out_specs=out_specs, check_vma=False)

time: 729 us -> 753 us (1.033)
  matrix products: 195 us -> 227 us
  other arithmetic: 52 us -> 35.5 us
    dot_general x8 -> x16, matrix products: 20.7 us -> 37.4 us  [score_block(): jnp.einsum('bhd,khd->hbk', query_block, key_heads, preferred_element_type...]
    convert_element_type x4 -> x8, other arithmetic: 15.5 us -> 3.39 us  [one_block(): grad_scores = (prob_full * (grad_probs - row_delta)).astype(jnp.bfloat16)]
    while x49 -> x32, local copies, waits for them, and re-layouts: 0.55 us -> 12.5 us  [the longest x1 0.46 us: attend_backward(): lax.scan(one_block, (empty_sum, empty_sum), (query_heads.reshape(block_co...]
    dot_general x4 -> x8, matrix products: 13.4 us -> 23.4 us  [one_block(): jnp.einsum('hbk,bhd->khd', grad_scores, query_block, preferred_element_ty...]
    dot_general x4 -> x8, matrix products: 9.16 us -> 15.6 us  [one_block(): jnp.einsum('hbk,khd->bhd', probs_low, value_heads, preferred_element_type...]
    dot_general x4 -> x8, matrix products: 17.1 us -> 14.8 us  [one_block(): jnp.einsum('bhd,khd->hbk', grad_block, value_heads, preferred_element_typ...]
    dot_general x4 -> x8, matrix products: 20.6 us -> 22.6 us  [one_block(): jnp.einsum('hbk,bhd->khd', probs_low, grad_block, preferred_element_type=...]
where the time goes in v6:
time: 753 us; the launch traced here: 743 us
  waiting for transfers between devices  293 us (39%)
  matrix products  227 us (30%)
  local copies, waits for them, and re-layouts  67.7 us (9%)
  blocking collectives  57.5 us (8%)
  starting transfers between devices  46.4 us (6%)
  other arithmetic  35.5 us (5%)
  between operations  15.2 us (2%)
    all_to_all x1, waiting for transfers between devices, seq_gathered_grad(): lax.all_to_all(right, 'seq', split_axis=1, concat_axis=0, tiled=True)  61.5 us
    all_to_all x3, waiting for transfers between devices, batch_gathered_grad(): lax.all_to_all(left, 'batch', split_axis=1, concat_axis=0, tiled=True)  54.3 us
    all_to_all x1, waiting for transfers between devices, block(): lax.all_to_all(packed.reshape(local_rows, 3, seq_count, feature_count //...  41.8 us
    dot_general x5, matrix products, product(): return jnp.dot(left, right, preferred_element_type=jnp.float32)  40.6 us
    psum x1, blocking collectives, block(): small_total = lax.psum(jnp.concatenate(small_grads), ('seq', 'batch'))  38.4 us
    dot_general x16, matrix products, score_block(): jnp.einsum('bhd,khd->hbk', query_block, key_heads, preferred_element_type...  37.4 us
    dot_general x5, matrix products, times_transposed(): lax.dot_general(left, right, (((1,), (1,)), ((), ())), preferred_element_...  35.8 us
    dot_general x5, matrix products, contract_rows(): lax.dot_general(left, right, (((0,), (0,)), ((), ())), preferred_element_...  30.8 us
  transfers between devices with their start and end apart: 22, of which 12 were waited for; matrix products, arithmetic and copies ran while one was open for 31% of the time, Pallas kernels for 0%

profile of v6, /device:TPU:0, one launch (start us, length us, event | category | flops | bytes accessed | tf_op | source)
XLA Modules:
  0.0 742.7 jit_solution(4550428058418218396)
XLA Ops:
  16.0 7.2 convolution_convert_fusion.1
  29.8 6.5 all-to-all-start
  36.6 41.8 %all-to-all-done = bf16[256,3,8,144]{0,3,1,2:T(8,128)(2,1)} async-done(((bf16[256,3,8,144]{0,3,1,2:T(8,128)(2,1)}), bf16[256,3,8,144]{0,3,1,2:T(8,128)(2,1)}, u32[]{:S(2)}, u32[]{:S(2)}) %all-to-all-start) | async-done | bytes 1769504 | tf_op jit(solution)/shard_map/all_to_all | solution.py:216
  89.9 45.8 %while.27 = (s32[]{:T(128)}, bf16[8,256,144]{1,2,0:T(8,128)(2,1)}, f32[8,2,256,1]{2,1,3,0:T(2,128)S(1)}, s32[8,256]{1,0:T(8,128)S(1)}, s32[2048]{0:T(1024)S(1)},...) while((s32[]{:T(128)}, bf16[8,256,144]{1,2,0:T(8,128)(2,1)}, ...), condition=%wide.region_7.8_spmd, body=%wide.region_4.7_spmd.sunk | while | flops 309890560 | bytes 15133813 | solution.py:79
  140.7 20.8 %all-to-all-done.1 = bf16[8,256,144]{1,2,0:T(8,128)(2,1)} async-done(((bf16[8,256,144]{1,2,0:T(8,128)(2,1)}), bf16[8,256,144]{1,2,0:T(8,128)(2,1)}, u32[]{:S(2)}, u32[]{:S(2)}) %all-to-all-start.1) | async-done | bytes 589856 | tf_op jit(solution)/shard_map/all_to_all | solution.py:228
  166.3 17.1 %multiply_convert_fusion.1 = (bf16[256,4608]{1,0:T(8,128)(2,1)}, f32[256,4608]{1,0:T(8,128)}, f32[256,4608]{1,0:T(8,128)}) fusion(f32[4608]{0:T(1024)S(1)} %convert_element_type.134, bf16[256,1152]{1,0:T(8,128)(2,1)} %add_convert_fusion.2, bf16[1152,4608]{1,0:T(8,128)(2,1)} %param.33), kind=kOutput, calls=%fused_computation.48 | convolution fusion | flops 2795765760 | bytes 23021568 | tf_op jit(solution)/shard_map/dot_general | solution.py:17
  183.4 14.1 %convert_reduce_fusion = (f32[4608]{0:T(1024)S(1)}, bf16[256,4608]{1,0:T(8,128)(2,1)}) fusion(f32[256,4608]{1,0:T(8,128)} %get-tuple-element.290, f32[256,4608]{1,0:T(8,128)} %get-tuple-element.315, bf16[4608,1152]{1,0:T(8,128)(2,1)} %param.35, bf16[1,256,1152]{2,1,0:T(8,128)(2,1)S(1)} %copy-done.13), kind=kOutput, calls=%fused_computation.46 | convolution fusion | flops 2736778752 | bytes 23021568 | tf_op jit(solution)/shard_map/dot_general | solution.py:27
  197.5 8.1 %multiply_reduce_fusion.1 = (f32[1152]{0:T(1024)S(1)}, f32[256]{0:T(256)S(1)}, f32[1152]{0:T(1024)S(1)}, f32[256,1152]{1,0:T(8,128)S(1)}) fusion(f32[256,1152]{1,0:T(8,128)S(1)} %copy-done.6, f32[256]{0:T(256)S(1)} %fusion.54, f32[256]{0:T(256)S(1)} %broadcast_multiply_fusion, f32[1152]{0:T(1024)S(1)} %convert_element_type.131, ...), kind=kOutput, calls=%fused_computation.97 | convolution fusion | flops 2720265728 | bytes 15352320 | tf_op jit(solution)/shard_map/dot_general | solution.py:27
  218.2 16.0 %all-to-all-done.2 = bf16[256,8,144]{0,2,1:T(8,128)(2,1)} async-done(((bf16[256,8,144]{0,2,1:T(8,128)(2,1)}), bf16[256,8,144]{0,2,1:T(8,128)(2,1)}, u32[]{:S(2)}, u32[]{:S(2)}) %all-to-all-start.2) | async-done | bytes 589856 | tf_op jit(solution)/shard_map/all_to_all | solution.py:254
  235.1 112.7 %while.28 = (s32[]{:T(128)}, f32[2048,2,72]{0,2,1:T(8,128)}, f32[2048,2,72]{0,2,1:T(8,128)}, bf16[8,256,144]{1,2,0:T(8,128)(2,1)}, bf16[8,256,2,72]{1,3,2,0:T(8,...) while((s32[]{:T(128)}, f32[2048,2,72]{0,2,1:T(8,128)}, ...), condition=%wide.region_14.15_spmd.clone, body=%wide.region_12.14_spmd.clone.sunk | while | flops 766189056 | bytes 73086176 | solution.py:125
  355.8 15.5 %all-to-all-done.5 = bf16[8,256,144]{1,2,0:T(8,128)(2,1)} async-done(((bf16[8,256,144]{1,2,0:T(8,128)(2,1)}), bf16[8,256,144]{1,2,0:T(8,128)(2,1)}, u32[]{:S(2)}, u32[]{:S(2)}) %all-to-all-start.5) | async-done | bytes 589856 | tf_op jit(solution)/shard_map/all_to_all | solution.py:264
  375.6 15.9 %all-to-all-done.4 = bf16[8,256,144]{1,2,0:T(8,128)(2,1)S(1)} async-done(((bf16[8,256,144]{1,2,0:T(8,128)(2,1)}), bf16[8,256,144]{1,2,0:T(8,128)(2,1)S(1)}, u32[]{:S(2)}, u32[]{:S(2)}) %all-to-all-start.4) | async-done | bytes 589856 | tf_op jit(solution)/shard_map/all_to_all | solution.py:263
  391.5 19.1 %all_to_all.174 = bf16[8,256,144]{1,2,0:T(8,128)(2,1)S(1)} all-to-all(bf16[8,256,144]{1,2,0:T(8,128)(2,1)S(1)} %copy-done.12), channel_id=1, replica_groups=mesh['seq'=8,'batch'=4] {'seq'}, dimensions={0} | all-to-all | bytes 1179648 | tf_op jit(solution)/shard_map/all_to_all | solution.py:262
  432.5 9.4 %all-to-all-done.7 = bf16[256,4,288]{0,2,1:T(8,128)(2,1)S(1)} async-done(((bf16[256,4,288]{0,2,1:T(8,128)(2,1)}), bf16[256,4,288]{0,2,1:T(8,128)(2,1)S(1)}, u32[]{:S(2)}, u32[]{:S(2)}) %all-to-all-start.7) | async-done | bytes 589856 | tf_op jit(solution)/shard_map/all_to_all | solution.py:149
  451.2 34.7 %all-to-all-done.9 = bf16[256,4,1152]{2,0,1:T(8,128)(2,1)S(1)} async-done(((bf16[256,4,1152]{2,0,1:T(8,128)(2,1)}), bf16[256,4,1152]{2,0,1:T(8,128)(2,1)S(1)}, u32[]{:S(2)}, u32[]{:S(2)}) %all-to-all-start.9) | async-done | bytes 2359328 | tf_op jit(solution)/shard_map/all_to_all | solution.py:149
  486.0 6.5 convolution_convert_fusion
  502.9 10.2 %all-to-all-done.6 = bf16[256,4,576]{0,2,1:T(8,128)(2,1)S(1)} async-done(((bf16[256,4,576]{0,2,1:T(8,128)(2,1)}), bf16[256,4,576]{0,2,1:T(8,128)(2,1)S(1)}, u32[]{:S(2)}, u32[]{:S(2)}) %all-to-all-start.6) | async-done | bytes 1179680 | tf_op jit(solution)/shard_map/all_to_all | solution.py:149
  526.8 61.5 %all-to-all-done.8 = bf16[256,8,576]{0,2,1:T(8,128)(2,1)S(1)} async-done(((bf16[256,8,576]{0,2,1:T(8,128)(2,1)}), bf16[256,8,576]{0,2,1:T(8,128)(2,1)S(1)}, u32[]{:S(2)}, u32[]{:S(2)}) %all-to-all-start.8) | async-done | bytes 2359328 | tf_op jit(solution)/shard_map/all_to_all | solution.py:142
  590.1 8.3 %convolution_convert_fusion.2 = bf16[1152,576]{1,0:T(8,128)(2,1)} fusion(bf16[2048,1152]{1,0:T(8,128)(2,1)} %all-gather.13.cloned.1.call-done, bf16[2048,576]{0,1:T(8,128)(2,1)} %bitcast.219), kind=kOutput, calls=%fused_computation.62 | convolution fusion | flops 2718572544 | bytes 8404992 | tf_op jit(solution)/shard_map/dot_general | solution.py:21
  598.4 8.9 %fusion.32 = bf16[1,256,1152]{2,1,0:T(8,128)(2,1)} fusion(f32[256,1152]{1,0:T(8,128)S(1)} %copy-done.7, bf16[256,4608]{1,0:T(8,128)(2,1)} %get-tuple-element.289, bf16[4608,1152]{1,0:T(8,128)(2,1)} %param.35, f32[1152]{0:T(1024)S(1)} %convert_element_type.136), kind=kOutput, calls=%fused_computation.73 | convolution fusion | flops 2718793728 | bytes 14750208 | tf_op jit(solution)/shard_map/dot_general | solution.py:17
  607.4 38.4 %psum.7 = f32[12672]{0:T(1024)S(1)} all-reduce(f32[12672]{0:T(1024)S(1)} %constant_dynamic-update-slice_fusion), channel_id=1, replica_groups=mesh['seq'=8,'batch'=4] {'seq','batch'}, use_global_device_ids=true, to_apply=%region_26.27 | all-reduce | flops 12672 | bytes 101376 | tf_op jit(solution)/shard_map/psum | solution.py:291
  663.3 11.0 %collective-permute-done.2 = f32[288,144]{1,0:T(8,128)} collective-permute-done((f32[288,144]{1,0:T(8,128)}, f32[288,144]{1,0:T(8,128)}, u32[]{:S(2)}, u32[]{:S(2)}) %collective-permute-start.2) | collective-permute-done | bytes 165920 | tf_op jit(solution)/shard_map/ppermute | solution.py:173
  678.4 23.8 %reduce-scatter.6.cloned.1.call-done = bf16[576,144]{0,1:T(8,128)(2,1)} async-done(((bf16[576,1152]{0,1:T(8,128)(2,1)}), bf16[576,144]{0,1:T(8,128)(2,1)}) %reduce-scatter.6.cloned.1.call-update) | async-done | bytes 165904 | tf_op jit(solution)/shard_map/reduce_scatter | solution.py:152
  703.8 30.0 %reduce-scatter.12.cloned.1.call-done = bf16[288,576]{1,0:T(8,128)(2,1)} async-done(((bf16[1152,576]{1,0:T(8,128)(2,1)}), bf16[288,576]{1,0:T(8,128)(2,1)}) %reduce-scatter.12.cloned.1.call-update) | async-done | bytes 331792 | tf_op jit(solution)/shard_map/reduce_scatter | solution.py:144
  (365 shorter events, 302.3 us)
Async XLA Ops:
  7.2 154.3 %copy-start = (bf16[1152,1152]{1,0:T(8,128)(2,1)S(1)}, bf16[1152,1152]{1,0:T(8,128)(2,1)}, u32[]{:S(2)}) copy-start(bf16[1152,1152]{1,0:T(8,128)(2,1)} %param.29) | copy-start | bytes 7962628
  29.8 48.6 %all-to-all-start = ((bf16[256,3,8,144]{0,3,1,2:T(8,128)(2,1)}), bf16[256,3,8,144]{0,3,1,2:T(8,128)(2,1)}, u32[]{:S(2)}, u32[]{:S(2)}) async-start(bf16[256,3,8,144]{0,3,1,2:T(8,128)(2,1)} %copy.82), calls=%async_computation | async-start | bytes 3538944 | tf_op jit(solution)/shard_map/all_to_all | solution.py:216
  135.6 25.9 %all-to-all-start.1 = ((bf16[8,256,144]{1,2,0:T(8,128)(2,1)}), bf16[8,256,144]{1,2,0:T(8,128)(2,1)}, u32[]{:S(2)}, u32[]{:S(2)}) async-start(bf16[8,256,144]{1,2,0:T(8,128)(2,1)} %get-tuple-element.118), calls=%async_computation.1 | async-start | bytes 1179648 | tf_op jit(solution)/shard_map/all_to_all | solution.py:228
  139.8 280.9 %all-gather.9.cloned.1.call-start = ((), (), s32[]{:S(2)}) async-start(), calls=%async_computation.17 | async-start | bytes 5308416 | tf_op jit(solution)/shard_map/all_gather | solution.py:160
  213.3 20.9 %all-to-all-start.2 = ((bf16[256,8,144]{0,2,1:T(8,128)(2,1)}), bf16[256,8,144]{0,2,1:T(8,128)(2,1)}, u32[]{:S(2)}, u32[]{:S(2)}) async-start(bf16[256,8,144]{0,2,1:T(8,128)(2,1)} %bitcast.18), calls=%async_computation.2 | async-start | bytes 1179648 | tf_op jit(solution)/shard_map/all_to_all | solution.py:254
  217.5 229.0 %all-gather.11.cloned.1.call-start = ((), (), s32[]{:S(2)}) async-start(), calls=%async_computation.19 | async-start | bytes 2949120 | tf_op jit(solution)/shard_map/all_gather | solution.py:150
  350.3 20.9 %all-to-all-start.5 = ((bf16[8,256,144]{1,2,0:T(8,128)(2,1)}), bf16[8,256,144]{1,2,0:T(8,128)(2,1)}, u32[]{:S(2)}, u32[]{:S(2)}) async-start(bf16[8,256,144]{1,2,0:T(8,128)(2,1)} %copy.88), calls=%async_computation.5 | async-start | bytes 1179648 | tf_op jit(solution)/shard_map/all_to_all | solution.py:264
  371.3 20.2 %all-to-all-start.4 = ((bf16[8,256,144]{1,2,0:T(8,128)(2,1)}), bf16[8,256,144]{1,2,0:T(8,128)(2,1)S(1)}, u32[]{:S(2)}, u32[]{:S(2)}) async-start(bf16[8,256,144]{1,2,0:T(8,128)(2,1)} %copy.87), calls=%async_computation.4 | async-start | bytes 1179648 | tf_op jit(solution)/shard_map/all_to_all | solution.py:263
  374.8 76.4 %all-gather.15.cloned.1.call-start = ((), (), s32[]{:S(2)}) async-start(), calls=%async_computation.24 | async-start | bytes 2949120 | tf_op jit(solution)/shard_map/all_gather | solution.py:150
  375.5 145.6 %all-gather.7.cloned.1.call-start = ((), (), s32[]{:S(2)}) async-start(), calls=%async_computation.15 | async-start | bytes 2949120 | tf_op jit(solution)/shard_map/all_gather | solution.py:150
  419.6 170.5 %all-gather.13.cloned.1.call-start = ((), (), s32[]{:S(2)}) async-start(), calls=%async_computation.21 | async-start | bytes 5308416 | tf_op jit(solution)/shard_map/all_gather | solution.py:141
  420.2 232.1 %reduce-scatter.8.cloned.1.call-start = ((), (), s32[]{:S(2)}) async-start(), calls=%async_computation.18 | async-start | bytes 1474560 | tf_op jit(solution)/shard_map/reduce_scatter | solution.py:162
  426.8 15.0 %all-to-all-start.7 = ((bf16[256,4,288]{0,2,1:T(8,128)(2,1)}), bf16[256,4,288]{0,2,1:T(8,128)(2,1)S(1)}, u32[]{:S(2)}, u32[]{:S(2)}) async-start(bf16[256,4,288]{0,2,1:T(8,128)(2,1)} %bitcast.34), calls=%async_computation.9 | async-start | bytes 1179648 | tf_op jit(solution)/shard_map/all_to_all | solution.py:149
  441.9 44.1 %all-to-all-start.9 = ((bf16[256,4,1152]{2,0,1:T(8,128)(2,1)}), bf16[256,4,1152]{2,0,1:T(8,128)(2,1)S(1)}, u32[]{:S(2)}, u32[]{:S(2)}) async-start(bf16[256,4,1152]{2,0,1:T(8,128)(2,1)} %bitcast.164), calls=%async_computation.13 | async-start | bytes 4718592 | tf_op jit(solution)/shard_map/all_to_all | solution.py:149
  445.5 216.2 %reduce-scatter.10.cloned.1.call-start = ((), (), s32[]{:S(2)}) async-start(), calls=%async_computation.20 | async-start | bytes 995328 | tf_op jit(solution)/shard_map/reduce_scatter | solution.py:152
  451.1 225.4 %reduce-scatter.14.cloned.1.call-start = ((), (), s32[]{:S(2)}) async-start(), calls=%async_computation.23 | async-start | bytes 2985984 | tf_op jit(solution)/shard_map/reduce_scatter | solution.py:152
  495.1 18.0 %all-to-all-start.6 = ((bf16[256,4,576]{0,2,1:T(8,128)(2,1)}), bf16[256,4,576]{0,2,1:T(8,128)(2,1)S(1)}, u32[]{:S(2)}, u32[]{:S(2)}) async-start(bf16[256,4,576]{0,2,1:T(8,128)(2,1)} %pad_maximum_fusion), calls=%async_computation.6 | async-start | bytes 2359296 | tf_op jit(solution)/shard_map/all_to_all | solution.py:149
  514.2 74.2 %all-to-all-start.8 = ((bf16[256,8,576]{0,2,1:T(8,128)(2,1)}), bf16[256,8,576]{0,2,1:T(8,128)(2,1)S(1)}, u32[]{:S(2)}, u32[]{:S(2)}) async-start(bf16[256,8,576]{0,2,1:T(8,128)(2,1)} %bitcast.36), calls=%async_computation.11 | async-start | bytes 4718592 | tf_op jit(solution)/shard_map/all_to_all | solution.py:142
  518.7 183.5 %reduce-scatter.6.cloned.1.call-start = ((), (), s32[]{:S(2)}) async-start(), calls=%async_computation.16 | async-start | bytes 1658880 | tf_op jit(solution)/shard_map/reduce_scatter | solution.py:152
  526.4 207.4 %reduce-scatter.12.cloned.1.call-start = ((), (), s32[]{:S(2)}) async-start(), calls=%async_computation.22 | async-start | bytes 1843200 | tf_op jit(solution)/shard_map/reduce_scatter | solution.py:144
  653.3 82.4 %copy-start.1 = (bf16[1152,1152]{1,0:T(8,128)(2,1)S(1)}, bf16[1152,1152]{1,0:T(8,128)(2,1)}, u32[]{:S(2)}) copy-start(bf16[1152,1152]{1,0:T(8,128)(2,1)} %param.29) | copy-start | bytes 7962628
  654.3 19.9 %collective-permute-start.2 = (f32[288,144]{1,0:T(8,128)}, f32[288,144]{1,0:T(8,128)}, u32[]{:S(2)}, u32[]{:S(2)}) collective-permute-start(f32[288,144]{1,0:T(8,128)} %get-tuple-element.301), channel_id=1, source_target_pairs={{0,8},{4,20},{8,0},{12,12},{16,24},{20,4},{24,16},{28,28},{1,9},{5... | collective-permute-start | bytes 497672 | tf_op jit(solution)/shard_map/ppermute | solution.py:173
  659.6 14.7 %collective-permute-start.1 = (f32[288,144]{1,0:T(8,128)S(1)}, f32[288,144]{1,0:T(8,128)}, u32[]{:S(2)}, u32[]{:S(2)}) collective-permute-start(f32[288,144]{1,0:T(8,128)S(1)} %get-tuple-element.302), channel_id=1, source_target_pairs={{0,20},{4,0},{8,12},{12,24},{16,4},{20,16},{24,28},{28,8},{1,21},{... | collective-permute-start | bytes 497672 | tf_op jit(solution)/shard_map/ppermute | solution.py:173
  659.7 14.6 %collective-permute-start = (f32[288,144]{1,0:T(8,128)S(1)}, f32[288,144]{1,0:T(8,128)}, u32[]{:S(2)}, u32[]{:S(2)}) collective-permute-start(f32[288,144]{1,0:T(8,128)S(1)} %get-tuple-element.300), channel_id=1, source_target_pairs={{0,0},{4,12},{8,24},{12,4},{16,16},{20,28},{24,8},{28,20},{1,1},{5... | collective-permute-start | bytes 497672 | tf_op jit(solution)/shard_map/ppermute | solution.py:173
  (51 other events, 709.4 us)
Sparse Core Ops, SparseCore 0:
  142.3 53.6 all-gather.8
  220.1 38.7 all-gather.10
  377.5 38.7 all-gather.14
  419.7 66.4 all-gather.6
  488.3 65.8 all-gather.12
  556.9 34.6 reduce-scatter.7
  593.9 32.1 reduce-scatter.9
  628.4 37.8 reduce-scatter.13
  668.6 33.4 reduce-scatter.5
  704.9 28.8 reduce-scatter.11

commit v7 on v6

--- a/solution.py
+++ b/solution.py
@@ -7,7 +7,6 @@
 
 
 HD = 72
-ATTENTION_BLOCK = 256
 
 
 norm_eps = 1e-05
@@ -60,7 +59,7 @@
 def attend_forward(query_heads, key_flat, value_flat, segment):
     length, head_cols = query_heads.shape
     head_count = head_cols // HD
-    block_rows = min(ATTENTION_BLOCK, length)
+    block_rows = min(512, length)
     block_count = length // block_rows
     key_heads = key_flat.reshape(length, head_count, HD)
     value_heads = value_flat.reshape(length, head_count, HD)
@@ -89,7 +88,7 @@
 def attend_backward(query_heads, key_flat, value_flat, segment, grad_context, log_total):
     length, head_cols = query_heads.shape
     head_count = head_cols // HD
-    block_rows = min(ATTENTION_BLOCK, length)
+    block_rows = min(512, length)
     block_count = length // block_rows
     score_scale = 1.0 / math.sqrt(HD)
     key_heads = key_flat.reshape(length, head_count, HD)
@@ -288,7 +287,7 @@
         grad_down_bias,
     )
     small_sizes = [piece.shape[0] for piece in small_grads]
-    small_total = lax.psum(jnp.concatenate(small_grads), ("seq", "batch"))
+    small_total = lax.psum(lax.psum(jnp.concatenate(small_grads), "seq"), "batch")
     summed_small = []
     offset = 0
     for size in small_sizes:

time: 753 us -> 730 us (0.969)
  matrix products: 227 us -> 195 us
  other arithmetic: 35.5 us -> 52.1 us
    dot_general x16 -> x8, matrix products: 37.4 us -> 20.7 us  [score_block(): jnp.einsum('bhd,khd->hbk', query_block, key_heads, preferred_element_type...]
    convert_element_type x8 -> x4, other arithmetic: 3.39 us -> 15.6 us  [one_block(): grad_scores = (prob_full * (grad_probs - row_delta)).astype(jnp.bfloat16)]
    while x32 -> x49, local copies, waits for them, and re-layouts: 12.5 us -> 0.55 us  [the longest x1 0.46 us: attend_backward(): lax.scan(one_block, (empty_sum, empty_sum), (query_heads.reshape(block_co...]
    dot_general x8 -> x4, matrix products: 23.4 us -> 13.4 us  [one_block(): jnp.einsum('hbk,bhd->khd', grad_scores, query_block, preferred_element_ty...]
    dot_general x8 -> x4, matrix products: 15.6 us -> 9.16 us  [one_block(): jnp.einsum('hbk,khd->bhd', probs_low, value_heads, preferred_element_type...]
    psum x1 -> x2, blocking collectives: 38.4 us -> 44 us  [the longest x1 27.2 us: block(): lax.psum(jnp.concatenate(small_grads), 'seq')]
    dot_general x8 -> x4, matrix products: 14.8 us -> 17 us  [one_block(): jnp.einsum('bhd,khd->hbk', grad_block, value_heads, preferred_element_typ...]
    dot_general x8 -> x4, matrix products: 22.6 us -> 20.6 us  [one_block(): jnp.einsum('hbk,bhd->khd', probs_low, grad_block, preferred_element_type=...]
where the time goes in v7:
time: 730 us; the launch traced here: 724 us
  waiting for transfers between devices  289 us (40%)
  matrix products  195 us (27%)
  local copies, waits for them, and re-layouts  64.9 us (9%)
  blocking collectives  63.3 us (9%)
  other arithmetic  52.1 us (7%)
  starting transfers between devices  43.4 us (6%)
  between operations  15.3 us (2%)
    all_to_all x1, waiting for transfers between devices, seq_gathered_grad(): lax.all_to_all(right, 'seq', split_axis=1, concat_axis=0, tiled=True)  61.5 us
    all_to_all x3, waiting for transfers between devices, batch_gathered_grad(): lax.all_to_all(left, 'batch', split_axis=1, concat_axis=0, tiled=True)  54.5 us
    all_to_all x1, waiting for transfers between devices, block(): lax.all_to_all(packed.reshape(local_rows, 3, seq_count, feature_count //...  41.7 us
    dot_general x5, matrix products, product(): return jnp.dot(left, right, preferred_element_type=jnp.float32)  40.7 us
    dot_general x5, matrix products, times_transposed(): lax.dot_general(left, right, (((1,), (1,)), ((), ())), preferred_element_...  37.1 us
    dot_general x5, matrix products, contract_rows(): lax.dot_general(left, right, (((0,), (0,)), ((), ())), preferred_element_...  30.8 us
    reduce_scatter x1, waiting for transfers between devices, seq_gathered_grad(): summed = lax.psum_scatter(partial, 'batch', scatter_dimension=0, tiled=True)  30 us
    psum x1, blocking collectives, block(): lax.psum(jnp.concatenate(small_grads), 'seq')  27.2 us
  transfers between devices with their start and end apart: 22, of which 12 were waited for; matrix products, arithmetic and copies ran while one was open for 31% of the time, Pallas kernels for 0%

profile of v7, /device:TPU:0, one launch (start us, length us, event | category | flops | bytes accessed | tf_op | source)
XLA Modules:
  0.0 723.8 jit_solution(4402578698723130334)
XLA Ops:
  16.0 7.3 %convolution_convert_fusion.1 = bf16[256,3456]{1,0:T(8,128)(2,1)} fusion(bf16[256,1152]{1,0:T(8,128)(2,1)S(1)} %add_convert_fusion.3, bf16[1152,3456]{1,0:T(8,128)(2,1)} %param.28), kind=kOutput, calls=%fused_computation.53 | convolution fusion | flops 2039316480 | bytes 10321920 | tf_op jit(solution)/shard_map/dot_general | solution.py:16
  30.0 6.6 all-to-all-start
  36.9 41.7 %all-to-all-done = bf16[256,3,8,144]{0,3,1,2:T(8,128)(2,1)} async-done(((bf16[256,3,8,144]{0,3,1,2:T(8,128)(2,1)}), bf16[256,3,8,144]{0,3,1,2:T(8,128)(2,1)}, u32[]{:S(2)}, u32[]{:S(2)}) %all-to-all-start) | async-done | bytes 1769504 | tf_op jit(solution)/shard_map/all_to_all | solution.py:215
  93.9 36.5 %while.27 = (s32[]{:T(128)}, bf16[4,512,144]{1,2,0:T(8,128)(2,1)}, f32[4,2,512,1]{2,1,3,0:T(2,128)S(1)}, s32[4,512]{1,0:T(4,128)S(1)}, s32[2048]{0:T(1024)S(1)},...) while((s32[]{:T(128)}, bf16[4,512,144]{1,2,0:T(8,128)(2,1)}, ...), condition=%wide.region_7.8_spmd, body=%wide.region_4.7_spmd.sunk | while | flops 628169728 | bytes 33536144 | solution.py:78
  142.1 20.8 %all-to-all-done.1 = bf16[8,256,144]{1,2,0:T(8,128)(2,1)} async-done(((bf16[8,256,144]{1,2,0:T(8,128)(2,1)}), bf16[8,256,144]{1,2,0:T(8,128)(2,1)}, u32[]{:S(2)}, u32[]{:S(2)}) %all-to-all-start.1) | async-done | bytes 589856 | tf_op jit(solution)/shard_map/all_to_all | solution.py:227
  167.7 17.2 %multiply_convert_fusion.1 = (bf16[256,4608]{1,0:T(8,128)(2,1)}, f32[256,4608]{1,0:T(8,128)}, f32[256,4608]{1,0:T(8,128)}) fusion(f32[4608]{0:T(1024)S(1)} %convert_element_type.134, bf16[256,1152]{1,0:T(8,128)(2,1)} %add_convert_fusion.2, bf16[1152,4608]{1,0:T(8,128)(2,1)} %param.33), kind=kOutput, calls=%fused_computation.57 | convolution fusion | flops 2795765760 | bytes 23021568 | tf_op jit(solution)/shard_map/dot_general | solution.py:16
  184.9 14.8 %convert_reduce_fusion = (f32[4608]{0:T(1024)}, bf16[256,4608]{1,0:T(8,128)(2,1)}) fusion(f32[256,4608]{1,0:T(8,128)} %get-tuple-element.290, f32[256,4608]{1,0:T(8,128)} %get-tuple-element.315, bf16[4608,1152]{1,0:T(8,128)(2,1)} %param.35, bf16[1,256,1152]{2,1,0:T(8,128)(2,1)S(1)} %copy-done.14), kind=kOutput, calls=%fused_computation.55 | convolution fusion | flops 2736778752 | bytes 23021568 | tf_op jit(solution)/shard_map/dot_general | solution.py:26
  199.6 8.7 %multiply_reduce_fusion.1 = (f32[1152]{0:T(1024)}, f32[256]{0:T(256)S(1)}, f32[1152]{0:T(1024)}, f32[256,1152]{1,0:T(8,128)S(1)}) fusion(f32[256,1152]{1,0:T(8,128)S(1)} %copy-done.7, f32[256]{0:T(256)S(1)} %fusion.69, f32[256]{0:T(256)S(1)} %broadcast_multiply_fusion, f32[1152]{0:T(1024)S(1)} %convert_element_type.131, ...), kind=kOutput, calls=%fused_computation.106 | convolution fusion | flops 2720265728 | bytes 15352320 | tf_op jit(solution)/shard_map/dot_general | solution.py:26
  220.8 15.9 %all-to-all-done.2 = bf16[256,8,144]{0,2,1:T(8,128)(2,1)S(1)} async-done(((bf16[256,8,144]{0,2,1:T(8,128)(2,1)}), bf16[256,8,144]{0,2,1:T(8,128)(2,1)S(1)}, u32[]{:S(2)}, u32[]{:S(2)}) %all-to-all-start.2) | async-done | bytes 589856 | tf_op jit(solution)/shard_map/all_to_all | solution.py:253
  239.1 87.2 %while.28 = (s32[]{:T(128)}, f32[2048,2,72]{0,2,1:T(8,128)S(1)}, f32[2048,2,72]{0,2,1:T(8,128)}, bf16[4,512,144]{1,2,0:T(8,128)(2,1)}, bf16[4,512,2,72]{1,3,2,0:...) while((s32[]{:T(128)}, f32[2048,2,72]{0,2,1:T(8,128)S(1)}, ...), condition=%wide.region_14.15_spmd.clone, body=%wide.region_12.14_spmd.clone.sunk | while | flops 1543781376 | bytes 136800560 | solution.py:124
  334.3 15.5 %all-to-all-done.5 = bf16[8,256,144]{1,2,0:T(8,128)(2,1)} async-done(((bf16[8,256,144]{1,2,0:T(8,128)(2,1)}), bf16[8,256,144]{1,2,0:T(8,128)(2,1)}, u32[]{:S(2)}, u32[]{:S(2)}) %all-to-all-start.5) | async-done | bytes 589856 | tf_op jit(solution)/shard_map/all_to_all | solution.py:263
  357.5 13.3 %all-to-all-done.4 = bf16[8,256,144]{1,2,0:T(8,128)(2,1)} async-done(((bf16[8,256,144]{1,2,0:T(8,128)(2,1)}), bf16[8,256,144]{1,2,0:T(8,128)(2,1)}, u32[]{:S(2)}, u32[]{:S(2)}) %all-to-all-start.4) | async-done | bytes 589856 | tf_op jit(solution)/shard_map/all_to_all | solution.py:262
  370.8 19.3 %all_to_all.180 = bf16[8,256,144]{1,2,0:T(8,128)(2,1)S(1)} all-to-all(bf16[8,256,144]{1,2,0:T(8,128)(2,1)S(1)} %copy.108), channel_id=1, replica_groups=mesh['seq'=8,'batch'=4] {'seq'}, dimensions={0} | all-to-all | bytes 1179648 | tf_op jit(solution)/shard_map/all_to_all | solution.py:261
  411.8 9.8 %all-to-all-done.7 = bf16[256,4,288]{0,2,1:T(8,128)(2,1)S(1)} async-done(((bf16[256,4,288]{0,2,1:T(8,128)(2,1)}), bf16[256,4,288]{0,2,1:T(8,128)(2,1)S(1)}, u32[]{:S(2)}, u32[]{:S(2)}) %all-to-all-start.7) | async-done | bytes 589856 | tf_op jit(solution)/shard_map/all_to_all | solution.py:148
  431.1 34.5 %all-to-all-done.9 = bf16[256,4,1152]{2,0,1:T(8,128)(2,1)S(1)} async-done(((bf16[256,4,1152]{2,0,1:T(8,128)(2,1)}), bf16[256,4,1152]{2,0,1:T(8,128)(2,1)S(1)}, u32[]{:S(2)}, u32[]{:S(2)}) %all-to-all-start.9) | async-done | bytes 2359328 | tf_op jit(solution)/shard_map/all_to_all | solution.py:148
  482.4 10.2 %all-to-all-done.6 = bf16[256,4,576]{0,2,1:T(8,128)(2,1)S(1)} async-done(((bf16[256,4,576]{0,2,1:T(8,128)(2,1)}), bf16[256,4,576]{0,2,1:T(8,128)(2,1)S(1)}, u32[]{:S(2)}, u32[]{:S(2)}) %all-to-all-start.6) | async-done | bytes 1179680 | tf_op jit(solution)/shard_map/all_to_all | solution.py:148
  506.5 61.5 %all-to-all-done.8 = bf16[256,8,576]{0,2,1:T(8,128)(2,1)S(1)} async-done(((bf16[256,8,576]{0,2,1:T(8,128)(2,1)}), bf16[256,8,576]{0,2,1:T(8,128)(2,1)S(1)}, u32[]{:S(2)}, u32[]{:S(2)}) %all-to-all-start.8) | async-done | bytes 2359328 | tf_op jit(solution)/shard_map/all_to_all | solution.py:141
  569.8 8.3 %convolution_convert_fusion.2 = bf16[1152,576]{1,0:T(8,128)(2,1)} fusion(bf16[2048,1152]{1,0:T(8,128)(2,1)} %all-gather.13.cloned.1.call-done, bf16[2048,576]{0,1:T(8,128)(2,1)} %bitcast.219), kind=kOutput, calls=%fused_computation.71 | convolution fusion | flops 2718572544 | bytes 8404992 | tf_op jit(solution)/shard_map/dot_general | solution.py:20
  578.2 8.9 %fusion.47 = bf16[1,256,1152]{2,1,0:T(8,128)(2,1)} fusion(f32[256,1152]{1,0:T(8,128)S(1)} %copy-done.8, bf16[256,4608]{1,0:T(8,128)(2,1)} %get-tuple-element.289, bf16[4608,1152]{1,0:T(8,128)(2,1)} %param.35, f32[1152]{0:T(1024)S(1)} %convert_element_type.136), kind=kOutput, calls=%fused_computation.82 | convolution fusion | flops 2718793728 | bytes 14750208 | tf_op jit(solution)/shard_map/dot_general | solution.py:16
  587.2 27.2 %psum.14 = f32[12672]{0:T(1024)S(1)} all-reduce(f32[12672]{0:T(1024)S(1)} %constant_dynamic-update-slice_fusion), channel_id=1, replica_groups=mesh['seq'=8,'batch'=4] {'seq'}, use_global_device_ids=true, to_apply=%region_26.27 | all-reduce | flops 12672 | bytes 101376 | tf_op jit(solution)/shard_map/psum | solution.py:290
  614.4 16.8 %psum.15 = f32[12672]{0:T(1024)S(1)} all-reduce(f32[12672]{0:T(1024)S(1)} %psum.14), channel_id=1, replica_groups=mesh['seq'=8,'batch'=4] {'batch'}, use_global_device_ids=true, to_apply=%region_27.28 | all-reduce | flops 12672 | bytes 101376 | tf_op jit(solution)/shard_map/psum | solution.py:290
  645.4 9.2 %collective-permute-done.2 = f32[288,144]{1,0:T(8,128)} collective-permute-done((f32[288,144]{1,0:T(8,128)}, f32[288,144]{1,0:T(8,128)}, u32[]{:S(2)}, u32[]{:S(2)}) %collective-permute-start.2) | collective-permute-done | bytes 165920 | tf_op jit(solution)/shard_map/ppermute | solution.py:172
  658.7 24.4 %reduce-scatter.6.cloned.1.call-done = bf16[576,144]{0,1:T(8,128)(2,1)} async-done(((bf16[576,1152]{0,1:T(8,128)(2,1)}), bf16[576,144]{0,1:T(8,128)(2,1)}) %reduce-scatter.6.cloned.1.call-update) | async-done | bytes 165904 | tf_op jit(solution)/shard_map/reduce_scatter | solution.py:151
  684.8 30.0 %reduce-scatter.12.cloned.1.call-done = bf16[288,576]{1,0:T(8,128)(2,1)} async-done(((bf16[1152,576]{1,0:T(8,128)(2,1)}), bf16[288,576]{1,0:T(8,128)(2,1)}) %reduce-scatter.12.cloned.1.call-update) | async-done | bytes 331792 | tf_op jit(solution)/shard_map/reduce_scatter | solution.py:143
  (329 shorter events, 286.0 us)
Async XLA Ops:
  7.2 155.8 %copy-start = (bf16[1152,1152]{1,0:T(8,128)(2,1)S(1)}, bf16[1152,1152]{1,0:T(8,128)(2,1)}, u32[]{:S(2)}) copy-start(bf16[1152,1152]{1,0:T(8,128)(2,1)} %param.29) | copy-start | bytes 7962628
  30.0 48.6 %all-to-all-start = ((bf16[256,3,8,144]{0,3,1,2:T(8,128)(2,1)}), bf16[256,3,8,144]{0,3,1,2:T(8,128)(2,1)}, u32[]{:S(2)}, u32[]{:S(2)}) async-start(bf16[256,3,8,144]{0,3,1,2:T(8,128)(2,1)} %copy.98), calls=%async_computation | async-start | bytes 3538944 | tf_op jit(solution)/shard_map/all_to_all | solution.py:215
  137.1 25.9 %all-to-all-start.1 = ((bf16[8,256,144]{1,2,0:T(8,128)(2,1)}), bf16[8,256,144]{1,2,0:T(8,128)(2,1)}, u32[]{:S(2)}, u32[]{:S(2)}) async-start(bf16[8,256,144]{1,2,0:T(8,128)(2,1)} %copy.102), calls=%async_computation.1 | async-start | bytes 1179648 | tf_op jit(solution)/shard_map/all_to_all | solution.py:227
  141.3 258.7 %all-gather.9.cloned.1.call-start = ((), (), s32[]{:S(2)}) async-start(), calls=%async_computation.17 | async-start | bytes 5308416 | tf_op jit(solution)/shard_map/all_gather | solution.py:159
  216.5 20.2 %all-to-all-start.2 = ((bf16[256,8,144]{0,2,1:T(8,128)(2,1)}), bf16[256,8,144]{0,2,1:T(8,128)(2,1)S(1)}, u32[]{:S(2)}, u32[]{:S(2)}) async-start(bf16[256,8,144]{0,2,1:T(8,128)(2,1)} %bitcast.18), calls=%async_computation.2 | async-start | bytes 1179648 | tf_op jit(solution)/shard_map/all_to_all | solution.py:253
  220.1 206.0 %all-gather.11.cloned.1.call-start = ((), (), s32[]{:S(2)}) async-start(), calls=%async_computation.19 | async-start | bytes 2949120 | tf_op jit(solution)/shard_map/all_gather | solution.py:149
  328.8 21.1 %all-to-all-start.5 = ((bf16[8,256,144]{1,2,0:T(8,128)(2,1)}), bf16[8,256,144]{1,2,0:T(8,128)(2,1)}, u32[]{:S(2)}, u32[]{:S(2)}) async-start(bf16[8,256,144]{1,2,0:T(8,128)(2,1)} %copy.110), calls=%async_computation.5 | async-start | bytes 1179648 | tf_op jit(solution)/shard_map/all_to_all | solution.py:263
  349.9 20.9 %all-to-all-start.4 = ((bf16[8,256,144]{1,2,0:T(8,128)(2,1)}), bf16[8,256,144]{1,2,0:T(8,128)(2,1)}, u32[]{:S(2)}, u32[]{:S(2)}) async-start(bf16[8,256,144]{1,2,0:T(8,128)(2,1)} %copy.109), calls=%async_computation.4 | async-start | bytes 1179648 | tf_op jit(solution)/shard_map/all_to_all | solution.py:262
  354.1 77.0 %all-gather.15.cloned.1.call-start = ((), (), s32[]{:S(2)}) async-start(), calls=%async_computation.24 | async-start | bytes 2949120 | tf_op jit(solution)/shard_map/all_gather | solution.py:149
  354.8 145.9 %all-gather.7.cloned.1.call-start = ((), (), s32[]{:S(2)}) async-start(), calls=%async_computation.15 | async-start | bytes 2949120 | tf_op jit(solution)/shard_map/all_gather | solution.py:149
  399.2 170.6 %all-gather.13.cloned.1.call-start = ((), (), s32[]{:S(2)}) async-start(), calls=%async_computation.21 | async-start | bytes 5308416 | tf_op jit(solution)/shard_map/all_gather | solution.py:140
  399.8 237.9 %reduce-scatter.8.cloned.1.call-start = ((), (), s32[]{:S(2)}) async-start(), calls=%async_computation.18 | async-start | bytes 1474560 | tf_op jit(solution)/shard_map/reduce_scatter | solution.py:161
  406.1 15.5 %all-to-all-start.7 = ((bf16[256,4,288]{0,2,1:T(8,128)(2,1)}), bf16[256,4,288]{0,2,1:T(8,128)(2,1)S(1)}, u32[]{:S(2)}, u32[]{:S(2)}) async-start(bf16[256,4,288]{0,2,1:T(8,128)(2,1)} %bitcast.33), calls=%async_computation.9 | async-start | bytes 1179648 | tf_op jit(solution)/shard_map/all_to_all | solution.py:148
  421.5 44.1 %all-to-all-start.9 = ((bf16[256,4,1152]{2,0,1:T(8,128)(2,1)}), bf16[256,4,1152]{2,0,1:T(8,128)(2,1)S(1)}, u32[]{:S(2)}, u32[]{:S(2)}) async-start(bf16[256,4,1152]{2,0,1:T(8,128)(2,1)} %bitcast.164), calls=%async_computation.13 | async-start | bytes 4718592 | tf_op jit(solution)/shard_map/all_to_all | solution.py:148
  425.2 218.7 %reduce-scatter.10.cloned.1.call-start = ((), (), s32[]{:S(2)}) async-start(), calls=%async_computation.20 | async-start | bytes 995328 | tf_op jit(solution)/shard_map/reduce_scatter | solution.py:151
  430.8 226.0 %reduce-scatter.14.cloned.1.call-start = ((), (), s32[]{:S(2)}) async-start(), calls=%async_computation.23 | async-start | bytes 2985984 | tf_op jit(solution)/shard_map/reduce_scatter | solution.py:151
  474.6 18.1 %all-to-all-start.6 = ((bf16[256,4,576]{0,2,1:T(8,128)(2,1)}), bf16[256,4,576]{0,2,1:T(8,128)(2,1)S(1)}, u32[]{:S(2)}, u32[]{:S(2)}) async-start(bf16[256,4,576]{0,2,1:T(8,128)(2,1)} %pad_maximum_fusion), calls=%async_computation.6 | async-start | bytes 2359296 | tf_op jit(solution)/shard_map/all_to_all | solution.py:148
  493.7 74.3 %all-to-all-start.8 = ((bf16[256,8,576]{0,2,1:T(8,128)(2,1)}), bf16[256,8,576]{0,2,1:T(8,128)(2,1)S(1)}, u32[]{:S(2)}, u32[]{:S(2)}) async-start(bf16[256,8,576]{0,2,1:T(8,128)(2,1)} %bitcast.35), calls=%async_computation.11 | async-start | bytes 4718592 | tf_op jit(solution)/shard_map/all_to_all | solution.py:141
  498.2 184.9 %reduce-scatter.6.cloned.1.call-start = ((), (), s32[]{:S(2)}) async-start(), calls=%async_computation.16 | async-start | bytes 1658880 | tf_op jit(solution)/shard_map/reduce_scatter | solution.py:151
  506.0 208.8 %reduce-scatter.12.cloned.1.call-start = ((), (), s32[]{:S(2)}) async-start(), calls=%async_computation.22 | async-start | bytes 1843200 | tf_op jit(solution)/shard_map/reduce_scatter | solution.py:143
  636.1 80.5 %copy-start.1 = (bf16[1152,1152]{1,0:T(8,128)(2,1)S(1)}, bf16[1152,1152]{1,0:T(8,128)(2,1)}, u32[]{:S(2)}) copy-start(bf16[1152,1152]{1,0:T(8,128)(2,1)} %param.29) | copy-start | bytes 7962628
  639.8 14.8 %collective-permute-start.2 = (f32[288,144]{1,0:T(8,128)}, f32[288,144]{1,0:T(8,128)}, u32[]{:S(2)}, u32[]{:S(2)}) collective-permute-start(f32[288,144]{1,0:T(8,128)} %get-tuple-element.301), channel_id=1, source_target_pairs={{0,8},{4,20},{8,0},{12,12},{16,24},{20,4},{24,16},{28,28},{1,9},{5... | collective-permute-start | bytes 497672 | tf_op jit(solution)/shard_map/ppermute | solution.py:172
  641.8 12.9 %collective-permute-start.1 = (f32[288,144]{1,0:T(8,128)S(1)}, f32[288,144]{1,0:T(8,128)}, u32[]{:S(2)}, u32[]{:S(2)}) collective-permute-start(f32[288,144]{1,0:T(8,128)S(1)} %get-tuple-element.302), channel_id=1, source_target_pairs={{0,20},{4,0},{8,12},{12,24},{16,4},{20,16},{24,28},{28,8},{1,21},{... | collective-permute-start | bytes 497672 | tf_op jit(solution)/shard_map/ppermute | solution.py:172
  641.8 12.8 %collective-permute-start = (f32[288,144]{1,0:T(8,128)S(1)}, f32[288,144]{1,0:T(8,128)}, u32[]{:S(2)}, u32[]{:S(2)}) collective-permute-start(f32[288,144]{1,0:T(8,128)S(1)} %get-tuple-element.300), channel_id=1, source_target_pairs={{0,0},{4,12},{8,24},{12,4},{16,16},{20,28},{24,8},{28,20},{1,1},{5... | collective-permute-start | bytes 497672 | tf_op jit(solution)/shard_map/ppermute | solution.py:172
  (62 other events, 602.1 us)
Sparse Core Ops, SparseCore 0:
  143.7 53.6 all-gather.8
  222.7 38.7 all-gather.10
  356.7 38.7 all-gather.14
  399.4 66.5 all-gather.6
  468.0 65.8 all-gather.12
  536.7 34.6 reduce-scatter.7
  573.7 32.2 reduce-scatter.9
  608.2 37.7 reduce-scatter.13
  648.4 34.6 reduce-scatter.5
  685.9 28.8 reduce-scatter.11

commit v8 on v5

--- a/solution.py
+++ b/solution.py
@@ -144,22 +144,30 @@
     return jnp.sum(swapped.astype(jnp.float32), axis=dim)
 
 
-EXCHANGE_SUM = ("hidden", "skip")
-
-
-def seq_gathered_grad(left, right, by_exchange):
+def gather_by_exchange(values, axis):
+    count = lax.axis_size(axis)
+    copies = jnp.broadcast_to(values[None], (count,) + values.shape)
+    swapped = lax.all_to_all(copies, axis, split_axis=0, concat_axis=0, tiled=True)
+    return swapped.reshape((count * values.shape[0],) + values.shape[1:])
+
+
+EXCHANGE_ONLY = ("skip",)
+
+
+def seq_gathered_grad(left, right):
     left_all = lax.all_gather(left, "seq", axis=0, tiled=True)
     right_cols = lax.all_to_all(right, "seq", split_axis=1, concat_axis=0, tiled=True)
     partial = contract_rows(left_all, right_cols).astype(jnp.bfloat16)
-    if by_exchange:
-        return scatter_sum(partial, "batch", 0)
     summed = lax.psum_scatter(partial, "batch", scatter_dimension=0, tiled=True)
     return summed.astype(jnp.float32)
 
 
-def batch_gathered_grad(left, right, by_exchange):
+def batch_gathered_grad(left, right, by_exchange=False):
     left_rows = lax.all_to_all(left, "batch", split_axis=1, concat_axis=0, tiled=True)
-    right_all = lax.all_gather(right, "batch", axis=0, tiled=True)
+    if by_exchange:
+        right_all = gather_by_exchange(right, "batch")
+    else:
+        right_all = lax.all_gather(right, "batch", axis=0, tiled=True)
     partial = contract_rows(left_rows, right_all).astype(jnp.bfloat16)
     if by_exchange:
         return scatter_sum(partial, "seq", 1)
@@ -188,13 +196,17 @@
     return jnp.concatenate(slots, axis=1)
 
 
+def padded_size(sizes):
+    return -(-sum(sizes) // 4096) * 4096
+
+
 GRAD_PLAN = {"skip": "batch", "qkv": "seq", "out": "batch", "hidden": "seq", "down": "batch"}
 
 
 def weight_grad(name, left, right):
     if GRAD_PLAN[name] == "seq":
-        return seq_gathered_grad(left, right, name in EXCHANGE_SUM)
-    return batch_gathered_grad(left, right, name in EXCHANGE_SUM)
+        return seq_gathered_grad(left, right)
+    return batch_gathered_grad(left, right, name in EXCHANGE_ONLY)
 
 
 def block(
@@ -302,7 +314,7 @@
         grad_down_bias,
     )
     small_sizes = [piece.shape[0] for piece in small_grads]
-    small_total = lax.psum(jnp.concatenate(small_grads), ("seq", "batch"))
+    small_total = lax.psum(jnp.pad(jnp.concatenate(small_grads), (0, padded_size(small_sizes) - sum(small_sizes))), ("seq", "batch"))
     summed_small = []
     offset = 0
     for size in small_sizes:

time: 696 us -> 663 us (0.953)
  blocking collectives: 95.2 us -> 0 us
  waiting for transfers between devices: 210 us -> 263 us
  starting transfers between devices: 49.2 us -> 59.6 us
    psum x1 -> x0, blocking collectives: 50.5 us -> none  [block(): small_total = lax.psum(jnp.concatenate(small_grads), ('seq', 'batch'))]
    all_to_all x2 -> x0, blocking collectives: 44.7 us -> none  [the longest x1 25.4 us: batch_gathered_grad(): lax.all_to_all(left, 'batch', split_axis=1, concat_axis=0, tiled=True)]
    all_to_all x0 -> x2, waiting for transfers between devices: none -> 38.8 us  [the longest x1 21.1 us: gather_by_exchange(): lax.all_to_all(copies, axis, split_axis=0, concat_axis=0, tiled=True)]
    all_to_all x1, waiting for transfers between devices: 13.3 us -> 31.4 us  [block(): lax.all_to_all(grad_key, 'seq', split_axis=0, concat_axis=1, tiled=True)]
    all_to_all x0 -> x2, starting transfers between devices: none -> 8.68 us  [the longest x1 4.49 us: gather_by_exchange(): lax.all_to_all(copies, axis, split_axis=0, concat_axis=0, tiled=True)]
    all_to_all x2 -> x3, waiting for transfers between devices: 25.4 us -> 21.9 us  [batch_gathered_grad(): lax.all_to_all(left, 'batch', split_axis=1, concat_axis=0, tiled=True)]
  transfers between devices with their start and end apart: 21 -> 24, of which waited for: 9 -> 11; matrix products, arithmetic and copies ran while one was open for 34% -> 28% of each run, Pallas kernels for 0% -> 0%
where the time goes in v8:
time: 663 us; the launch traced here: 656 us
  waiting for transfers between devices  263 us (40%)
  matrix products  194 us (29%)
  local copies, waits for them, and re-layouts  69.6 us (10%)
  starting transfers between devices  59.6 us (9%)
  other arithmetic  52.2 us (8%)
  between operations  16.8 us (3%)
    all_to_all x1, waiting for transfers between devices, seq_gathered_grad(): lax.all_to_all(right, 'seq', split_axis=1, concat_axis=0, tiled=True)  70.3 us
    all_to_all x1, waiting for transfers between devices, block(): lax.all_to_all(packed.reshape(local_rows, 3, seq_count, feature_count //...  41.7 us
    dot_general x5, matrix products, product(): return jnp.dot(left, right, preferred_element_type=jnp.float32)  40.3 us
    dot_general x5, matrix products, times_transposed(): lax.dot_general(left, right, (((1,), (1,)), ((), ())), preferred_element_...  35.9 us
    all_to_all x1, waiting for transfers between devices, block(): lax.all_to_all(grad_key, 'seq', split_axis=0, concat_axis=1, tiled=True)  31.4 us
    dot_general x5, matrix products, contract_rows(): lax.dot_general(left, right, (((0,), (0,)), ((), ())), preferred_element_...  30.8 us
    all_to_all x3, waiting for transfers between devices, batch_gathered_grad(): lax.all_to_all(left, 'batch', split_axis=1, concat_axis=0, tiled=True)  21.9 us
    all_to_all x1, waiting for transfers between devices, gather_by_exchange(): lax.all_to_all(copies, axis, split_axis=0, concat_axis=0, tiled=True)  21.1 us
  transfers between devices with their start and end apart: 24, of which 11 were waited for; matrix products, arithmetic and copies ran while one was open for 28% of the time, Pallas kernels for 0%

profile of v8, /device:TPU:0, one launch (start us, length us, event | category | flops | bytes accessed | tf_op | source)
XLA Modules:
  0.0 656.1 jit_solution(6048097082113639409)
XLA Ops:
  16.8 7.2 %convolution_convert_fusion.1 = bf16[256,3456]{1,0:T(8,128)(2,1)} fusion(bf16[256,1152]{1,0:T(8,128)(2,1)S(1)} %add_convert_fusion.3, bf16[1152,3456]{1,0:T(8,128)(2,1)} %param.28), kind=kOutput, calls=%fused_computation.53 | convolution fusion | flops 2039316480 | bytes 10321920 | tf_op jit(solution)/shard_map/dot_general | solution.py:16
  30.7 6.6 %all-to-all-start = ((bf16[256,3,8,144]{0,3,1,2:T(8,128)(2,1)}), bf16[256,3,8,144]{0,3,1,2:T(8,128)(2,1)}, u32[]{:S(2)}, u32[]{:S(2)}) async-start(bf16[256,3,8,144]{0,3,1,2:T(8,128)(2,1)} %copy.100), calls=%async_computation | async-start | bytes 3538944 | tf_op jit(solution)/shard_map/all_to_all | solution.py:242
  37.6 41.7 %all-to-all-done = bf16[256,3,8,144]{0,3,1,2:T(8,128)(2,1)} async-done(((bf16[256,3,8,144]{0,3,1,2:T(8,128)(2,1)}), bf16[256,3,8,144]{0,3,1,2:T(8,128)(2,1)}, u32[]{:S(2)}, u32[]{:S(2)}) %all-to-all-start) | async-done | bytes 1769504 | tf_op jit(solution)/shard_map/all_to_all | solution.py:242
  94.6 36.5 %while.27 = (s32[]{:T(128)}, bf16[4,512,144]{1,2,0:T(8,128)(2,1)}, f32[4,2,512,1]{2,1,3,0:T(2,128)S(1)}, s32[4,512]{1,0:T(4,128)S(1)}, s32[2048]{0:T(1024)S(1)},...) while((s32[]{:T(128)}, bf16[4,512,144]{1,2,0:T(8,128)(2,1)}, ...), condition=%wide.region_7.8_spmd, body=%wide.region_4.7_spmd.sunk | while | flops 628169728 | bytes 33536144 | solution.py:78
  142.5 16.2 %all-to-all-done.1 = bf16[8,256,144]{1,2,0:T(8,128)(2,1)} async-done(((bf16[8,256,144]{1,2,0:T(8,128)(2,1)}), bf16[8,256,144]{1,2,0:T(8,128)(2,1)}, u32[]{:S(2)}, u32[]{:S(2)}) %all-to-all-start.1) | async-done | bytes 589856 | tf_op jit(solution)/shard_map/all_to_all | solution.py:254
  163.4 17.1 %multiply_convert_fusion.1 = (bf16[256,4608]{1,0:T(8,128)(2,1)}, f32[256,4608]{1,0:T(8,128)}, f32[256,4608]{1,0:T(8,128)}) fusion(f32[4608]{0:T(1024)S(1)} %convert_element_type.136, bf16[256,1152]{1,0:T(8,128)(2,1)} %add_convert_fusion.2, bf16[1152,4608]{1,0:T(8,128)(2,1)} %param.33), kind=kOutput, calls=%fused_computation.57 | convolution fusion | flops 2795765760 | bytes 23021568 | tf_op jit(solution)/shard_map/dot_general | solution.py:16
  180.5 14.0 %convert_reduce_fusion = (f32[4608]{0:T(1024)S(1)}, bf16[256,4608]{1,0:T(8,128)(2,1)}) fusion(f32[256,4608]{1,0:T(8,128)} %get-tuple-element.290, f32[256,4608]{1,0:T(8,128)} %get-tuple-element.315, bf16[4608,1152]{1,0:T(8,128)(2,1)} %param.35, bf16[1,256,1152]{2,1,0:T(8,128)(2,1)S(1)} %copy-done.14), kind=kOutput, calls=%fused_computation.55 | convolution fusion | flops 2736778752 | bytes 23021568 | tf_op jit(solution)/shard_map/dot_general | solution.py:26
  194.5 8.1 %multiply_reduce_fusion.1 = (f32[1152]{0:T(1024)S(1)}, f32[256]{0:T(256)S(1)}, f32[1152]{0:T(1024)S(1)}, f32[256,1152]{1,0:T(8,128)S(1)}) fusion(f32[256,1152]{1,0:T(8,128)S(1)} %copy-done.7, f32[256]{0:T(256)S(1)} %fusion.71, f32[256]{0:T(256)S(1)} %broadcast_multiply_fusion, f32[1152]{0:T(1024)S(1)} %convert_element_type.133, ...), kind=kOutput, calls=%fused_computation.109 | convolution fusion | flops 2720265728 | bytes 15352320 | tf_op jit(solution)/shard_map/dot_general | solution.py:26
  215.9 16.1 %all-to-all-done.2 = bf16[256,8,144]{0,2,1:T(8,128)(2,1)S(1)} async-done(((bf16[256,8,144]{0,2,1:T(8,128)(2,1)}), bf16[256,8,144]{0,2,1:T(8,128)(2,1)S(1)}, u32[]{:S(2)}, u32[]{:S(2)}) %all-to-all-start.2) | async-done | bytes 589856 | tf_op jit(solution)/shard_map/all_to_all | solution.py:280
  238.7 87.8 %while.28 = (s32[]{:T(128)}, f32[2048,2,72]{0,2,1:T(8,128)S(1)}, f32[2048,2,72]{0,2,1:T(8,128)}, bf16[4,512,144]{1,2,0:T(8,128)(2,1)}, bf16[4,512,2,72]{1,3,2,0:...) while((s32[]{:T(128)}, f32[2048,2,72]{0,2,1:T(8,128)S(1)}, ...), condition=%wide.region_14.15_spmd.clone, body=%wide.region_12.14_spmd.clone.sunk | while | flops 1543781376 | bytes 136800560 | solution.py:124
  253.2 5.5 fusion.147
  297.3 5.2 fusion.147
  334.4 15.5 %all-to-all-done.5 = bf16[8,256,144]{1,2,0:T(8,128)(2,1)} async-done(((bf16[8,256,144]{1,2,0:T(8,128)(2,1)}), bf16[8,256,144]{1,2,0:T(8,128)(2,1)}, u32[]{:S(2)}, u32[]{:S(2)}) %all-to-all-start.5) | async-done | bytes 589856 | tf_op jit(solution)/shard_map/all_to_all | solution.py:290
  355.1 31.4 %all-to-all-done.4 = bf16[8,256,144]{1,2,0:T(8,128)(2,1)S(1)} async-done(((bf16[8,256,144]{1,2,0:T(8,128)(2,1)}), bf16[8,256,144]{1,2,0:T(8,128)(2,1)S(1)}, u32[]{:S(2)}, u32[]{:S(2)}) %all-to-all-start.4) | async-done | bytes 589856 | tf_op jit(solution)/shard_map/all_to_all | solution.py:289
  397.3 17.7 %all-to-all-done.3 = bf16[8,256,144]{1,2,0:T(8,128)(2,1)} async-done(((bf16[8,256,144]{1,2,0:T(8,128)(2,1)}), bf16[8,256,144]{1,2,0:T(8,128)(2,1)}, u32[]{:S(2)}, u32[]{:S(2)}) %all-to-all-start.3) | async-done | bytes 589856 | tf_op jit(solution)/shard_map/all_to_all | solution.py:288
  419.6 6.7 %multiply_reduce_fusion.2 = (f32[1152]{0:T(1024)S(1)}, f32[256]{0:T(256)S(1)}, f32[1152]{0:T(1024)S(1)}, f32[256,1152]{1,0:T(8,128)S(1)}) fusion(f32[256,1152]{1,0:T(8,128)S(1)} %copy-done.10, f32[256]{0:T(256)S(1)} %copy-done.35, f32[256]{0:T(256)S(1)} %copy-done.30, f32[1152]{0:T(1024)S(1)} %copy-done.28, bf16[1152,3456]{1,0:T(8,128)(2,1)} %param.28, ...), kind=kOutput, calls=%fused_computation.111 | convolution fusion | flops 2046096896 | bytes 12108288 | tf_op jit(solution)/shard_map/dot_general | solution.py:26
  440.6 6.2 convolution_convert_fusion.3
  446.8 21.9 %all-to-all-done.11 = bf16[256,4,1152]{2,0,1:T(8,128)(2,1)} async-done(((bf16[256,4,1152]{2,0,1:T(8,128)(2,1)}), bf16[256,4,1152]{2,0,1:T(8,128)(2,1)}, u32[]{:S(2)}, u32[]{:S(2)}) %all-to-all-start.11) | async-done | bytes 2359328 | tf_op jit(solution)/shard_map/all_to_all | solution.py:166
  474.8 7.2 %convolution_convert_fusion = bf16[1152,1152]{0,1:T(8,128)(2,1)} fusion(bf16[1024,1152]{1,0:T(8,128)(2,1)} %bitcast.40, bf16[1,1024,1152]{2,1,0:T(8,128)(2,1)} %all-gather.12.cloned.1.call-done), kind=kOutput, calls=%fused_computation.50 | convolution fusion | flops 2719236096 | bytes 7372800 | tf_op jit(solution)/shard_map/dot_general | solution.py:20
  486.1 21.1 %all-to-all-done.7 = bf16[4,256,1152]{2,1,0:T(8,128)(2,1)} async-done(((bf16[4,256,1152]{2,1,0:T(8,128)(2,1)}), bf16[4,256,1152]{2,1,0:T(8,128)(2,1)}, u32[]{:S(2)}, u32[]{:S(2)}) %all-to-all-start.7) | async-done | bytes 2359328 | tf_op jit(solution)/shard_map/all_to_all | solution.py:150
  518.6 70.3 %all-to-all-done.10 = bf16[256,8,576]{0,2,1:T(8,128)(2,1)S(1)} async-done(((bf16[256,8,576]{0,2,1:T(8,128)(2,1)}), bf16[256,8,576]{0,2,1:T(8,128)(2,1)S(1)}, u32[]{:S(2)}, u32[]{:S(2)}) %all-to-all-start.10) | async-done | bytes 2359328 | tf_op jit(solution)/shard_map/all_to_all | solution.py:159
  595.3 8.2 %convolution_convert_fusion.2 = bf16[1152,576]{1,0:T(8,128)(2,1)} fusion(bf16[2048,1152]{1,0:T(8,128)(2,1)} %all-gather.10.cloned.1.call-done, bf16[2048,576]{0,1:T(8,128)(2,1)} %bitcast.223), kind=kOutput, calls=%fused_computation.72 | convolution fusion | flops 2718572544 | bytes 8404992 | tf_op jit(solution)/shard_map/dot_general | solution.py:20
  603.5 8.8 %fusion.48 = bf16[1,256,1152]{2,1,0:T(8,128)(2,1)} fusion(f32[256,1152]{1,0:T(8,128)S(1)} %copy-done.8, bf16[256,4608]{1,0:T(8,128)(2,1)} %get-tuple-element.289, bf16[4608,1152]{1,0:T(8,128)(2,1)} %param.35, f32[1152]{0:T(1024)S(1)} %convert_element_type.138), kind=kOutput, calls=%fused_computation.84 | convolution fusion | flops 2718793728 | bytes 14750208 | tf_op jit(solution)/shard_map/dot_general | solution.py:16
  633.2 8.1 %collective-permute-done.2 = f32[288,144]{1,0:T(8,128)S(1)} collective-permute-done((f32[288,144]{1,0:T(8,128)}, f32[288,144]{1,0:T(8,128)S(1)}, u32[]{:S(2)}, u32[]{:S(2)}) %collective-permute-start.2) | collective-permute-done | bytes 165920 | tf_op jit(solution)/shard_map/ppermute | solution.py:195
  (321 shorter events, 278.0 us)
Async XLA Ops:
  30.7 48.7 %all-to-all-start = ((bf16[256,3,8,144]{0,3,1,2:T(8,128)(2,1)}), bf16[256,3,8,144]{0,3,1,2:T(8,128)(2,1)}, u32[]{:S(2)}, u32[]{:S(2)}) async-start(bf16[256,3,8,144]{0,3,1,2:T(8,128)(2,1)} %copy.100), calls=%async_computation | async-start | bytes 3538944 | tf_op jit(solution)/shard_map/all_to_all | solution.py:242
  137.7 20.9 %all-to-all-start.1 = ((bf16[8,256,144]{1,2,0:T(8,128)(2,1)}), bf16[8,256,144]{1,2,0:T(8,128)(2,1)}, u32[]{:S(2)}, u32[]{:S(2)}) async-start(bf16[8,256,144]{1,2,0:T(8,128)(2,1)} %copy.104), calls=%async_computation.1 | async-start | bytes 1179648 | tf_op jit(solution)/shard_map/all_to_all | solution.py:254
  141.9 287.8 %all-gather.8.cloned.1.call-start = ((), (), s32[]{:S(2)}) async-start(), calls=%async_computation.19 | async-start | bytes 2949120 | tf_op jit(solution)/shard_map/all_gather | solution.py:170
  205.2 235.4 %all-gather.6.cloned.1.call-start = ((), (), s32[]{:S(2)}) async-start(), calls=%async_computation.17 | async-start | bytes 5308416 | tf_op jit(solution)/shard_map/all_gather | solution.py:182
  205.9 268.9 %all-gather.12.cloned.1.call-start = ((), (), s32[]{:S(2)}) async-start(), calls=%async_computation.24 | async-start | bytes 2949120 | tf_op jit(solution)/shard_map/all_gather | solution.py:170
  211.8 20.2 %all-to-all-start.2 = ((bf16[256,8,144]{0,2,1:T(8,128)(2,1)}), bf16[256,8,144]{0,2,1:T(8,128)(2,1)S(1)}, u32[]{:S(2)}, u32[]{:S(2)}) async-start(bf16[256,8,144]{0,2,1:T(8,128)(2,1)} %bitcast.18), calls=%async_computation.2 | async-start | bytes 1179648 | tf_op jit(solution)/shard_map/all_to_all | solution.py:280
  215.3 380.0 %all-gather.10.cloned.1.call-start = ((), (), s32[]{:S(2)}) async-start(), calls=%async_computation.21 | async-start | bytes 5308416 | tf_op jit(solution)/shard_map/all_gather | solution.py:158
  232.0 96.9 %all-to-all-start.9 = ((bf16[256,4,288]{0,2,1:T(8,128)(2,1)}), bf16[256,4,288]{0,2,1:T(8,128)(2,1)}, u32[]{:S(2)}, u32[]{:S(2)}) async-start(bf16[256,4,288]{0,2,1:T(8,128)(2,1)} %bitcast.35), calls=%async_computation.10 | async-start | bytes 1179648 | tf_op jit(solution)/shard_map/all_to_all | solution.py:166
  328.9 21.1 %all-to-all-start.5 = ((bf16[8,256,144]{1,2,0:T(8,128)(2,1)}), bf16[8,256,144]{1,2,0:T(8,128)(2,1)}, u32[]{:S(2)}, u32[]{:S(2)}) async-start(bf16[8,256,144]{1,2,0:T(8,128)(2,1)} %copy.112), calls=%async_computation.5 | async-start | bytes 1179648 | tf_op jit(solution)/shard_map/all_to_all | solution.py:290
  350.0 36.5 %all-to-all-start.4 = ((bf16[8,256,144]{1,2,0:T(8,128)(2,1)}), bf16[8,256,144]{1,2,0:T(8,128)(2,1)S(1)}, u32[]{:S(2)}, u32[]{:S(2)}) async-start(bf16[8,256,144]{1,2,0:T(8,128)(2,1)} %copy.111), calls=%async_computation.4 | async-start | bytes 1179648 | tf_op jit(solution)/shard_map/all_to_all | solution.py:289
  387.3 27.7 %all-to-all-start.3 = ((bf16[8,256,144]{1,2,0:T(8,128)(2,1)}), bf16[8,256,144]{1,2,0:T(8,128)(2,1)}, u32[]{:S(2)}, u32[]{:S(2)}) async-start(bf16[8,256,144]{1,2,0:T(8,128)(2,1)} %copy.110), calls=%async_computation.3 | async-start | bytes 1179648 | tf_op jit(solution)/shard_map/all_to_all | solution.py:288
  415.0 20.8 %all-to-all-start.6 = ((bf16[256,4,576]{0,2,1:T(8,128)(2,1)}), bf16[256,4,576]{0,2,1:T(8,128)(2,1)}, u32[]{:S(2)}, u32[]{:S(2)}) async-start(bf16[256,4,576]{0,2,1:T(8,128)(2,1)} %pad_maximum_fusion), calls=%async_computation.6 | async-start | bytes 2359296 | tf_op jit(solution)/shard_map/all_to_all | solution.py:166
  419.3 198.8 %all-reduce.3.cloned.1.call-start = ((), (), s32[]{:S(2)}) async-start(), calls=%async_computation.16 | async-start | bytes 131072 | tf_op jit(solution)/shard_map/psum | solution.py:317
  429.7 191.2 %reduce-scatter.7.cloned.1.call-start = ((), (), s32[]{:S(2)}) async-start(), calls=%async_computation.20 | async-start | bytes 995328 | tf_op jit(solution)/shard_map/reduce_scatter | solution.py:174
  435.8 32.9 %all-to-all-start.11 = ((bf16[256,4,1152]{2,0,1:T(8,128)(2,1)}), bf16[256,4,1152]{2,0,1:T(8,128)(2,1)}, u32[]{:S(2)}, u32[]{:S(2)}) async-start(bf16[256,4,1152]{2,0,1:T(8,128)(2,1)} %bitcast.168), calls=%async_computation.14 | async-start | bytes 4718592 | tf_op jit(solution)/shard_map/all_to_all | solution.py:166
  440.4 182.1 %reduce-scatter.5.cloned.1.call-start = ((), (), s32[]{:S(2)}) async-start(), calls=%async_computation.18 | async-start | bytes 1474560 | tf_op jit(solution)/shard_map/reduce_scatter | solution.py:184
  470.3 36.9 %all-to-all-start.7 = ((bf16[4,256,1152]{2,1,0:T(8,128)(2,1)}), bf16[4,256,1152]{2,1,0:T(8,128)(2,1)}, u32[]{:S(2)}, u32[]{:S(2)}) async-start(bf16[4,256,1152]{2,1,0:T(8,128)(2,1)} %broadcast_in_dim.94), calls=%async_computation.7 | async-start | bytes 4718592 | tf_op jit(solution)/shard_map/all_to_all | solution.py:150
  474.8 169.7 %reduce-scatter.11.cloned.1.call-start = ((), (), s32[]{:S(2)}) async-start(), calls=%async_computation.23 | async-start | bytes 2985984 | tf_op jit(solution)/shard_map/reduce_scatter | solution.py:174
  507.2 81.7 %all-to-all-start.10 = ((bf16[256,8,576]{0,2,1:T(8,128)(2,1)}), bf16[256,8,576]{0,2,1:T(8,128)(2,1)S(1)}, u32[]{:S(2)}, u32[]{:S(2)}) async-start(bf16[256,8,576]{0,2,1:T(8,128)(2,1)} %bitcast.213), calls=%async_computation.12 | async-start | bytes 4718592 | tf_op jit(solution)/shard_map/all_to_all | solution.py:159
  588.9 41.9 %all-to-all-start.8 = ((bf16[576,8,144]{0,2,1:T(8,128)(2,1)}), bf16[576,8,144]{0,2,1:T(8,128)(2,1)}, u32[]{:S(2)}, u32[]{:S(2)}) async-start(bf16[576,8,144]{0,2,1:T(8,128)(2,1)} %bitcast.215), calls=%async_computation.8 | async-start | bytes 2949120 | tf_op jit(solution)/shard_map/all_to_all | solution.py:143
  593.2 53.1 %reduce-scatter.9.cloned.1.call-start = ((), (), s32[]{:S(2)}) async-start(), calls=%async_computation.22 | async-start | bytes 1843200 | tf_op jit(solution)/shard_map/reduce_scatter | solution.py:161
  624.8 16.4 %collective-permute-start.2 = (f32[288,144]{1,0:T(8,128)}, f32[288,144]{1,0:T(8,128)S(1)}, u32[]{:S(2)}, u32[]{:S(2)}) collective-permute-start(f32[288,144]{1,0:T(8,128)} %get-tuple-element.301), channel_id=1, source_target_pairs={{0,8},{4,20},{8,0},{12,12},{16,24},{20,4},{24,16},{28,28},{1,9},{5... | collective-permute-start | bytes 497672 | tf_op jit(solution)/shard_map/ppermute | solution.py:195
  628.6 13.8 %collective-permute-start.1 = (f32[288,144]{1,0:T(8,128)}, f32[288,144]{1,0:T(8,128)S(1)}, u32[]{:S(2)}, u32[]{:S(2)}) collective-permute-start(f32[288,144]{1,0:T(8,128)} %get-tuple-element.302), channel_id=1, source_target_pairs={{0,20},{4,0},{8,12},{12,24},{16,4},{20,16},{24,28},{28,8},{1,21},{... | collective-permute-start | bytes 497672 | tf_op jit(solution)/shard_map/ppermute | solution.py:195
  629.4 13.0 %collective-permute-start = (f32[288,144]{1,0:T(8,128)S(1)}, f32[288,144]{1,0:T(8,128)}, u32[]{:S(2)}, u32[]{:S(2)}) collective-permute-start(f32[288,144]{1,0:T(8,128)S(1)} %get-tuple-element.300), channel_id=1, source_target_pairs={{0,0},{4,12},{8,24},{12,4},{16,16},{20,28},{24,8},{28,20},{1,1},{5... | collective-permute-start | bytes 497672 | tf_op jit(solution)/shard_map/ppermute | solution.py:195
  (59 other events, 612.7 us)
Sparse Core Ops, SparseCore 0:
  205.3 41.9 all-gather.7
  249.0 50.9 all-gather.5
  301.8 36.0 all-gather.11
  340.0 75.4 all-gather.9
  434.3 31.3 reduce-scatter.6
  468.5 44.3 reduce-scatter.4
  515.2 71.6 reduce-scatter.10
  603.7 30.9 reduce-scatter.8
Sparse Core Ops, SparseCore 1:
  429.8 163.5 all-reduce.2

commit v9 on v8

--- a/solution.py
+++ b/solution.py
@@ -196,8 +196,8 @@
     return jnp.concatenate(slots, axis=1)
 
 
-def padded_size(sizes):
-    return -(-sum(sizes) // 4096) * 4096
+def back_to_tokens(values):
+    return lax.all_to_all(values, "seq", split_axis=0, concat_axis=1, tiled=True)
 
 
 GRAD_PLAN = {"skip": "batch", "qkv": "seq", "out": "batch", "hidden": "seq", "down": "batch"}
@@ -284,11 +284,7 @@
         query_heads, key_heads, value_heads, segment, grad_context_heads, log_total
     )
     grad_packed = jnp.concatenate(
-        [
-            lax.all_to_all(grad_query, "seq", split_axis=0, concat_axis=1, tiled=True),
-            lax.all_to_all(grad_key, "seq", split_axis=0, concat_axis=1, tiled=True),
-            lax.all_to_all(grad_value, "seq", split_axis=0, concat_axis=1, tiled=True),
-        ],
+        [back_to_tokens(grad_query), back_to_tokens(grad_key), back_to_tokens(grad_value)],
         axis=1,
     )
     grad_qkv_weight = qkv_grad_from_heads(
@@ -314,7 +310,7 @@
         grad_down_bias,
     )
     small_sizes = [piece.shape[0] for piece in small_grads]
-    small_total = lax.psum(jnp.pad(jnp.concatenate(small_grads), (0, padded_size(small_sizes) - sum(small_sizes))), ("seq", "batch"))
+    small_total = lax.psum(jnp.concatenate(small_grads), ("seq", "batch"))
     summed_small = []
     offset = 0
     for size in small_sizes:

time: 663 us -> 700 us (1.056)
  blocking collectives: 0 us -> 45.1 us
    psum x0 -> x1, blocking collectives: none -> 45.1 us  [block(): small_total = lax.psum(jnp.concatenate(small_grads), ('seq', 'batch'))]
  transfers between devices with their start and end apart: 24 -> 23, of which waited for: 11 -> 11; matrix products, arithmetic and copies ran while one was open for 28% -> 26% of each run, Pallas kernels for 0% -> 0%
where the time goes in v9:
time: 700 us; the launch traced here: 694 us
  waiting for transfers between devices  260 us (37%)
  matrix products  194 us (28%)
  local copies, waits for them, and re-layouts  65.6 us (9%)
  starting transfers between devices  59.9 us (9%)
  other arithmetic  53.3 us (8%)
  blocking collectives  45.1 us (6%)
  between operations  15.6 us (2%)
    all_to_all x3, waiting for transfers between devices, back_to_tokens(): lax.all_to_all(values, 'seq', split_axis=0, concat_axis=1, tiled=True)  65 us
    all_to_all x1, waiting for transfers between devices, seq_gathered_grad(): lax.all_to_all(right, 'seq', split_axis=1, concat_axis=0, tiled=True)  64.4 us
    psum x1, blocking collectives, block(): small_total = lax.psum(jnp.concatenate(small_grads), ('seq', 'batch'))  45.1 us
    all_to_all x1, waiting for transfers between devices, block(): lax.all_to_all(packed.reshape(local_rows, 3, seq_count, feature_count //...  41.7 us
    dot_general x5, matrix products, product(): return jnp.dot(left, right, preferred_element_type=jnp.float32)  40.3 us
    dot_general x5, matrix products, times_transposed(): lax.dot_general(left, right, (((1,), (1,)), ((), ())), preferred_element_...  38.2 us
    dot_general x5, matrix products, contract_rows(): lax.dot_general(left, right, (((0,), (0,)), ((), ())), preferred_element_...  28.7 us
    all_to_all x3, waiting for transfers between devices, batch_gathered_grad(): lax.all_to_all(left, 'batch', split_axis=1, concat_axis=0, tiled=True)  27 us
  transfers between devices with their start and end apart: 23, of which 11 were waited for; matrix products, arithmetic and copies ran while one was open for 26% of the time, Pallas kernels for 0%

profile of v9, /device:TPU:0, one launch (start us, length us, event | category | flops | bytes accessed | tf_op | source)
XLA Modules:
  0.0 693.9 jit_solution(18293187898331484029)
XLA Ops:
  16.0 7.2 %convolution_convert_fusion.1 = bf16[256,3456]{1,0:T(8,128)(2,1)} fusion(bf16[256,1152]{1,0:T(8,128)(2,1)S(1)} %add_convert_fusion.3, bf16[1152,3456]{1,0:T(8,128)(2,1)} %param.28), kind=kOutput, calls=%fused_computation.53 | convolution fusion | flops 2039316480 | bytes 10321920 | tf_op jit(solution)/shard_map/dot_general | solution.py:16
  29.8 6.6 all-to-all-start
  36.8 41.7 %all-to-all-done = bf16[256,3,8,144]{0,3,1,2:T(8,128)(2,1)} async-done(((bf16[256,3,8,144]{0,3,1,2:T(8,128)(2,1)}), bf16[256,3,8,144]{0,3,1,2:T(8,128)(2,1)}, u32[]{:S(2)}, u32[]{:S(2)}) %all-to-all-start) | async-done | bytes 1769504 | tf_op jit(solution)/shard_map/all_to_all | solution.py:242
  93.8 36.5 %while.27 = (s32[]{:T(128)}, bf16[4,512,144]{1,2,0:T(8,128)(2,1)}, f32[4,2,512,1]{2,1,3,0:T(2,128)S(1)}, s32[4,512]{1,0:T(4,128)S(1)}, s32[2048]{0:T(1024)S(1)},...) while((s32[]{:T(128)}, bf16[4,512,144]{1,2,0:T(8,128)(2,1)}, ...), condition=%wide.region_7.8_spmd, body=%wide.region_4.7_spmd.sunk | while | flops 628169728 | bytes 33536144 | solution.py:78
  141.7 16.2 %all-to-all-done.1 = bf16[8,256,144]{1,2,0:T(8,128)(2,1)} async-done(((bf16[8,256,144]{1,2,0:T(8,128)(2,1)}), bf16[8,256,144]{1,2,0:T(8,128)(2,1)}, u32[]{:S(2)}, u32[]{:S(2)}) %all-to-all-start.1) | async-done | bytes 589856 | tf_op jit(solution)/shard_map/all_to_all | solution.py:254
  162.6 17.1 %multiply_convert_fusion.1 = (bf16[256,4608]{1,0:T(8,128)(2,1)}, f32[256,4608]{1,0:T(8,128)}, f32[256,4608]{1,0:T(8,128)}) fusion(f32[4608]{0:T(1024)S(1)} %convert_element_type.134, bf16[256,1152]{1,0:T(8,128)(2,1)} %add_convert_fusion.2, bf16[1152,4608]{1,0:T(8,128)(2,1)} %param.33), kind=kOutput, calls=%fused_computation.57 | convolution fusion | flops 2795765760 | bytes 23021568 | tf_op jit(solution)/shard_map/dot_general | solution.py:16
  179.7 14.6 %convert_reduce_fusion = (f32[4608]{0:T(1024)}, bf16[256,4608]{1,0:T(8,128)(2,1)}) fusion(f32[256,4608]{1,0:T(8,128)} %get-tuple-element.290, f32[256,4608]{1,0:T(8,128)} %get-tuple-element.315, bf16[4608,1152]{1,0:T(8,128)(2,1)} %param.35, bf16[1,256,1152]{2,1,0:T(8,128)(2,1)S(1)} %copy-done.14), kind=kOutput, calls=%fused_computation.55 | convolution fusion | flops 2736778752 | bytes 23021568 | tf_op jit(solution)/shard_map/dot_general | solution.py:26
  194.3 8.8 %multiply_reduce_fusion.1 = (f32[1152]{0:T(1024)}, f32[256]{0:T(256)S(1)}, f32[1152]{0:T(1024)}, f32[256,1152]{1,0:T(8,128)S(1)}) fusion(f32[256,1152]{1,0:T(8,128)S(1)} %copy-done.7, f32[256]{0:T(256)S(1)} %fusion.71, f32[256]{0:T(256)S(1)} %broadcast_multiply_fusion, f32[1152]{0:T(1024)S(1)} %convert_element_type.131, ...), kind=kOutput, calls=%fused_computation.109 | convolution fusion | flops 2720265728 | bytes 15352320 | tf_op jit(solution)/shard_map/dot_general | solution.py:26
  219.3 14.0 %all-to-all-done.2 = bf16[256,8,144]{0,2,1:T(8,128)(2,1)S(1)} async-done(((bf16[256,8,144]{0,2,1:T(8,128)(2,1)}), bf16[256,8,144]{0,2,1:T(8,128)(2,1)S(1)}, u32[]{:S(2)}, u32[]{:S(2)}) %all-to-all-start.2) | async-done | bytes 589856 | tf_op jit(solution)/shard_map/all_to_all | solution.py:280
  239.6 15.5 %all-to-all-done.6 = bf16[256,4,576]{0,2,1:T(8,128)(2,1)} async-done(((bf16[256,4,576]{0,2,1:T(8,128)(2,1)}), bf16[256,4,576]{0,2,1:T(8,128)(2,1)}, u32[]{:S(2)}, u32[]{:S(2)}) %all-to-all-start.6) | async-done | bytes 1179680 | tf_op jit(solution)/shard_map/all_to_all | solution.py:166
  260.1 87.4 %while.28 = (s32[]{:T(128)}, f32[2048,2,72]{0,2,1:T(8,128)S(1)}, f32[2048,2,72]{0,2,1:T(8,128)}, bf16[4,512,144]{1,2,0:T(8,128)(2,1)}, bf16[4,512,2,72]{1,3,2,0:...) while((s32[]{:T(128)}, f32[2048,2,72]{0,2,1:T(8,128)S(1)}, ...), condition=%wide.region_14.15_spmd.clone, body=%wide.region_12.14_spmd.clone.sunk | while | flops 1543781376 | bytes 136800560 | solution.py:124
  355.9 32.0 %all-to-all-done.5 = bf16[8,256,144]{1,2,0:T(8,128)(2,1)} async-done(((bf16[8,256,144]{1,2,0:T(8,128)(2,1)}), bf16[8,256,144]{1,2,0:T(8,128)(2,1)}, u32[]{:S(2)}, u32[]{:S(2)}) %all-to-all-start.5) | async-done | bytes 589856 | tf_op jit(solution)/shard_map/all_to_all | solution.py:200
  393.6 26.0 %all-to-all-done.4 = bf16[8,256,144]{1,2,0:T(8,128)(2,1)} async-done(((bf16[8,256,144]{1,2,0:T(8,128)(2,1)}), bf16[8,256,144]{1,2,0:T(8,128)(2,1)}, u32[]{:S(2)}, u32[]{:S(2)}) %all-to-all-start.4) | async-done | bytes 589856 | tf_op jit(solution)/shard_map/all_to_all | solution.py:200
  433.6 7.0 %all-to-all-done.3 = bf16[8,256,144]{1,2,0:T(8,128)(2,1)} async-done(((bf16[8,256,144]{1,2,0:T(8,128)(2,1)}), bf16[8,256,144]{1,2,0:T(8,128)(2,1)}, u32[]{:S(2)}, u32[]{:S(2)}) %all-to-all-start.3) | async-done | bytes 589856 | tf_op jit(solution)/shard_map/all_to_all | solution.py:200
  445.2 7.7 %multiply_reduce_fusion.2 = (f32[1152]{0:T(1024)S(1)}, f32[256]{0:T(256)S(1)}, f32[1152]{0:T(1024)S(1)}, f32[256,1152]{1,0:T(8,128)}) fusion(f32[256,1152]{1,0:T(8,128)S(1)} %copy-done.10, f32[256]{0:T(256)S(1)} %copy-done.34, f32[256]{0:T(256)S(1)} %copy-done.29, f32[1152]{0:T(1024)S(1)} %copy-done.25, bf16[1152,3456]{1,0:T(8,128)(2,1)} %param.28, ...), kind=kOutput, calls=%fused_computation.111 | convolution fusion | flops 2046096896 | bytes 12108288 | tf_op jit(solution)/shard_map/dot_general | solution.py:26
  452.9 6.1 convolution_convert_fusion.3
  461.3 11.5 %all-to-all-done.11 = bf16[256,4,1152]{2,0,1:T(8,128)(2,1)} async-done(((bf16[256,4,1152]{2,0,1:T(8,128)(2,1)}), bf16[256,4,1152]{2,0,1:T(8,128)(2,1)}, u32[]{:S(2)}, u32[]{:S(2)}) %all-to-all-start.11) | async-done | bytes 2359328 | tf_op jit(solution)/shard_map/all_to_all | solution.py:166
  479.2 7.4 %convolution_convert_fusion = bf16[1152,1152]{0,1:T(8,128)(2,1)} fusion(bf16[1024,1152]{1,0:T(8,128)(2,1)} %bitcast.40, bf16[1,1024,1152]{2,1,0:T(8,128)(2,1)} %all-gather.12.cloned.1.call-done), kind=kOutput, calls=%fused_computation.50 | convolution fusion | flops 2719236096 | bytes 7372800 | tf_op jit(solution)/shard_map/dot_general | solution.py:20
  490.7 19.8 %all-to-all-done.7 = bf16[4,256,1152]{2,1,0:T(8,128)(2,1)} async-done(((bf16[4,256,1152]{2,1,0:T(8,128)(2,1)}), bf16[4,256,1152]{2,1,0:T(8,128)(2,1)}, u32[]{:S(2)}, u32[]{:S(2)}) %all-to-all-start.7) | async-done | bytes 2359328 | tf_op jit(solution)/shard_map/all_to_all | solution.py:150
  515.1 8.8 %fusion.48 = bf16[1,256,1152]{2,1,0:T(8,128)(2,1)} fusion(f32[256,1152]{1,0:T(8,128)S(1)} %copy-done.8, bf16[256,4608]{1,0:T(8,128)(2,1)} %get-tuple-element.289, bf16[4608,1152]{1,0:T(8,128)(2,1)} %param.35, f32[1152]{0:T(1024)S(1)} %convert_element_type.136), kind=kOutput, calls=%fused_computation.84 | convolution fusion | flops 2718793728 | bytes 14750208 | tf_op jit(solution)/shard_map/dot_general | solution.py:16
  529.3 64.4 %all-to-all-done.10 = bf16[256,8,576]{0,2,1:T(8,128)(2,1)} async-done(((bf16[256,8,576]{0,2,1:T(8,128)(2,1)}), bf16[256,8,576]{0,2,1:T(8,128)(2,1)}, u32[]{:S(2)}, u32[]{:S(2)}) %all-to-all-start.10) | async-done | bytes 2359328 | tf_op jit(solution)/shard_map/all_to_all | solution.py:159
  600.4 7.4 %convolution_convert_fusion.2 = bf16[1152,576]{1,0:T(8,128)(2,1)} fusion(bf16[2048,1152]{1,0:T(8,128)(2,1)} %all-gather.10.cloned.1.call-done, bf16[2048,576]{0,1:T(8,128)(2,1)S(1)} %bitcast.222), kind=kOutput, calls=%fused_computation.72 | convolution fusion | flops 2718572544 | bytes 8404992 | tf_op jit(solution)/shard_map/dot_general | solution.py:20
  608.0 45.1 %psum.7 = f32[12672]{0:T(1024)S(1)} all-reduce(f32[12672]{0:T(1024)S(1)} %constant_dynamic-update-slice_fusion), channel_id=1, replica_groups=mesh['seq'=8,'batch'=4] {'seq','batch'}, use_global_device_ids=true, to_apply=%region_26.27 | all-reduce | flops 12672 | bytes 101376 | tf_op jit(solution)/shard_map/psum | solution.py:313
  671.0 9.8 %collective-permute-done.2 = f32[288,144]{1,0:T(8,128)S(1)} collective-permute-done((f32[288,144]{1,0:T(8,128)}, f32[288,144]{1,0:T(8,128)S(1)}, u32[]{:S(2)}, u32[]{:S(2)}) %collective-permute-start.2) | collective-permute-done | bytes 165920 | tf_op jit(solution)/shard_map/ppermute | solution.py:195
  (320 shorter events, 283.2 us)
Async XLA Ops:
  7.2 150.7 %copy-start = (bf16[1152,1152]{1,0:T(8,128)(2,1)S(1)}, bf16[1152,1152]{1,0:T(8,128)(2,1)}, u32[]{:S(2)}) copy-start(bf16[1152,1152]{1,0:T(8,128)(2,1)} %param.29) | copy-start | bytes 7962628
  29.8 48.7 %all-to-all-start = ((bf16[256,3,8,144]{0,3,1,2:T(8,128)(2,1)}), bf16[256,3,8,144]{0,3,1,2:T(8,128)(2,1)}, u32[]{:S(2)}, u32[]{:S(2)}) async-start(bf16[256,3,8,144]{0,3,1,2:T(8,128)(2,1)} %copy.100), calls=%async_computation | async-start | bytes 3538944 | tf_op jit(solution)/shard_map/all_to_all | solution.py:242
  136.9 20.9 %all-to-all-start.1 = ((bf16[8,256,144]{1,2,0:T(8,128)(2,1)}), bf16[8,256,144]{1,2,0:T(8,128)(2,1)}, u32[]{:S(2)}, u32[]{:S(2)}) async-start(bf16[8,256,144]{1,2,0:T(8,128)(2,1)} %copy.104), calls=%async_computation.1 | async-start | bytes 1179648 | tf_op jit(solution)/shard_map/all_to_all | solution.py:254
  141.1 288.2 %all-gather.8.cloned.1.call-start = ((), (), s32[]{:S(2)}) async-start(), calls=%async_computation.18 | async-start | bytes 2949120 | tf_op jit(solution)/shard_map/all_gather | solution.py:170
  206.2 246.7 %all-gather.6.cloned.1.call-start = ((), (), s32[]{:S(2)}) async-start(), calls=%async_computation.16 | async-start | bytes 5308416 | tf_op jit(solution)/shard_map/all_gather | solution.py:182
  207.0 272.2 %all-gather.12.cloned.1.call-start = ((), (), s32[]{:S(2)}) async-start(), calls=%async_computation.23 | async-start | bytes 2949120 | tf_op jit(solution)/shard_map/all_gather | solution.py:170
  212.9 20.4 %all-to-all-start.2 = ((bf16[256,8,144]{0,2,1:T(8,128)(2,1)}), bf16[256,8,144]{0,2,1:T(8,128)(2,1)S(1)}, u32[]{:S(2)}, u32[]{:S(2)}) async-start(bf16[256,8,144]{0,2,1:T(8,128)(2,1)} %bitcast.18), calls=%async_computation.2 | async-start | bytes 1179648 | tf_op jit(solution)/shard_map/all_to_all | solution.py:280
  233.2 21.9 %all-to-all-start.6 = ((bf16[256,4,576]{0,2,1:T(8,128)(2,1)}), bf16[256,4,576]{0,2,1:T(8,128)(2,1)}, u32[]{:S(2)}, u32[]{:S(2)}) async-start(bf16[256,4,576]{0,2,1:T(8,128)(2,1)} %pad_maximum_fusion), calls=%async_computation.6 | async-start | bytes 2359296 | tf_op jit(solution)/shard_map/all_to_all | solution.py:166
  237.5 362.8 %all-gather.10.cloned.1.call-start = ((), (), s32[]{:S(2)}) async-start(), calls=%async_computation.20 | async-start | bytes 5308416 | tf_op jit(solution)/shard_map/all_gather | solution.py:158
  255.1 94.9 %all-to-all-start.9 = ((bf16[256,4,288]{0,2,1:T(8,128)(2,1)}), bf16[256,4,288]{0,2,1:T(8,128)(2,1)}, u32[]{:S(2)}, u32[]{:S(2)}) async-start(bf16[256,4,288]{0,2,1:T(8,128)(2,1)} %bitcast.35), calls=%async_computation.10 | async-start | bytes 1179648 | tf_op jit(solution)/shard_map/all_to_all | solution.py:166
  349.9 37.9 %all-to-all-start.5 = ((bf16[8,256,144]{1,2,0:T(8,128)(2,1)}), bf16[8,256,144]{1,2,0:T(8,128)(2,1)}, u32[]{:S(2)}, u32[]{:S(2)}) async-start(bf16[8,256,144]{1,2,0:T(8,128)(2,1)} %copy.112), calls=%async_computation.5 | async-start | bytes 1179648 | tf_op jit(solution)/shard_map/all_to_all | solution.py:200
  387.9 31.8 %all-to-all-start.4 = ((bf16[8,256,144]{1,2,0:T(8,128)(2,1)}), bf16[8,256,144]{1,2,0:T(8,128)(2,1)}, u32[]{:S(2)}, u32[]{:S(2)}) async-start(bf16[8,256,144]{1,2,0:T(8,128)(2,1)} %copy.111), calls=%async_computation.4 | async-start | bytes 1179648 | tf_op jit(solution)/shard_map/all_to_all | solution.py:200
  419.6 20.9 %all-to-all-start.3 = ((bf16[8,256,144]{1,2,0:T(8,128)(2,1)}), bf16[8,256,144]{1,2,0:T(8,128)(2,1)}, u32[]{:S(2)}, u32[]{:S(2)}) async-start(bf16[8,256,144]{1,2,0:T(8,128)(2,1)} %copy.110), calls=%async_computation.3 | async-start | bytes 1179648 | tf_op jit(solution)/shard_map/all_to_all | solution.py:200
  423.8 236.3 %reduce-scatter.7.cloned.1.call-start = ((), (), s32[]{:S(2)}) async-start(), calls=%async_computation.19 | async-start | bytes 995328 | tf_op jit(solution)/shard_map/reduce_scatter | solution.py:174
  440.6 32.2 %all-to-all-start.11 = ((bf16[256,4,1152]{2,0,1:T(8,128)(2,1)}), bf16[256,4,1152]{2,0,1:T(8,128)(2,1)}, u32[]{:S(2)}, u32[]{:S(2)}) async-start(bf16[256,4,1152]{2,0,1:T(8,128)(2,1)} %bitcast.213), calls=%async_computation.14 | async-start | bytes 4718592 | tf_op jit(solution)/shard_map/all_to_all | solution.py:166
  445.1 216.7 %reduce-scatter.5.cloned.1.call-start = ((), (), s32[]{:S(2)}) async-start(), calls=%async_computation.17 | async-start | bytes 1474560 | tf_op jit(solution)/shard_map/reduce_scatter | solution.py:184
  474.4 36.2 %all-to-all-start.7 = ((bf16[4,256,1152]{2,1,0:T(8,128)(2,1)}), bf16[4,256,1152]{2,1,0:T(8,128)(2,1)}, u32[]{:S(2)}, u32[]{:S(2)}) async-start(bf16[4,256,1152]{2,1,0:T(8,128)(2,1)} %broadcast_in_dim.94), calls=%async_computation.7 | async-start | bytes 4718592 | tf_op jit(solution)/shard_map/all_to_all | solution.py:150
  478.9 203.9 %reduce-scatter.11.cloned.1.call-start = ((), (), s32[]{:S(2)}) async-start(), calls=%async_computation.22 | async-start | bytes 2985984 | tf_op jit(solution)/shard_map/reduce_scatter | solution.py:174
  510.6 83.1 %all-to-all-start.10 = ((bf16[256,8,576]{0,2,1:T(8,128)(2,1)}), bf16[256,8,576]{0,2,1:T(8,128)(2,1)}, u32[]{:S(2)}, u32[]{:S(2)}) async-start(bf16[256,8,576]{0,2,1:T(8,128)(2,1)} %bitcast.212), calls=%async_computation.12 | async-start | bytes 4718592 | tf_op jit(solution)/shard_map/all_to_all | solution.py:159
  593.7 75.0 %all-to-all-start.8 = ((bf16[576,8,144]{0,2,1:T(8,128)(2,1)}), bf16[576,8,144]{0,2,1:T(8,128)(2,1)}, u32[]{:S(2)}, u32[]{:S(2)}) async-start(bf16[576,8,144]{0,2,1:T(8,128)(2,1)} %bitcast.32), calls=%async_computation.8 | async-start | bytes 2949120 | tf_op jit(solution)/shard_map/all_to_all | solution.py:143
  598.0 86.7 %reduce-scatter.9.cloned.1.call-start = ((), (), s32[]{:S(2)}) async-start(), calls=%async_computation.21 | async-start | bytes 1843200 | tf_op jit(solution)/shard_map/reduce_scatter | solution.py:161
  664.0 16.7 %collective-permute-start.2 = (f32[288,144]{1,0:T(8,128)}, f32[288,144]{1,0:T(8,128)S(1)}, u32[]{:S(2)}, u32[]{:S(2)}) collective-permute-start(f32[288,144]{1,0:T(8,128)} %get-tuple-element.301), channel_id=1, source_target_pairs={{0,8},{4,20},{8,0},{12,12},{16,24},{20,4},{24,16},{28,28},{1,9},{5... | collective-permute-start | bytes 497672 | tf_op jit(solution)/shard_map/ppermute | solution.py:195
  665.9 14.8 %collective-permute-start.1 = (f32[288,144]{1,0:T(8,128)}, f32[288,144]{1,0:T(8,128)S(1)}, u32[]{:S(2)}, u32[]{:S(2)}) collective-permute-start(f32[288,144]{1,0:T(8,128)} %get-tuple-element.302), channel_id=1, source_target_pairs={{0,20},{4,0},{8,12},{12,24},{16,4},{20,16},{24,28},{28,8},{1,21},{... | collective-permute-start | bytes 497672 | tf_op jit(solution)/shard_map/ppermute | solution.py:195
  667.3 13.5 %collective-permute-start = (f32[288,144]{1,0:T(8,128)S(1)}, f32[288,144]{1,0:T(8,128)}, u32[]{:S(2)}, u32[]{:S(2)}) collective-permute-start(f32[288,144]{1,0:T(8,128)S(1)} %get-tuple-element.300), channel_id=1, source_target_pairs={{0,0},{4,12},{8,24},{12,4},{16,16},{20,28},{24,8},{28,20},{1,1},{5... | collective-permute-start | bytes 497672 | tf_op jit(solution)/shard_map/ppermute | solution.py:195
  (59 other events, 476.8 us)
Sparse Core Ops, SparseCore 0:
  206.3 44.8 all-gather.7
  252.9 52.3 all-gather.5
  307.2 36.0 all-gather.11
  345.4 76.4 all-gather.9
  433.7 33.5 reduce-scatter.6
  470.0 43.0 reduce-scatter.4
  515.4 72.4 reduce-scatter.10
  607.9 30.9 reduce-scatter.8

commit v10 on v8

--- a/solution.py
+++ b/solution.py
@@ -162,8 +162,26 @@
     return summed.astype(jnp.float32)
 
 
-def batch_gathered_grad(left, right, by_exchange=False):
-    left_rows = lax.all_to_all(left, "batch", split_axis=1, concat_axis=0, tiled=True)
+def split_rows_together(lefts):
+    count = lax.axis_size("batch")
+    rows = lefts[0].shape[0]
+    widths = [left.shape[1] // count for left in lefts]
+    joined = jnp.concatenate(
+        [left.reshape(rows, count, width) for left, width in zip(lefts, widths)], axis=2
+    )
+    moved = lax.all_to_all(joined, "batch", split_axis=1, concat_axis=0, tiled=True)
+    moved = moved.reshape(count * rows, sum(widths))
+    pieces = []
+    offset = 0
+    for width in widths:
+        pieces.append(moved[:, offset : offset + width])
+        offset += width
+    return pieces
+
+
+def batch_gathered_grad(left, right, by_exchange=False, left_rows=None):
+    if left_rows is None:
+        left_rows = lax.all_to_all(left, "batch", split_axis=1, concat_axis=0, tiled=True)
     if by_exchange:
         right_all = gather_by_exchange(right, "batch")
     else:
@@ -196,14 +214,12 @@
     return jnp.concatenate(slots, axis=1)
 
 
-def padded_size(sizes):
-    return -(-sum(sizes) // 4096) * 4096
-
-
 GRAD_PLAN = {"skip": "batch", "qkv": "seq", "out": "batch", "hidden": "seq", "down": "batch"}
 
 
-def weight_grad(name, left, right):
+def weight_grad(name, left, right, left_rows=None):
+    if left_rows is not None:
+        return batch_gathered_grad(left, right, name in EXCHANGE_ONLY, left_rows)
     if GRAD_PLAN[name] == "seq":
         return seq_gathered_grad(left, right)
     return batch_gathered_grad(left, right, name in EXCHANGE_ONLY)
@@ -264,7 +280,8 @@
         jnp.bfloat16
     )
     grad_out_rows = cotangent[0]
-    grad_down_weight = weight_grad("down", hidden_act, grad_out_rows)
+    hidden_rows, context_rows = split_rows_together((hidden_act, context_tok))
+    grad_down_weight = weight_grad("down", hidden_act, grad_out_rows, hidden_rows)
     grad_down_bias = column_sums(grad_out_rows)
     grad_act = times_transposed(grad_out_rows, down_weight)
     grad_pre = gelu_pull(grad_act)[0].astype(jnp.bfloat16)
@@ -275,7 +292,7 @@
     grad_middle = grad_out_rows.astype(jnp.float32) + grad_middle_norm
     grad_attended = grad_middle.astype(jnp.bfloat16)
     grad_out_bias = column_sums(grad_attended)
-    grad_out_weight = weight_grad("out", context_tok, grad_attended)
+    grad_out_weight = weight_grad("out", context_tok, grad_attended, context_rows)
     grad_context = times_transposed(grad_attended, out_weight).astype(jnp.bfloat16)
     grad_context_heads = lax.all_to_all(
         grad_context, "seq", split_axis=1, concat_axis=0, tiled=True
@@ -314,7 +331,7 @@
         grad_down_bias,
     )
     small_sizes = [piece.shape[0] for piece in small_grads]
-    small_total = lax.psum(jnp.pad(jnp.concatenate(small_grads), (0, padded_size(small_sizes) - sum(small_sizes))), ("seq", "batch"))
+    small_total = lax.psum(jnp.concatenate(small_grads), ("seq", "batch"))
     summed_small = []
     offset = 0
     for size in small_sizes:

time: 663 us -> 699 us (1.054)
  blocking collectives: 0 us -> 45.4 us
  waiting for transfers between devices: 263 us -> 246 us
  local copies, waits for them, and re-layouts: 69.6 us -> 77 us
    psum x0 -> x1, blocking collectives: none -> 45.4 us  [block(): small_total = lax.psum(jnp.concatenate(small_grads), ('seq', 'batch'))]
    all_to_all x0 -> x1, waiting for transfers between devices: none -> 32.7 us  [split_rows_together(): lax.all_to_all(joined, 'batch', split_axis=1, concat_axis=0, tiled=True)]
    all_to_all x3 -> x1, waiting for transfers between devices: 21.9 us -> 0.01 us  [batch_gathered_grad(): lax.all_to_all(left, 'batch', split_axis=1, concat_axis=0, tiled=True)]
    all_to_all x1, waiting for transfers between devices: 17.7 us -> 0.01 us  [block(): lax.all_to_all(grad_query, 'seq', split_axis=0, concat_axis=1, tiled=True)]
    all_to_all x3 -> x1, starting transfers between devices: 13.2 us -> 4.43 us  [batch_gathered_grad(): lax.all_to_all(left, 'batch', split_axis=1, concat_axis=0, tiled=True)]
    all_to_all x2 -> x1, local copies, waits for them, and re-layouts: 3.55 us -> 12.3 us  [split_rows_together(): lax.all_to_all(joined, 'batch', split_axis=1, concat_axis=0, tiled=True)]
    all_to_all x1, waiting for transfers between devices: 70.3 us -> 61.7 us  [seq_gathered_grad(): lax.all_to_all(right, 'seq', split_axis=1, concat_axis=0, tiled=True)]
  transfers between devices with their start and end apart: 24 -> 22, of which waited for: 11 -> 9; matrix products, arithmetic and copies ran while one was open for 28% -> 28% of each run, Pallas kernels for 0% -> 0%
where the time goes in v10:
time: 699 us; the launch traced here: 692 us
  waiting for transfers between devices  246 us (35%)
  matrix products  195 us (28%)
  local copies, waits for them, and re-layouts  77 us (11%)
  other arithmetic  56.2 us (8%)
  starting transfers between devices  56.2 us (8%)
  blocking collectives  45.4 us (6%)
  between operations  15.3 us (2%)
    all_to_all x1, waiting for transfers between devices, seq_gathered_grad(): lax.all_to_all(right, 'seq', split_axis=1, concat_axis=0, tiled=True)  61.7 us
    psum x1, blocking collectives, block(): small_total = lax.psum(jnp.concatenate(small_grads), ('seq', 'batch'))  45.4 us
    all_to_all x1, waiting for transfers between devices, block(): lax.all_to_all(packed.reshape(local_rows, 3, seq_count, feature_count //...  41.7 us
    dot_general x5, matrix products, product(): return jnp.dot(left, right, preferred_element_type=jnp.float32)  40.6 us
    dot_general x5, matrix products, times_transposed(): lax.dot_general(left, right, (((1,), (1,)), ((), ())), preferred_element_...  38.2 us
    all_to_all x1, waiting for transfers between devices, split_rows_together(): lax.all_to_all(joined, 'batch', split_axis=1, concat_axis=0, tiled=True)  32.7 us
    dot_general x5, matrix products, contract_rows(): lax.dot_general(left, right, (((0,), (0,)), ((), ())), preferred_element_...  28.7 us
    all_to_all x1, waiting for transfers between devices, block(): lax.all_to_all(grad_key, 'seq', split_axis=0, concat_axis=1, tiled=True)  27.3 us
  transfers between devices with their start and end apart: 22, of which 9 were waited for; matrix products, arithmetic and copies ran while one was open for 28% of the time, Pallas kernels for 0%

profile of v10, /device:TPU:0, one launch (start us, length us, event | category | flops | bytes accessed | tf_op | source)
XLA Modules:
  0.0 692.3 jit_solution(17591589361882013513)
XLA Ops:
  16.0 7.2 %convolution_convert_fusion.1 = bf16[256,3456]{1,0:T(8,128)(2,1)} fusion(bf16[256,1152]{1,0:T(8,128)(2,1)S(1)} %add_convert_fusion.3, bf16[1152,3456]{1,0:T(8,128)(2,1)} %param.28), kind=kOutput, calls=%fused_computation.53 | convolution fusion | flops 2039316480 | bytes 10321920 | tf_op jit(solution)/shard_map/dot_general | solution.py:16
  29.8 6.9 all-to-all-start
  37.0 41.7 %all-to-all-done = bf16[256,3,8,144]{0,3,1,2:T(8,128)(2,1)} async-done(((bf16[256,3,8,144]{0,3,1,2:T(8,128)(2,1)}), bf16[256,3,8,144]{0,3,1,2:T(8,128)(2,1)}, u32[]{:S(2)}, u32[]{:S(2)}) %all-to-all-start) | async-done | bytes 1769504 | tf_op jit(solution)/shard_map/all_to_all | solution.py:258
  94.0 36.5 %while.27 = (s32[]{:T(128)}, bf16[4,512,144]{1,2,0:T(8,128)(2,1)}, f32[4,2,512,1]{2,1,3,0:T(2,128)S(1)}, s32[4,512]{1,0:T(4,128)S(1)}, s32[2048]{0:T(1024)S(1)},...) while((s32[]{:T(128)}, bf16[4,512,144]{1,2,0:T(8,128)(2,1)}, ...), condition=%wide.region_7.8_spmd, body=%wide.region_4.7_spmd.sunk | while | flops 628169728 | bytes 33536144 | solution.py:78
  141.7 16.4 %all-to-all-done.1 = bf16[8,256,144]{1,2,0:T(8,128)(2,1)} async-done(((bf16[8,256,144]{1,2,0:T(8,128)(2,1)}), bf16[8,256,144]{1,2,0:T(8,128)(2,1)}, u32[]{:S(2)}, u32[]{:S(2)}) %all-to-all-start.1) | async-done | bytes 589856 | tf_op jit(solution)/shard_map/all_to_all | solution.py:270
  162.8 17.2 %multiply_convert_fusion.1 = (bf16[256,4608]{1,0:T(8,128)(2,1)}, f32[256,4608]{1,0:T(8,128)}, f32[256,4608]{1,0:T(8,128)}) fusion(f32[4608]{0:T(1024)S(1)} %convert_element_type.134, bf16[256,1152]{1,0:T(8,128)(2,1)} %add_convert_fusion.2, bf16[1152,4608]{1,0:T(8,128)(2,1)} %param.33), kind=kOutput, calls=%fused_computation.57 | convolution fusion | flops 2795765760 | bytes 23021568 | tf_op jit(solution)/shard_map/dot_general | solution.py:16
  180.0 14.6 %convert_reduce_fusion = (f32[4608]{0:T(1024)}, bf16[256,4608]{1,0:T(8,128)(2,1)}) fusion(f32[256,4608]{1,0:T(8,128)} %get-tuple-element.290, f32[256,4608]{1,0:T(8,128)} %get-tuple-element.315, bf16[4608,1152]{1,0:T(8,128)(2,1)} %param.35, bf16[1,256,1152]{2,1,0:T(8,128)(2,1)S(1)} %copy-done.14), kind=kOutput, calls=%fused_computation.55 | convolution fusion | flops 2736778752 | bytes 23021568 | tf_op jit(solution)/shard_map/dot_general | solution.py:26
  194.6 8.8 %multiply_reduce_fusion.1 = (f32[1152]{0:T(1024)}, f32[256]{0:T(256)S(1)}, f32[1152]{0:T(1024)}, f32[256,1152]{1,0:T(8,128)S(1)}) fusion(f32[256,1152]{1,0:T(8,128)S(1)} %copy-done.7, f32[256]{0:T(256)S(1)} %fusion.73, f32[256]{0:T(256)S(1)} %broadcast_multiply_fusion, f32[1152]{0:T(1024)S(1)} %convert_element_type.131, ...), kind=kOutput, calls=%fused_computation.110 | convolution fusion | flops 2720265728 | bytes 15352320 | tf_op jit(solution)/shard_map/dot_general | solution.py:26
  217.2 16.1 %all-to-all-done.2 = bf16[256,8,144]{0,2,1:T(8,128)(2,1)S(1)} async-done(((bf16[256,8,144]{0,2,1:T(8,128)(2,1)}), bf16[256,8,144]{0,2,1:T(8,128)(2,1)S(1)}, u32[]{:S(2)}, u32[]{:S(2)}) %all-to-all-start.2) | async-done | bytes 589856 | tf_op jit(solution)/shard_map/all_to_all | solution.py:297
  235.7 88.6 %while.28 = (s32[]{:T(128)}, f32[2048,2,72]{0,2,1:T(8,128)S(1)}, f32[2048,2,72]{0,2,1:T(8,128)}, bf16[4,512,144]{1,2,0:T(8,128)(2,1)}, bf16[4,512,2,72]{1,3,2,0:...) while((s32[]{:T(128)}, f32[2048,2,72]{0,2,1:T(8,128)S(1)}, ...), condition=%wide.region_14.15_spmd.clone, body=%wide.region_12.14_spmd.clone.sunk | while | flops 1543781376 | bytes 136800560 | solution.py:124
  250.2 5.8 fusion.147
  332.0 15.7 %all-to-all-done.5 = bf16[8,256,144]{1,2,0:T(8,128)(2,1)} async-done(((bf16[8,256,144]{1,2,0:T(8,128)(2,1)}), bf16[8,256,144]{1,2,0:T(8,128)(2,1)}, u32[]{:S(2)}, u32[]{:S(2)}) %all-to-all-start.5) | async-done | bytes 589856 | tf_op jit(solution)/shard_map/all_to_all | solution.py:307
  357.7 27.3 %all-to-all-done.4 = bf16[8,256,144]{1,2,0:T(8,128)(2,1)} async-done(((bf16[8,256,144]{1,2,0:T(8,128)(2,1)}), bf16[8,256,144]{1,2,0:T(8,128)(2,1)}, u32[]{:S(2)}, u32[]{:S(2)}) %all-to-all-start.4) | async-done | bytes 589856 | tf_op jit(solution)/shard_map/all_to_all | solution.py:306
  391.3 32.7 %all-to-all-done.9 = bf16[256,4,1440]{0,2,1:T(8,128)(2,1)} async-done(((bf16[256,4,1440]{0,2,1:T(8,128)(2,1)}), bf16[256,4,1440]{0,2,1:T(8,128)(2,1)}, u32[]{:S(2)}, u32[]{:S(2)}) %all-to-all-start.9) | async-done | bytes 2949152 | tf_op jit(solution)/shard_map/all_to_all | solution.py:172
  431.4 12.3 %copy.118 = bf16[4,256,1,1440]{1,0,3,2:T(4,128)(2,1)S(1)} copy(bf16[4,256,1,1440]{1,3,0,2:T(8,128)(2,1)} %bitcast.38) | data formatting | bytes 5898240 | tf_op jit(solution)/shard_map/all_to_all | solution.py:172
  455.0 7.7 %multiply_reduce_fusion.2 = (f32[1152]{0:T(1024)S(1)}, f32[256]{0:T(256)S(1)}, f32[1152]{0:T(1024)S(1)}, f32[256,1152]{1,0:T(8,128)}) fusion(f32[256,1152]{1,0:T(8,128)S(1)} %copy-done.10, f32[256]{0:T(256)S(1)} %copy-done.35, f32[256]{0:T(256)S(1)} %copy-done.30, f32[1152]{0:T(1024)S(1)} %copy-done.26, bf16[1152,3456]{1,0:T(8,128)(2,1)} %param.28, ...), kind=kOutput, calls=%fused_computation.112 | convolution fusion | flops 2046096896 | bytes 12108288 | tf_op jit(solution)/shard_map/dot_general | solution.py:26
  462.7 6.1 convolution_convert_fusion.3
  477.3 7.2 %convolution_convert_fusion = bf16[1152,1152]{0,1:T(8,128)(2,1)} fusion(bf16[1024,1440]{0,1:T(8,128)(2,1)} %bitcast.216, bf16[1,1024,1152]{2,1,0:T(8,128)(2,1)} %all-gather.12.cloned.1.call-done), kind=kOutput, calls=%fused_computation.50 | convolution fusion | flops 2719236096 | bytes 7372800 | tf_op jit(solution)/shard_map/dot_general | solution.py:20
  488.6 23.4 %all-to-all-done.7 = bf16[4,256,1152]{2,1,0:T(8,128)(2,1)} async-done(((bf16[4,256,1152]{2,1,0:T(8,128)(2,1)}), bf16[4,256,1152]{2,1,0:T(8,128)(2,1)}, u32[]{:S(2)}, u32[]{:S(2)}) %all-to-all-start.7) | async-done | bytes 2359328 | tf_op jit(solution)/shard_map/all_to_all | solution.py:150
  517.2 9.0 %fusion.48 = bf16[1,256,1152]{2,1,0:T(8,128)(2,1)} fusion(f32[256,1152]{1,0:T(8,128)S(1)} %copy-done.8, bf16[256,4608]{1,0:T(8,128)(2,1)} %get-tuple-element.289, bf16[4608,1152]{1,0:T(8,128)(2,1)} %param.35, f32[1152]{0:T(1024)S(1)} %convert_element_type.136), kind=kOutput, calls=%fused_computation.85 | convolution fusion | flops 2718793728 | bytes 14750208 | tf_op jit(solution)/shard_map/dot_general | solution.py:16
  531.6 61.7 %all-to-all-done.10 = bf16[256,8,576]{0,2,1:T(8,128)(2,1)} async-done(((bf16[256,8,576]{0,2,1:T(8,128)(2,1)}), bf16[256,8,576]{0,2,1:T(8,128)(2,1)}, u32[]{:S(2)}, u32[]{:S(2)}) %all-to-all-start.10) | async-done | bytes 2359328 | tf_op jit(solution)/shard_map/all_to_all | solution.py:159
  599.7 7.4 %convolution_convert_fusion.2 = bf16[1152,576]{1,0:T(8,128)(2,1)} fusion(bf16[2048,1152]{1,0:T(8,128)(2,1)} %all-gather.10.cloned.1.call-done, bf16[2048,576]{0,1:T(8,128)(2,1)S(1)} %bitcast.221), kind=kOutput, calls=%fused_computation.72 | convolution fusion | flops 2718572544 | bytes 8404992 | tf_op jit(solution)/shard_map/dot_general | solution.py:20
  607.3 45.4 %psum.7 = f32[12672]{0:T(1024)S(1)} all-reduce(f32[12672]{0:T(1024)S(1)} %constant_dynamic-update-slice_fusion), channel_id=1, replica_groups=mesh['seq'=8,'batch'=4] {'seq','batch'}, use_global_device_ids=true, to_apply=%region_26.27 | all-reduce | flops 12672 | bytes 101376 | tf_op jit(solution)/shard_map/psum | solution.py:334
  669.8 9.4 %collective-permute-done.2 = f32[288,144]{1,0:T(8,128)} collective-permute-done((f32[288,144]{1,0:T(8,128)S(1)}, f32[288,144]{1,0:T(8,128)}, u32[]{:S(2)}, u32[]{:S(2)}) %collective-permute-start.2) | collective-permute-done | bytes 165920 | tf_op jit(solution)/shard_map/ppermute | solution.py:213
  (322 shorter events, 276.5 us)
Async XLA Ops:
  7.2 151.0 %copy-start = (bf16[1152,1152]{1,0:T(8,128)(2,1)S(1)}, bf16[1152,1152]{1,0:T(8,128)(2,1)}, u32[]{:S(2)}) copy-start(bf16[1152,1152]{1,0:T(8,128)(2,1)} %param.29) | copy-start | bytes 7962628
  29.8 48.9 %all-to-all-start = ((bf16[256,3,8,144]{0,3,1,2:T(8,128)(2,1)}), bf16[256,3,8,144]{0,3,1,2:T(8,128)(2,1)}, u32[]{:S(2)}, u32[]{:S(2)}) async-start(bf16[256,3,8,144]{0,3,1,2:T(8,128)(2,1)} %copy.100), calls=%async_computation | async-start | bytes 3538944 | tf_op jit(solution)/shard_map/all_to_all | solution.py:258
  137.2 20.9 %all-to-all-start.1 = ((bf16[8,256,144]{1,2,0:T(8,128)(2,1)}), bf16[8,256,144]{1,2,0:T(8,128)(2,1)}, u32[]{:S(2)}, u32[]{:S(2)}) async-start(bf16[8,256,144]{1,2,0:T(8,128)(2,1)} %copy.104), calls=%async_computation.1 | async-start | bytes 1179648 | tf_op jit(solution)/shard_map/all_to_all | solution.py:270
  141.4 304.5 %all-gather.8.cloned.1.call-start = ((), (), s32[]{:S(2)}) async-start(), calls=%async_computation.17 | async-start | bytes 2949120 | tf_op jit(solution)/shard_map/all_gather | solution.py:188
  206.5 256.1 %all-gather.6.cloned.1.call-start = ((), (), s32[]{:S(2)}) async-start(), calls=%async_computation.15 | async-start | bytes 5308416 | tf_op jit(solution)/shard_map/all_gather | solution.py:200
  207.3 270.0 %all-gather.12.cloned.1.call-start = ((), (), s32[]{:S(2)}) async-start(), calls=%async_computation.22 | async-start | bytes 2949120 | tf_op jit(solution)/shard_map/all_gather | solution.py:188
  213.1 20.2 %all-to-all-start.2 = ((bf16[256,8,144]{0,2,1:T(8,128)(2,1)}), bf16[256,8,144]{0,2,1:T(8,128)(2,1)S(1)}, u32[]{:S(2)}, u32[]{:S(2)}) async-start(bf16[256,8,144]{0,2,1:T(8,128)(2,1)} %bitcast.18), calls=%async_computation.2 | async-start | bytes 1179648 | tf_op jit(solution)/shard_map/all_to_all | solution.py:297
  216.7 383.0 %all-gather.10.cloned.1.call-start = ((), (), s32[]{:S(2)}) async-start(), calls=%async_computation.19 | async-start | bytes 5308416 | tf_op jit(solution)/shard_map/all_gather | solution.py:158
  326.6 21.0 %all-to-all-start.5 = ((bf16[8,256,144]{1,2,0:T(8,128)(2,1)}), bf16[8,256,144]{1,2,0:T(8,128)(2,1)}, u32[]{:S(2)}, u32[]{:S(2)}) async-start(bf16[8,256,144]{1,2,0:T(8,128)(2,1)} %copy.112), calls=%async_computation.5 | async-start | bytes 1179648 | tf_op jit(solution)/shard_map/all_to_all | solution.py:307
  347.7 37.4 %all-to-all-start.4 = ((bf16[8,256,144]{1,2,0:T(8,128)(2,1)}), bf16[8,256,144]{1,2,0:T(8,128)(2,1)}, u32[]{:S(2)}, u32[]{:S(2)}) async-start(bf16[8,256,144]{1,2,0:T(8,128)(2,1)} %copy.111), calls=%async_computation.4 | async-start | bytes 1179648 | tf_op jit(solution)/shard_map/all_to_all | solution.py:306
  385.1 38.9 %all-to-all-start.9 = ((bf16[256,4,1440]{0,2,1:T(8,128)(2,1)}), bf16[256,4,1440]{0,2,1:T(8,128)(2,1)}, u32[]{:S(2)}, u32[]{:S(2)}) async-start(bf16[256,4,1440]{0,2,1:T(8,128)(2,1)} %pad_maximum_fusion), calls=%async_computation.10 | async-start | bytes 5898240 | tf_op jit(solution)/shard_map/all_to_all | solution.py:172
  424.0 26.3 %all-to-all-start.3 = ((bf16[8,256,144]{1,2,0:T(8,128)(2,1)}), bf16[8,256,144]{1,2,0:T(8,128)(2,1)}, u32[]{:S(2)}, u32[]{:S(2)}) async-start(bf16[8,256,144]{1,2,0:T(8,128)(2,1)} %copy.110), calls=%async_computation.3 | async-start | bytes 1179648 | tf_op jit(solution)/shard_map/all_to_all | solution.py:305
  428.2 231.6 %reduce-scatter.7.cloned.1.call-start = ((), (), s32[]{:S(2)}) async-start(), calls=%async_computation.18 | async-start | bytes 995328 | tf_op jit(solution)/shard_map/reduce_scatter | solution.py:192
  450.3 20.9 %all-to-all-start.6 = ((bf16[256,4,576]{0,2,1:T(8,128)(2,1)}), bf16[256,4,576]{0,2,1:T(8,128)(2,1)}, u32[]{:S(2)}, u32[]{:S(2)}) async-start(bf16[256,4,576]{0,2,1:T(8,128)(2,1)} %pad_maximum_fusion.1), calls=%async_computation.6 | async-start | bytes 2359296 | tf_op jit(solution)/shard_map/all_to_all | solution.py:184
  454.7 206.7 %reduce-scatter.5.cloned.1.call-start = ((), (), s32[]{:S(2)}) async-start(), calls=%async_computation.16 | async-start | bytes 1474560 | tf_op jit(solution)/shard_map/reduce_scatter | solution.py:202
  472.7 39.3 %all-to-all-start.7 = ((bf16[4,256,1152]{2,1,0:T(8,128)(2,1)}), bf16[4,256,1152]{2,1,0:T(8,128)(2,1)}, u32[]{:S(2)}, u32[]{:S(2)}) async-start(bf16[4,256,1152]{2,1,0:T(8,128)(2,1)} %broadcast_in_dim.94), calls=%async_computation.7 | async-start | bytes 4718592 | tf_op jit(solution)/shard_map/all_to_all | solution.py:150
  477.2 204.3 %reduce-scatter.11.cloned.1.call-start = ((), (), s32[]{:S(2)}) async-start(), calls=%async_computation.21 | async-start | bytes 2985984 | tf_op jit(solution)/shard_map/reduce_scatter | solution.py:192
  512.0 81.3 %all-to-all-start.10 = ((bf16[256,8,576]{0,2,1:T(8,128)(2,1)}), bf16[256,8,576]{0,2,1:T(8,128)(2,1)}, u32[]{:S(2)}, u32[]{:S(2)}) async-start(bf16[256,8,576]{0,2,1:T(8,128)(2,1)} %bitcast.210), calls=%async_computation.12 | async-start | bytes 4718592 | tf_op jit(solution)/shard_map/all_to_all | solution.py:159
  593.3 74.2 %all-to-all-start.8 = ((bf16[576,8,144]{0,2,1:T(8,128)(2,1)}), bf16[576,8,144]{0,2,1:T(8,128)(2,1)}, u32[]{:S(2)}, u32[]{:S(2)}) async-start(bf16[576,8,144]{0,2,1:T(8,128)(2,1)} %bitcast.32), calls=%async_computation.8 | async-start | bytes 2949120 | tf_op jit(solution)/shard_map/all_to_all | solution.py:143
  597.6 85.7 %reduce-scatter.9.cloned.1.call-start = ((), (), s32[]{:S(2)}) async-start(), calls=%async_computation.20 | async-start | bytes 1843200 | tf_op jit(solution)/shard_map/reduce_scatter | solution.py:161
  599.7 54.2 %copy-start.21 = (bf16[256,1152]{1,0:T(8,128)(2,1)S(1)}, bf16[256,1152]{1,0:T(8,128)(2,1)}, u32[]{:S(2)}) copy-start(bf16[256,1152]{1,0:T(8,128)(2,1)} %copy-done.20) | copy-start | bytes 1769476
  662.7 16.6 %collective-permute-start.2 = (f32[288,144]{1,0:T(8,128)S(1)}, f32[288,144]{1,0:T(8,128)}, u32[]{:S(2)}, u32[]{:S(2)}) collective-permute-start(f32[288,144]{1,0:T(8,128)S(1)} %get-tuple-element.301), channel_id=1, source_target_pairs={{0,8},{4,20},{8,0},{12,12},{16,24},{20,4},{24,16},{28,28},{1,9},{5... | collective-permute-start | bytes 497672 | tf_op jit(solution)/shard_map/ppermute | solution.py:213
  664.8 14.5 %collective-permute-start.1 = (f32[288,144]{1,0:T(8,128)S(1)}, f32[288,144]{1,0:T(8,128)}, u32[]{:S(2)}, u32[]{:S(2)}) collective-permute-start(f32[288,144]{1,0:T(8,128)S(1)} %get-tuple-element.302), channel_id=1, source_target_pairs={{0,20},{4,0},{8,12},{12,24},{16,4},{20,16},{24,28},{28,8},{1,21},{... | collective-permute-start | bytes 497672 | tf_op jit(solution)/shard_map/ppermute | solution.py:213
  666.1 13.2 %collective-permute-start = (f32[288,144]{1,0:T(8,128)S(1)}, f32[288,144]{1,0:T(8,128)}, u32[]{:S(2)}, u32[]{:S(2)}) collective-permute-start(f32[288,144]{1,0:T(8,128)S(1)} %get-tuple-element.300), channel_id=1, source_target_pairs={{0,0},{4,12},{8,24},{12,4},{16,16},{20,28},{24,8},{28,20},{1,1},{5... | collective-permute-start | bytes 497672 | tf_op jit(solution)/shard_map/ppermute | solution.py:213
  (59 other events, 433.5 us)
Sparse Core Ops, SparseCore 0:
  206.7 36.2 all-gather.7
  244.6 51.1 all-gather.5
  297.7 36.1 all-gather.11
  335.9 63.8 all-gather.9
  450.4 32.5 reduce-scatter.6
  485.7 39.0 reduce-scatter.4
  527.1 67.5 reduce-scatter.10
  607.3 30.9 reduce-scatter.8

commit v11 on v8

--- a/solution.py
+++ b/solution.py
@@ -181,23 +181,56 @@
     piece = grad_heads.shape[1] // 3
     left_all = lax.all_gather(left, "seq", axis=0, tiled=True)
     partial = contract_rows(left_all, grad_heads).astype(jnp.bfloat16)
-    summed = lax.psum_scatter(partial, "batch", scatter_dimension=0, tiled=True)
-    summed = summed.astype(jnp.float32)
     inverse = pow(3, -1, seq_count)
     slots = []
     for slot in range(3):
         target = ((me - slot) * inverse) % seq_count
         chunk = (3 * target + slot) // seq_count
-        sent = lax.dynamic_slice_in_dim(summed, chunk * piece, piece, axis=1)
+        sent = lax.dynamic_slice_in_dim(partial, chunk * piece, piece, axis=1)
         pairs = []
         for source in range(seq_count):
             pairs.append((source, ((source - slot) * inverse) % seq_count))
         slots.append(lax.ppermute(sent, "seq", pairs))
-    return jnp.concatenate(slots, axis=1)
-
-
-def padded_size(sizes):
-    return -(-sum(sizes) // 4096) * 4096
+    placed = jnp.concatenate(slots, axis=1)
+    summed = lax.psum_scatter(placed, "batch", scatter_dimension=0, tiled=True)
+    return summed.astype(jnp.float32)
+
+
+def split_high_low(values):
+    high = values.astype(jnp.bfloat16)
+    low = (values - high.astype(jnp.float32)).astype(jnp.bfloat16)
+    return jnp.concatenate([high, low], axis=0)
+
+
+def join_high_low(values):
+    half = values.shape[0] // 2
+    return values[:half] + values[half:]
+
+
+def skip_grad_with_small(left, right, small):
+    batch_count = lax.axis_size("batch")
+    seq_count = lax.axis_size("seq")
+    rows, width = right.shape
+    small_rows = -(-small.shape[0] // width)
+    small_flat = jnp.pad(small, (0, small_rows * width - small.shape[0]))
+    left_rows = lax.all_to_all(left, "batch", split_axis=1, concat_axis=0, tiled=True)
+    payload = jnp.concatenate(
+        [right, split_high_low(small_flat.reshape(small_rows, width))], axis=0
+    )
+    got = gather_by_exchange(payload, "batch").reshape(batch_count, -1, width)
+    right_all = got[:, :rows].reshape(batch_count * rows, width)
+    batch_sum = join_high_low(jnp.sum(got[:, rows:].astype(jnp.float32), axis=0))
+    partial = contract_rows(left_rows, right_all).astype(jnp.bfloat16)
+    out_rows, cols = partial.shape
+    piece = cols // seq_count
+    extra = split_high_low(batch_sum).reshape(-1, 1, piece)
+    extra = jnp.broadcast_to(extra, (extra.shape[0], seq_count, piece))
+    pieces = jnp.concatenate([partial.reshape(out_rows, seq_count, piece), extra], axis=0)
+    swapped = lax.all_to_all(pieces, "seq", split_axis=1, concat_axis=1, tiled=True)
+    summed = jnp.sum(swapped.astype(jnp.float32), axis=1)
+    weight_block = summed[:out_rows]
+    small_sum = join_high_low(summed[out_rows:].reshape(2 * small_rows, width))
+    return weight_block, small_sum.reshape(-1)[: small.shape[0]]
 
 
 GRAD_PLAN = {"skip": "batch", "qkv": "seq", "out": "batch", "hidden": "seq", "down": "batch"}
@@ -266,7 +299,7 @@
     grad_out_rows = cotangent[0]
     grad_down_weight = weight_grad("down", hidden_act, grad_out_rows)
     grad_down_bias = column_sums(grad_out_rows)
-    grad_act = times_transposed(grad_out_rows, down_weight)
+    grad_act = lax.optimization_barrier(times_transposed(grad_out_rows, down_weight))
     grad_pre = gelu_pull(grad_act)[0].astype(jnp.bfloat16)
     grad_hidden_weight = weight_grad("hidden", normed_two, grad_pre)
     grad_hidden_bias = column_sums(grad_pre)
@@ -298,11 +331,9 @@
     grad_mixed_norm, grad_attention_gain, grad_attention_shift = first_pull(grad_normed_one)
     grad_mixed = (grad_middle + grad_mixed_norm).astype(jnp.bfloat16)
     grad_skip_bias = column_sums(grad_mixed)
-    grad_skip_weight = weight_grad("skip", joined, grad_mixed)
     grad_joined = times_transposed(grad_mixed, skip_weight)
     grad_tokens = grad_joined[:, :feature_count][None]
     grad_long_skip = grad_joined[:, feature_count:][None]
-    summed_weights = (grad_skip_weight, grad_qkv_weight, grad_out_weight, grad_hidden_weight, grad_down_weight)
     small_grads = (
         grad_skip_bias,
         grad_attention_gain,
@@ -314,7 +345,10 @@
         grad_down_bias,
     )
     small_sizes = [piece.shape[0] for piece in small_grads]
-    small_total = lax.psum(jnp.pad(jnp.concatenate(small_grads), (0, padded_size(small_sizes) - sum(small_sizes))), ("seq", "batch"))
+    grad_skip_weight, small_total = skip_grad_with_small(
+        joined, grad_mixed, jnp.concatenate(small_grads)
+    )
+    summed_weights = (grad_skip_weight, grad_qkv_weight, grad_out_weight, grad_hidden_weight, grad_down_weight)
     summed_small = []
     offset = 0
     for size in small_sizes:

time: 663 us -> 656 us (0.989)
  waiting for transfers between devices: 263 us -> 251 us
  local copies, waits for them, and re-layouts: 69.6 us -> 79.8 us
    all_to_all x3 -> x2, waiting for transfers between devices: 21.9 us -> 0.01 us  [batch_gathered_grad(): lax.all_to_all(left, 'batch', split_axis=1, concat_axis=0, tiled=True)]
    all_to_all x1 -> x2, waiting for transfers between devices: 0.01 us -> 15.5 us  [the longest x1 13.3 us: skip_grad_with_small(): lax.all_to_all(pieces, 'seq', split_axis=1, concat_axis=1, tiled=True)]
    all_to_all x1, waiting for transfers between devices: 16.2 us -> 6.67 us  [block(): lax.all_to_all(context_heads, 'seq', split_axis=0, concat_axis=1, tiled=T...]
    ppermute x3, waiting for transfers between devices: 9.25 us -> 18 us  [qkv_grad_from_heads(): slots.append(lax.ppermute(sent, 'seq', pairs))]
    unnamed x82 -> x97, local copies, waits for them, and re-layouts: 10.4 us -> 14.7 us
  transfers between devices with their start and end apart: 24 -> 23, of which waited for: 11 -> 11; matrix products, arithmetic and copies ran while one was open for 28% -> 31% of each run, Pallas kernels for 0% -> 0%
where the time goes in v11:
time: 656 us; the launch traced here: 649 us
  waiting for transfers between devices  251 us (38%)
  matrix products  188 us (29%)
  local copies, waits for them, and re-layouts  79.8 us (12%)
  starting transfers between devices  57.2 us (9%)
  other arithmetic  57.1 us (9%)
  between operations  15.4 us (2%)
    all_to_all x1, waiting for transfers between devices, seq_gathered_grad(): lax.all_to_all(right, 'seq', split_axis=1, concat_axis=0, tiled=True)  66.9 us
    all_to_all x1, waiting for transfers between devices, block(): lax.all_to_all(packed.reshape(local_rows, 3, seq_count, feature_count //...  41.7 us
    dot_general x5, matrix products, product(): return jnp.dot(left, right, preferred_element_type=jnp.float32)  41.6 us
    dot_general x5, matrix products, times_transposed(): lax.dot_general(left, right, (((1,), (1,)), ((), ())), preferred_element_...  30.7 us
    all_to_all x1, waiting for transfers between devices, block(): lax.all_to_all(grad_key, 'seq', split_axis=0, concat_axis=1, tiled=True)  29.7 us
    dot_general x5, matrix products, contract_rows(): lax.dot_general(left, right, (((0,), (0,)), ((), ())), preferred_element_...  29.2 us
    all_to_all x1, waiting for transfers between devices, gather_by_exchange(): lax.all_to_all(copies, axis, split_axis=0, concat_axis=0, tiled=True)  26 us
    dot_general x4, matrix products, one_block(): jnp.einsum('hbk,bhd->khd', probs_low, grad_block, preferred_element_type=...  20.9 us
  transfers between devices with their start and end apart: 23, of which 11 were waited for; matrix products, arithmetic and copies ran while one was open for 31% of the time, Pallas kernels for 0%

profile of v11, /device:TPU:0, one launch (start us, length us, event | category | flops | bytes accessed | tf_op | source)
XLA Modules:
  0.0 649.5 jit_solution(16734261173036318095)
XLA Ops:
  16.0 7.2 %convolution_convert_fusion.1 = bf16[256,3456]{1,0:T(8,128)(2,1)} fusion(bf16[256,1152]{1,0:T(8,128)(2,1)S(1)} %add_convert_fusion.3, bf16[1152,3456]{1,0:T(8,128)(2,1)} %param.28), kind=kOutput, calls=%fused_computation.53 | convolution fusion | flops 2039316480 | bytes 10321920 | tf_op jit(solution)/shard_map/dot_general | solution.py:16
  29.8 6.7 %all-to-all-start = ((bf16[256,3,8,144]{0,3,1,2:T(8,128)(2,1)}), bf16[256,3,8,144]{0,3,1,2:T(8,128)(2,1)}, u32[]{:S(2)}, u32[]{:S(2)}) async-start(bf16[256,3,8,144]{0,3,1,2:T(8,128)(2,1)} %copy.131), calls=%async_computation | async-start | bytes 3538944 | tf_op jit(solution)/shard_map/all_to_all | solution.py:275
  36.9 41.7 %all-to-all-done = bf16[256,3,8,144]{0,3,1,2:T(8,128)(2,1)} async-done(((bf16[256,3,8,144]{0,3,1,2:T(8,128)(2,1)}), bf16[256,3,8,144]{0,3,1,2:T(8,128)(2,1)}, u32[]{:S(2)}, u32[]{:S(2)}) %all-to-all-start) | async-done | bytes 1769504 | tf_op jit(solution)/shard_map/all_to_all | solution.py:275
  93.8 36.5 %while.27 = (s32[]{:T(128)}, bf16[4,512,144]{1,2,0:T(8,128)(2,1)}, f32[4,2,512,1]{2,1,3,0:T(2,128)S(1)}, s32[4,512]{1,0:T(4,128)S(1)}, s32[2048]{0:T(1024)S(1)},...) while((s32[]{:T(128)}, bf16[4,512,144]{1,2,0:T(8,128)(2,1)}, ...), condition=%wide.region_7.8_spmd, body=%wide.region_4.7_spmd.sunk | while | flops 628169728 | bytes 33536144 | solution.py:78
  141.5 9.7 %fusion.67 = f32[256,4608]{1,0:T(8,128)} fusion(bf16[4608,1152]{1,0:T(8,128)(2,1)} %param.35, bf16[1,256,1152]{2,1,0:T(8,128)(2,1)} %param.37), kind=kOutput, calls=%fused_computation.126 | convolution fusion | flops 2717908992 | bytes 15925248 | tf_op jit(solution)/shard_map/dot_general | solution.py:26
  151.2 6.7 %all-to-all-done.1 = bf16[8,256,144]{1,2,0:T(8,128)(2,1)} async-done(((bf16[8,256,144]{1,2,0:T(8,128)(2,1)}), bf16[8,256,144]{1,2,0:T(8,128)(2,1)}, u32[]{:S(2)}, u32[]{:S(2)}) %all-to-all-start.1) | async-done | bytes 589856 | tf_op jit(solution)/shard_map/all_to_all | solution.py:287
  162.6 18.4 %convert_reduce_fusion = (f32[4608]{0:T(1024)S(1)}, bf16[256,4608]{1,0:T(8,128)(2,1)S(1)}, f32[256,4608]{1,0:T(8,128)}, f32[256,4608]{1,0:T(8,128)}) fusion(f32[256,4608]{1,0:T(8,128)} %fusion.67, f32[4608]{0:T(1024)S(1)} %convert_element_type.155, bf16[256,1152]{1,0:T(8,128)(2,1)} %add_convert_fusion.2, bf16[1152,4608]{1,0:T(8,128)(2,1)} %param.33), kind=kOutput, calls=%fused_computation.55 | convolution fusion | flops 2806377984 | bytes 27758592 | tf_op jit(solution)/shard_map/dot_general | solution.py:16
  182.4 7.4 %multiply_reduce_fusion.1 = (f32[1152]{0:T(1024)S(1)}, f32[256]{0:T(256)S(1)}, f32[1152]{0:T(1024)S(1)}, f32[256,1152]{1,0:T(8,128)S(1)}) fusion(f32[256,1152]{1,0:T(8,128)S(1)} %copy-done.7, f32[256]{0:T(256)S(1)} %fusion.71, f32[256]{0:T(256)S(1)} %broadcast_multiply_fusion, f32[1152]{0:T(1024)S(1)} %convert_element_type.152, ...), kind=kOutput, calls=%fused_computation.111 | convolution fusion | flops 2720265728 | bytes 15352320 | tf_op jit(solution)/shard_map/dot_general | solution.py:26
  203.0 16.1 %all-to-all-done.2 = bf16[256,8,144]{0,2,1:T(8,128)(2,1)S(1)} async-done(((bf16[256,8,144]{0,2,1:T(8,128)(2,1)}), bf16[256,8,144]{0,2,1:T(8,128)(2,1)S(1)}, u32[]{:S(2)}, u32[]{:S(2)}) %all-to-all-start.2) | async-done | bytes 589856 | tf_op jit(solution)/shard_map/all_to_all | solution.py:313
  225.6 87.6 %while.28 = (s32[]{:T(128)}, f32[2048,2,72]{0,2,1:T(8,128)S(1)}, f32[2048,2,72]{0,2,1:T(8,128)}, bf16[4,512,144]{1,2,0:T(8,128)(2,1)}, bf16[4,512,2,72]{1,3,2,0:...) while((s32[]{:T(128)}, f32[2048,2,72]{0,2,1:T(8,128)S(1)}, ...), condition=%wide.region_14.15_spmd.clone, body=%wide.region_12.14_spmd.clone.sunk | while | flops 1543781376 | bytes 136800560 | solution.py:124
  240.1 5.4 fusion.147
  262.3 5.2 fusion.147
  284.1 5.2 fusion.147
  320.4 15.4 %all-to-all-done.5 = bf16[8,256,144]{1,2,0:T(8,128)(2,1)S(1)} async-done(((bf16[8,256,144]{1,2,0:T(8,128)(2,1)}), bf16[8,256,144]{1,2,0:T(8,128)(2,1)S(1)}, u32[]{:S(2)}, u32[]{:S(2)}) %all-to-all-start.5) | async-done | bytes 589856 | tf_op jit(solution)/shard_map/all_to_all | solution.py:323
  344.3 29.7 %all-to-all-done.4 = bf16[8,256,144]{1,2,0:T(8,128)(2,1)} async-done(((bf16[8,256,144]{1,2,0:T(8,128)(2,1)}), bf16[8,256,144]{1,2,0:T(8,128)(2,1)}, u32[]{:S(2)}, u32[]{:S(2)}) %all-to-all-start.4) | async-done | bytes 589856 | tf_op jit(solution)/shard_map/all_to_all | solution.py:322
  388.8 13.4 %all-to-all-done.3 = bf16[8,256,144]{1,2,0:T(8,128)(2,1)} async-done(((bf16[8,256,144]{1,2,0:T(8,128)(2,1)}), bf16[8,256,144]{1,2,0:T(8,128)(2,1)}, u32[]{:S(2)}, u32[]{:S(2)}) %all-to-all-start.3) | async-done | bytes 589856 | tf_op jit(solution)/shard_map/all_to_all | solution.py:321
  406.6 6.5 multiply_reduce_fusion.2
  435.6 18.0 %collective-permute-done.2 = bf16[1152,144]{0,1:T(8,128)(2,1)S(1)} collective-permute-done((bf16[1152,144]{0,1:T(8,128)(2,1)S(1)}, bf16[1152,144]{0,1:T(8,128)(2,1)S(1)}, u32[]{:S(2)}, u32[]{:S(2)}) %collective-permute-start.2) | collective-permute-done | bytes 331808 | tf_op jit(solution)/shard_map/ppermute | solution.py:193
  461.8 7.3 %convolution_convert_fusion = bf16[1152,1152]{0,1:T(8,128)(2,1)} fusion(bf16[1024,1152]{1,0:T(8,128)(2,1)} %bitcast.40, bf16[1,1024,1152]{2,1,0:T(8,128)(2,1)} %all-gather.12.cloned.1.call-done), kind=kOutput, calls=%fused_computation.50 | convolution fusion | flops 2719236096 | bytes 7372800 | tf_op jit(solution)/shard_map/dot_general | solution.py:20
  473.5 26.0 %all-to-all-done.7 = bf16[4,278,1152]{2,1,0:T(8,128)(2,1)S(1)} async-done(((bf16[4,278,1152]{2,1,0:T(8,128)(2,1)}), bf16[4,278,1152]{2,1,0:T(8,128)(2,1)S(1)}, u32[]{:S(2)}, u32[]{:S(2)}) %all-to-all-start.7) | async-done | bytes 2562080 | tf_op jit(solution)/shard_map/all_to_all | solution.py:150
  516.3 66.9 %all-to-all-done.10 = bf16[256,8,576]{0,2,1:T(8,128)(2,1)S(1)} async-done(((bf16[256,8,576]{0,2,1:T(8,128)(2,1)}), bf16[256,8,576]{0,2,1:T(8,128)(2,1)S(1)}, u32[]{:S(2)}, u32[]{:S(2)}) %all-to-all-start.10) | async-done | bytes 2359328 | tf_op jit(solution)/shard_map/all_to_all | solution.py:159
  589.6 8.2 %convolution_convert_fusion.2 = bf16[1152,576]{1,0:T(8,128)(2,1)} fusion(bf16[2048,1152]{1,0:T(8,128)(2,1)} %all-gather.10.cloned.1.call-done, bf16[2048,576]{0,1:T(8,128)(2,1)} %bitcast.219), kind=kOutput, calls=%fused_computation.73 | convolution fusion | flops 2718572544 | bytes 8404992 | tf_op jit(solution)/shard_map/dot_general | solution.py:20
  597.8 8.8 %fusion.48 = bf16[1,256,1152]{2,1,0:T(8,128)(2,1)} fusion(f32[256,1152]{1,0:T(8,128)S(1)} %copy-done.8, bf16[256,4608]{1,0:T(8,128)(2,1)} %copy-done.13, bf16[4608,1152]{1,0:T(8,128)(2,1)} %param.35, f32[1152]{0:T(1024)S(1)} %convert_element_type.157), kind=kOutput, calls=%fused_computation.84 | convolution fusion | flops 2718793728 | bytes 14750208 | tf_op jit(solution)/shard_map/dot_general | solution.py:16
  616.2 13.3 %all-to-all-done.8 = bf16[752,8,144]{0,2,1:T(8,128)(2,1)} async-done(((bf16[752,8,144]{0,2,1:T(8,128)(2,1)}), bf16[752,8,144]{0,2,1:T(8,128)(2,1)}, u32[]{:S(2)}, u32[]{:S(2)}) %all-to-all-start.8) | async-done | bytes 1732640 | tf_op jit(solution)/shard_map/all_to_all | solution.py:229
  (360 shorter events, 290.4 us)
Async XLA Ops:
  7.2 150.7 %copy-start = (bf16[1152,1152]{1,0:T(8,128)(2,1)S(1)}, bf16[1152,1152]{1,0:T(8,128)(2,1)}, u32[]{:S(2)}) copy-start(bf16[1152,1152]{1,0:T(8,128)(2,1)} %param.29) | copy-start | bytes 7962628
  29.8 48.8 %all-to-all-start = ((bf16[256,3,8,144]{0,3,1,2:T(8,128)(2,1)}), bf16[256,3,8,144]{0,3,1,2:T(8,128)(2,1)}, u32[]{:S(2)}, u32[]{:S(2)}) async-start(bf16[256,3,8,144]{0,3,1,2:T(8,128)(2,1)} %copy.131), calls=%async_computation | async-start | bytes 3538944 | tf_op jit(solution)/shard_map/all_to_all | solution.py:275
  137.0 20.9 %all-to-all-start.1 = ((bf16[8,256,144]{1,2,0:T(8,128)(2,1)}), bf16[8,256,144]{1,2,0:T(8,128)(2,1)}, u32[]{:S(2)}, u32[]{:S(2)}) async-start(bf16[8,256,144]{1,2,0:T(8,128)(2,1)} %copy.135), calls=%async_computation.1 | async-start | bytes 1179648 | tf_op jit(solution)/shard_map/all_to_all | solution.py:287
  141.2 274.6 %all-gather.8.cloned.1.call-start = ((), (), s32[]{:S(2)}) async-start(), calls=%async_computation.17 | async-start | bytes 2949120 | tf_op jit(solution)/shard_map/all_gather | solution.py:170
  192.3 234.2 %all-gather.6.cloned.1.call-start = ((), (), s32[]{:S(2)}) async-start(), calls=%async_computation.16 | async-start | bytes 5308416 | tf_op jit(solution)/shard_map/all_gather | solution.py:182
  193.1 268.7 %all-gather.12.cloned.1.call-start = ((), (), s32[]{:S(2)}) async-start(), calls=%async_computation.22 | async-start | bytes 2949120 | tf_op jit(solution)/shard_map/all_gather | solution.py:170
  198.9 20.2 %all-to-all-start.2 = ((bf16[256,8,144]{0,2,1:T(8,128)(2,1)}), bf16[256,8,144]{0,2,1:T(8,128)(2,1)S(1)}, u32[]{:S(2)}, u32[]{:S(2)}) async-start(bf16[256,8,144]{0,2,1:T(8,128)(2,1)} %bitcast.18), calls=%async_computation.2 | async-start | bytes 1179648 | tf_op jit(solution)/shard_map/all_to_all | solution.py:313
  202.4 387.2 %all-gather.10.cloned.1.call-start = ((), (), s32[]{:S(2)}) async-start(), calls=%async_computation.19 | async-start | bytes 5308416 | tf_op jit(solution)/shard_map/all_gather | solution.py:158
  219.1 96.5 %all-to-all-start.9 = ((bf16[256,4,288]{0,2,1:T(8,128)(2,1)}), bf16[256,4,288]{0,2,1:T(8,128)(2,1)}, u32[]{:S(2)}, u32[]{:S(2)}) async-start(bf16[256,4,288]{0,2,1:T(8,128)(2,1)} %bitcast.35), calls=%async_computation.9 | async-start | bytes 1179648 | tf_op jit(solution)/shard_map/all_to_all | solution.py:166
  315.6 20.2 %all-to-all-start.5 = ((bf16[8,256,144]{1,2,0:T(8,128)(2,1)}), bf16[8,256,144]{1,2,0:T(8,128)(2,1)S(1)}, u32[]{:S(2)}, u32[]{:S(2)}) async-start(bf16[8,256,144]{1,2,0:T(8,128)(2,1)} %copy.143), calls=%async_computation.5 | async-start | bytes 1179648 | tf_op jit(solution)/shard_map/all_to_all | solution.py:323
  336.6 37.4 %all-to-all-start.4 = ((bf16[8,256,144]{1,2,0:T(8,128)(2,1)}), bf16[8,256,144]{1,2,0:T(8,128)(2,1)}, u32[]{:S(2)}, u32[]{:S(2)}) async-start(bf16[8,256,144]{1,2,0:T(8,128)(2,1)} %copy.142), calls=%async_computation.4 | async-start | bytes 1179648 | tf_op jit(solution)/shard_map/all_to_all | solution.py:322
  374.0 28.2 %all-to-all-start.3 = ((bf16[8,256,144]{1,2,0:T(8,128)(2,1)}), bf16[8,256,144]{1,2,0:T(8,128)(2,1)}, u32[]{:S(2)}, u32[]{:S(2)}) async-start(bf16[8,256,144]{1,2,0:T(8,128)(2,1)} %copy.141), calls=%async_computation.3 | async-start | bytes 1179648 | tf_op jit(solution)/shard_map/all_to_all | solution.py:321
  402.2 19.8 %all-to-all-start.6 = ((bf16[256,4,576]{0,2,1:T(8,128)(2,1)}), bf16[256,4,576]{0,2,1:T(8,128)(2,1)}, u32[]{:S(2)}, u32[]{:S(2)}) async-start(bf16[256,4,576]{0,2,1:T(8,128)(2,1)} %pad_maximum_fusion.1), calls=%async_computation.6 | async-start | bytes 2359296 | tf_op jit(solution)/shard_map/all_to_all | solution.py:216
  406.5 205.9 %reduce-scatter.7.cloned.1.call-start = ((), (), s32[]{:S(2)}) async-start(), calls=%async_computation.18 | async-start | bytes 995328 | tf_op jit(solution)/shard_map/reduce_scatter | solution.py:174
  422.0 33.5 %all-to-all-start.11 = ((bf16[256,4,1152]{2,0,1:T(8,128)(2,1)}), bf16[256,4,1152]{2,0,1:T(8,128)(2,1)}, u32[]{:S(2)}, u32[]{:S(2)}) async-start(bf16[256,4,1152]{2,0,1:T(8,128)(2,1)} %bitcast.164), calls=%async_computation.13 | async-start | bytes 4718592 | tf_op jit(solution)/shard_map/all_to_all | solution.py:166
  426.5 187.5 %reduce-scatter.13.cloned.1.call-start = ((), (), s32[]{:S(2)}) async-start(), calls=%async_computation.23 | async-start | bytes 1474560
  431.5 22.1 %collective-permute-start.2 = (bf16[1152,144]{0,1:T(8,128)(2,1)S(1)}, bf16[1152,144]{0,1:T(8,128)(2,1)S(1)}, u32[]{:S(2)}, u32[]{:S(2)}) collective-permute-start(bf16[1152,144]{0,1:T(8,128)(2,1)S(1)} %get-tuple-element.386), channel_id=1, source_target_pairs={{0,8},{4,20},{8,0},{12,12},{16,24},{20,4},{24,16},{28,28},{1,9},{5... | collective-permute-start | bytes 995336 | tf_op jit(solution)/shard_map/ppermute | solution.py:193
  433.4 20.2 %collective-permute-start.1 = (bf16[1152,144]{0,1:T(8,128)(2,1)S(1)}, bf16[1152,144]{0,1:T(8,128)(2,1)S(1)}, u32[]{:S(2)}, u32[]{:S(2)}) collective-permute-start(bf16[1152,144]{0,1:T(8,128)(2,1)S(1)} %get-tuple-element.387), channel_id=1, source_target_pairs={{0,20},{4,0},{8,12},{12,24},{16,4},{20,16},{24,28},{28,8},{1,21},{... | collective-permute-start | bytes 995336 | tf_op jit(solution)/shard_map/ppermute | solution.py:193
  434.9 18.7 %collective-permute-start = (bf16[1152,144]{0,1:T(8,128)(2,1)S(1)}, bf16[1152,144]{0,1:T(8,128)(2,1)S(1)}, u32[]{:S(2)}, u32[]{:S(2)}) collective-permute-start(bf16[1152,144]{0,1:T(8,128)(2,1)S(1)} %get-tuple-element.385), channel_id=1, source_target_pairs={{0,0},{4,12},{8,24},{12,4},{16,16},{20,28},{24,8},{28,20},{1,1},{5... | collective-permute-start | bytes 995336 | tf_op jit(solution)/shard_map/ppermute | solution.py:193
  457.2 42.3 %all-to-all-start.7 = ((bf16[4,278,1152]{2,1,0:T(8,128)(2,1)}), bf16[4,278,1152]{2,1,0:T(8,128)(2,1)S(1)}, u32[]{:S(2)}, u32[]{:S(2)}) async-start(bf16[4,278,1152]{2,1,0:T(8,128)(2,1)} %broadcast_in_dim.101), calls=%async_computation.7 | async-start | bytes 5160960 | tf_op jit(solution)/shard_map/all_to_all | solution.py:150
  461.5 177.1 %reduce-scatter.11.cloned.1.call-start = ((), (), s32[]{:S(2)}) async-start(), calls=%async_computation.21 | async-start | bytes 2985984 | tf_op jit(solution)/shard_map/reduce_scatter | solution.py:174
  501.0 82.2 %all-to-all-start.10 = ((bf16[256,8,576]{0,2,1:T(8,128)(2,1)}), bf16[256,8,576]{0,2,1:T(8,128)(2,1)S(1)}, u32[]{:S(2)}, u32[]{:S(2)}) async-start(bf16[256,8,576]{0,2,1:T(8,128)(2,1)} %bitcast.209), calls=%async_computation.11 | async-start | bytes 4718592 | tf_op jit(solution)/shard_map/all_to_all | solution.py:159
  583.2 46.3 %all-to-all-start.8 = ((bf16[752,8,144]{0,2,1:T(8,128)(2,1)}), bf16[752,8,144]{0,2,1:T(8,128)(2,1)}, u32[]{:S(2)}, u32[]{:S(2)}) async-start(bf16[752,8,144]{0,2,1:T(8,128)(2,1)} %pad_maximum_fusion), calls=%async_computation.8 | async-start | bytes 3538944 | tf_op jit(solution)/shard_map/all_to_all | solution.py:229
  587.5 53.0 %reduce-scatter.9.cloned.1.call-start = ((), (), s32[]{:S(2)}) async-start(), calls=%async_computation.20 | async-start | bytes 1843200 | tf_op jit(solution)/shard_map/reduce_scatter | solution.py:161
  (64 other events, 496.9 us)
Sparse Core Ops, SparseCore 0:
  192.5 42.1 all-gather.7
  236.3 50.7 all-gather.5
  288.9 36.0 all-gather.11
  327.1 75.7 all-gather.9
  420.0 33.5 reduce-scatter.6
  456.3 46.9 reduce-scatter.12
  505.6 72.0 reduce-scatter.10
  597.9 30.8 reduce-scatter.8

commit v12 on v11

--- a/solution.py
+++ b/solution.py
@@ -181,19 +181,19 @@
     piece = grad_heads.shape[1] // 3
     left_all = lax.all_gather(left, "seq", axis=0, tiled=True)
     partial = contract_rows(left_all, grad_heads).astype(jnp.bfloat16)
+    summed = lax.psum_scatter(partial, "batch", scatter_dimension=0, tiled=True)
+    summed = summed.astype(jnp.float32)
     inverse = pow(3, -1, seq_count)
     slots = []
     for slot in range(3):
         target = ((me - slot) * inverse) % seq_count
         chunk = (3 * target + slot) // seq_count
-        sent = lax.dynamic_slice_in_dim(partial, chunk * piece, piece, axis=1)
+        sent = lax.dynamic_slice_in_dim(summed, chunk * piece, piece, axis=1)
         pairs = []
         for source in range(seq_count):
             pairs.append((source, ((source - slot) * inverse) % seq_count))
         slots.append(lax.ppermute(sent, "seq", pairs))
-    placed = jnp.concatenate(slots, axis=1)
-    summed = lax.psum_scatter(placed, "batch", scatter_dimension=0, tiled=True)
-    return summed.astype(jnp.float32)
+    return jnp.concatenate(slots, axis=1)
 
 
 def split_high_low(values):

time: 656 us -> 650 us (level)
  waiting for transfers between devices: 251 us -> 235 us
    all_to_all x2, waiting for transfers between devices: 0.01 us -> 31.7 us  [batch_gathered_grad(): lax.all_to_all(left, 'batch', split_axis=1, concat_axis=0, tiled=True)]
    all_to_all x1, waiting for transfers between devices: 29.7 us -> 13.5 us  [block(): lax.all_to_all(grad_key, 'seq', split_axis=0, concat_axis=1, tiled=True)]
    all_to_all x1, waiting for transfers between devices: 26 us -> 13.4 us  [gather_by_exchange(): lax.all_to_all(copies, axis, split_axis=0, concat_axis=0, tiled=True)]
    ppermute x3, waiting for transfers between devices: 18 us -> 8.8 us  [qkv_grad_from_heads(): slots.append(lax.ppermute(sent, 'seq', pairs))]
    all_to_all x1, waiting for transfers between devices: 13.3 us -> 4.35 us  [skip_grad_with_small(): lax.all_to_all(pieces, 'seq', split_axis=1, concat_axis=1, tiled=True)]
    all_to_all x1, waiting for transfers between devices: 13.4 us -> 6.22 us  [block(): lax.all_to_all(grad_query, 'seq', split_axis=0, concat_axis=1, tiled=True)]
    unnamed x97 -> x92, local copies, waits for them, and re-layouts: 14.7 us -> 10.2 us
  transfers between devices with their start and end apart: 23 -> 23, of which waited for: 11 -> 13; matrix products, arithmetic and copies ran while one was open for 31% -> 37% of each run, Pallas kernels for 0% -> 0%
where the time goes in v12:
time: 650 us; the launch traced here: 637 us
  waiting for transfers between devices  235 us (36%)
  matrix products  192 us (30%)
  local copies, waits for them, and re-layouts  75.4 us (12%)
  other arithmetic  60.7 us (9%)
  starting transfers between devices  58.1 us (9%)
  between operations  15.3 us (2%)
    all_to_all x1, waiting for transfers between devices, seq_gathered_grad(): lax.all_to_all(right, 'seq', split_axis=1, concat_axis=0, tiled=True)  65.9 us
    all_to_all x1, waiting for transfers between devices, block(): lax.all_to_all(packed.reshape(local_rows, 3, seq_count, feature_count //...  41.7 us
    dot_general x5, matrix products, product(): return jnp.dot(left, right, preferred_element_type=jnp.float32)  41.7 us
    dot_general x5, matrix products, times_transposed(): lax.dot_general(left, right, (((1,), (1,)), ((), ())), preferred_element_...  32.2 us
    all_to_all x2, waiting for transfers between devices, batch_gathered_grad(): lax.all_to_all(left, 'batch', split_axis=1, concat_axis=0, tiled=True)  31.7 us
    dot_general x5, matrix products, contract_rows(): lax.dot_general(left, right, (((0,), (0,)), ((), ())), preferred_element_...  30.5 us
    dot_general x4, matrix products, one_block(): jnp.einsum('hbk,bhd->khd', probs_low, grad_block, preferred_element_type=...  21.3 us
    dot_general x8, matrix products, score_block(): jnp.einsum('bhd,khd->hbk', query_block, key_heads, preferred_element_type...  20.8 us
  transfers between devices with their start and end apart: 23, of which 13 were waited for; matrix products, arithmetic and copies ran while one was open for 37% of the time, Pallas kernels for 0%

profile of v12, /device:TPU:0, one launch (start us, length us, event | category | flops | bytes accessed | tf_op | source)
XLA Modules:
  0.0 637.1 jit_solution(6155554068792694)
XLA Ops:
  16.0 7.2 %convolution_convert_fusion.1 = bf16[256,3456]{1,0:T(8,128)(2,1)} fusion(bf16[256,1152]{1,0:T(8,128)(2,1)S(1)} %add_convert_fusion.3, bf16[1152,3456]{1,0:T(8,128)(2,1)} %param.28), kind=kOutput, calls=%fused_computation.53 | convolution fusion | flops 2039316480 | bytes 10321920 | tf_op jit(solution)/shard_map/dot_general | solution.py:16
  29.8 6.8 %all-to-all-start = ((bf16[256,3,8,144]{0,3,1,2:T(8,128)(2,1)}), bf16[256,3,8,144]{0,3,1,2:T(8,128)(2,1)}, u32[]{:S(2)}, u32[]{:S(2)}) async-start(bf16[256,3,8,144]{0,3,1,2:T(8,128)(2,1)} %copy.127), calls=%async_computation | async-start | bytes 3538944 | tf_op jit(solution)/shard_map/all_to_all | solution.py:275
  37.0 41.7 %all-to-all-done = bf16[256,3,8,144]{0,3,1,2:T(8,128)(2,1)} async-done(((bf16[256,3,8,144]{0,3,1,2:T(8,128)(2,1)}), bf16[256,3,8,144]{0,3,1,2:T(8,128)(2,1)}, u32[]{:S(2)}, u32[]{:S(2)}) %all-to-all-start) | async-done | bytes 1769504 | tf_op jit(solution)/shard_map/all_to_all | solution.py:275
  94.0 36.5 %while.27 = (s32[]{:T(128)}, bf16[4,512,144]{1,2,0:T(8,128)(2,1)}, f32[4,2,512,1]{2,1,3,0:T(2,128)S(1)}, s32[4,512]{1,0:T(4,128)S(1)}, s32[2048]{0:T(1024)S(1)},...) while((s32[]{:T(128)}, bf16[4,512,144]{1,2,0:T(8,128)(2,1)}, ...), condition=%wide.region_7.8_spmd, body=%wide.region_4.7_spmd.sunk | while | flops 628169728 | bytes 33536144 | solution.py:78
  142.6 9.7 %fusion.67 = f32[256,4608]{1,0:T(8,128)} fusion(bf16[4608,1152]{1,0:T(8,128)(2,1)} %param.35, bf16[1,256,1152]{2,1,0:T(8,128)(2,1)} %param.37), kind=kOutput, calls=%fused_computation.126 | convolution fusion | flops 2717908992 | bytes 15925248 | tf_op jit(solution)/shard_map/dot_general | solution.py:26
  152.4 10.6 %all-to-all-done.1 = bf16[8,256,144]{1,2,0:T(8,128)(2,1)} async-done(((bf16[8,256,144]{1,2,0:T(8,128)(2,1)}), bf16[8,256,144]{1,2,0:T(8,128)(2,1)}, u32[]{:S(2)}, u32[]{:S(2)}) %all-to-all-start.1) | async-done | bytes 589856 | tf_op jit(solution)/shard_map/all_to_all | solution.py:287
  167.7 18.4 %convert_reduce_fusion = (f32[4608]{0:T(1024)S(1)}, bf16[256,4608]{1,0:T(8,128)(2,1)S(1)}, f32[256,4608]{1,0:T(8,128)}, f32[256,4608]{1,0:T(8,128)}) fusion(f32[256,4608]{1,0:T(8,128)} %fusion.67, f32[4608]{0:T(1024)S(1)} %convert_element_type.155, bf16[256,1152]{1,0:T(8,128)(2,1)} %add_convert_fusion.2, bf16[1152,4608]{1,0:T(8,128)(2,1)} %param.33), kind=kOutput, calls=%fused_computation.55 | convolution fusion | flops 2806377984 | bytes 27758592 | tf_op jit(solution)/shard_map/dot_general | solution.py:16
  187.5 7.4 %multiply_reduce_fusion.1 = (f32[1152]{0:T(1024)S(1)}, f32[256]{0:T(256)S(1)}, f32[1152]{0:T(1024)S(1)}, f32[256,1152]{1,0:T(8,128)S(1)}) fusion(f32[256,1152]{1,0:T(8,128)S(1)} %copy-done.7, f32[256]{0:T(256)S(1)} %fusion.71, f32[256]{0:T(256)S(1)} %broadcast_multiply_fusion, f32[1152]{0:T(1024)S(1)} %convert_element_type.152, ...), kind=kOutput, calls=%fused_computation.111 | convolution fusion | flops 2720265728 | bytes 15352320 | tf_op jit(solution)/shard_map/dot_general | solution.py:26
  207.6 16.1 %all-to-all-done.2 = bf16[256,8,144]{0,2,1:T(8,128)(2,1)S(1)} async-done(((bf16[256,8,144]{0,2,1:T(8,128)(2,1)}), bf16[256,8,144]{0,2,1:T(8,128)(2,1)S(1)}, u32[]{:S(2)}, u32[]{:S(2)}) %all-to-all-start.2) | async-done | bytes 589856 | tf_op jit(solution)/shard_map/all_to_all | solution.py:313
  230.2 87.9 %while.28 = (s32[]{:T(128)}, f32[2048,2,72]{0,2,1:T(8,128)S(1)}, f32[2048,2,72]{0,2,1:T(8,128)}, bf16[4,512,144]{1,2,0:T(8,128)(2,1)}, bf16[4,512,2,72]{1,3,2,0:...) while((s32[]{:T(128)}, f32[2048,2,72]{0,2,1:T(8,128)S(1)}, ...), condition=%wide.region_14.15_spmd.clone, body=%wide.region_12.14_spmd.clone.sunk | while | flops 1543781376 | bytes 136800560 | solution.py:124
  288.3 5.8 fusion.147
  325.3 20.2 %all-to-all-done.5 = bf16[8,256,144]{1,2,0:T(8,128)(2,1)S(1)} async-done(((bf16[8,256,144]{1,2,0:T(8,128)(2,1)}), bf16[8,256,144]{1,2,0:T(8,128)(2,1)S(1)}, u32[]{:S(2)}, u32[]{:S(2)}) %all-to-all-start.5) | async-done | bytes 589856 | tf_op jit(solution)/shard_map/all_to_all | solution.py:323
  353.7 13.5 %all-to-all-done.4 = bf16[8,256,144]{1,2,0:T(8,128)(2,1)} async-done(((bf16[8,256,144]{1,2,0:T(8,128)(2,1)}), bf16[8,256,144]{1,2,0:T(8,128)(2,1)}, u32[]{:S(2)}, u32[]{:S(2)}) %all-to-all-start.4) | async-done | bytes 589856 | tf_op jit(solution)/shard_map/all_to_all | solution.py:322
  382.1 6.2 all-to-all-done.3
  392.7 6.5 %multiply_reduce_fusion.2 = (f32[1152]{0:T(1024)S(1)}, f32[256]{0:T(256)S(1)}, f32[1152]{0:T(1024)S(1)}, f32[256,1152]{1,0:T(8,128)S(1)}) fusion(f32[256,1152]{1,0:T(8,128)S(1)} %copy-done.10, f32[256]{0:T(256)S(1)} %copy-done.40, f32[256]{0:T(256)S(1)} %copy-done.35, f32[1152]{0:T(1024)S(1)} %copy-done.33, bf16[1152,3456]{1,0:T(8,128)(2,1)} %param.28, ...), kind=kOutput, calls=%fused_computation.113 | convolution fusion | flops 2046096896 | bytes 12108288 | tf_op jit(solution)/shard_map/dot_general | solution.py:26
  400.9 6.1 convolution_convert_fusion.3
  414.2 31.7 %all-to-all-done.11 = bf16[256,4,1152]{2,0,1:T(8,128)(2,1)} async-done(((bf16[256,4,1152]{2,0,1:T(8,128)(2,1)}), bf16[256,4,1152]{2,0,1:T(8,128)(2,1)}, u32[]{:S(2)}, u32[]{:S(2)}) %all-to-all-start.11) | async-done | bytes 2359328 | tf_op jit(solution)/shard_map/all_to_all | solution.py:166
  456.1 7.2 %convolution_convert_fusion = bf16[1152,1152]{0,1:T(8,128)(2,1)} fusion(bf16[1024,1152]{1,0:T(8,128)(2,1)} %bitcast.40, bf16[1,1024,1152]{2,1,0:T(8,128)(2,1)} %all-gather.12.cloned.1.call-done), kind=kOutput, calls=%fused_computation.50 | convolution fusion | flops 2719236096 | bytes 7372800 | tf_op jit(solution)/shard_map/dot_general | solution.py:20
  467.6 13.4 %all-to-all-done.7 = bf16[4,278,1152]{2,1,0:T(8,128)(2,1)S(1)} async-done(((bf16[4,278,1152]{2,1,0:T(8,128)(2,1)}), bf16[4,278,1152]{2,1,0:T(8,128)(2,1)S(1)}, u32[]{:S(2)}, u32[]{:S(2)}) %all-to-all-start.7) | async-done | bytes 2562080 | tf_op jit(solution)/shard_map/all_to_all | solution.py:150
  498.0 65.9 %all-to-all-done.10 = bf16[256,8,576]{0,2,1:T(8,128)(2,1)S(1)} async-done(((bf16[256,8,576]{0,2,1:T(8,128)(2,1)}), bf16[256,8,576]{0,2,1:T(8,128)(2,1)S(1)}, u32[]{:S(2)}, u32[]{:S(2)}) %all-to-all-start.10) | async-done | bytes 2359328 | tf_op jit(solution)/shard_map/all_to_all | solution.py:159
  570.3 8.2 %convolution_convert_fusion.2 = bf16[1152,576]{1,0:T(8,128)(2,1)} fusion(bf16[2048,1152]{1,0:T(8,128)(2,1)} %all-gather.10.cloned.1.call-done, bf16[2048,576]{0,1:T(8,128)(2,1)} %bitcast.219), kind=kOutput, calls=%fused_computation.73 | convolution fusion | flops 2718572544 | bytes 8404992 | tf_op jit(solution)/shard_map/dot_general | solution.py:20
  578.5 8.8 %fusion.48 = bf16[1,256,1152]{2,1,0:T(8,128)(2,1)} fusion(f32[256,1152]{1,0:T(8,128)S(1)} %copy-done.8, bf16[256,4608]{1,0:T(8,128)(2,1)} %copy-done.13, bf16[4608,1152]{1,0:T(8,128)(2,1)} %param.35, f32[1152]{0:T(1024)S(1)} %convert_element_type.157), kind=kOutput, calls=%fused_computation.84 | convolution fusion | flops 2718793728 | bytes 14750208 | tf_op jit(solution)/shard_map/dot_general | solution.py:16
  587.3 5.7 fusion.84
  605.4 6.3 collective-permute-done.1
  (356 shorter events, 297.8 us)
Async XLA Ops:
  7.2 155.7 %copy-start = (bf16[1152,1152]{1,0:T(8,128)(2,1)S(1)}, bf16[1152,1152]{1,0:T(8,128)(2,1)}, u32[]{:S(2)}) copy-start(bf16[1152,1152]{1,0:T(8,128)(2,1)} %param.29) | copy-start | bytes 7962628
  29.8 48.9 %all-to-all-start = ((bf16[256,3,8,144]{0,3,1,2:T(8,128)(2,1)}), bf16[256,3,8,144]{0,3,1,2:T(8,128)(2,1)}, u32[]{:S(2)}, u32[]{:S(2)}) async-start(bf16[256,3,8,144]{0,3,1,2:T(8,128)(2,1)} %copy.127), calls=%async_computation | async-start | bytes 3538944 | tf_op jit(solution)/shard_map/all_to_all | solution.py:275
  137.1 25.9 %all-to-all-start.1 = ((bf16[8,256,144]{1,2,0:T(8,128)(2,1)}), bf16[8,256,144]{1,2,0:T(8,128)(2,1)}, u32[]{:S(2)}, u32[]{:S(2)}) async-start(bf16[8,256,144]{1,2,0:T(8,128)(2,1)} %copy.131), calls=%async_computation.1 | async-start | bytes 1179648 | tf_op jit(solution)/shard_map/all_to_all | solution.py:287
  141.3 259.4 %all-gather.6.cloned.1.call-start = ((), (), s32[]{:S(2)}) async-start(), calls=%async_computation.16 | async-start | bytes 5308416 | tf_op jit(solution)/shard_map/all_gather | solution.py:182
  142.0 309.3 %all-gather.8.cloned.1.call-start = ((), (), s32[]{:S(2)}) async-start(), calls=%async_computation.18 | async-start | bytes 2949120 | tf_op jit(solution)/shard_map/all_gather | solution.py:170
  197.5 258.6 %all-gather.12.cloned.1.call-start = ((), (), s32[]{:S(2)}) async-start(), calls=%async_computation.23 | async-start | bytes 2949120 | tf_op jit(solution)/shard_map/all_gather | solution.py:170
  203.3 20.4 %all-to-all-start.2 = ((bf16[256,8,144]{0,2,1:T(8,128)(2,1)}), bf16[256,8,144]{0,2,1:T(8,128)(2,1)S(1)}, u32[]{:S(2)}, u32[]{:S(2)}) async-start(bf16[256,8,144]{0,2,1:T(8,128)(2,1)} %bitcast.18), calls=%async_computation.2 | async-start | bytes 1179648 | tf_op jit(solution)/shard_map/all_to_all | solution.py:313
  207.0 363.2 %all-gather.10.cloned.1.call-start = ((), (), s32[]{:S(2)}) async-start(), calls=%async_computation.20 | async-start | bytes 5308416 | tf_op jit(solution)/shard_map/all_gather | solution.py:158
  223.7 96.8 %all-to-all-start.9 = ((bf16[256,4,288]{0,2,1:T(8,128)(2,1)}), bf16[256,4,288]{0,2,1:T(8,128)(2,1)}, u32[]{:S(2)}, u32[]{:S(2)}) async-start(bf16[256,4,288]{0,2,1:T(8,128)(2,1)} %bitcast.35), calls=%async_computation.10 | async-start | bytes 1179648 | tf_op jit(solution)/shard_map/all_to_all | solution.py:166
  320.5 24.9 %all-to-all-start.5 = ((bf16[8,256,144]{1,2,0:T(8,128)(2,1)}), bf16[8,256,144]{1,2,0:T(8,128)(2,1)S(1)}, u32[]{:S(2)}, u32[]{:S(2)}) async-start(bf16[8,256,144]{1,2,0:T(8,128)(2,1)} %copy.139), calls=%async_computation.5 | async-start | bytes 1179648 | tf_op jit(solution)/shard_map/all_to_all | solution.py:323
  346.3 20.9 %all-to-all-start.4 = ((bf16[8,256,144]{1,2,0:T(8,128)(2,1)}), bf16[8,256,144]{1,2,0:T(8,128)(2,1)}, u32[]{:S(2)}, u32[]{:S(2)}) async-start(bf16[8,256,144]{1,2,0:T(8,128)(2,1)} %copy.138), calls=%async_computation.4 | async-start | bytes 1179648 | tf_op jit(solution)/shard_map/all_to_all | solution.py:322
  367.2 21.1 %all-to-all-start.3 = ((bf16[8,256,144]{1,2,0:T(8,128)(2,1)}), bf16[8,256,144]{1,2,0:T(8,128)(2,1)}, u32[]{:S(2)}, u32[]{:S(2)}) async-start(bf16[8,256,144]{1,2,0:T(8,128)(2,1)} %copy.137), calls=%async_computation.3 | async-start | bytes 1179648 | tf_op jit(solution)/shard_map/all_to_all | solution.py:321
  388.3 19.4 %all-to-all-start.6 = ((bf16[256,4,576]{0,2,1:T(8,128)(2,1)}), bf16[256,4,576]{0,2,1:T(8,128)(2,1)}, u32[]{:S(2)}, u32[]{:S(2)}) async-start(bf16[256,4,576]{0,2,1:T(8,128)(2,1)} %pad_maximum_fusion.1), calls=%async_computation.6 | async-start | bytes 2359296 | tf_op jit(solution)/shard_map/all_to_all | solution.py:216
  392.6 200.4 %reduce-scatter.5.cloned.1.call-start = ((), (), s32[]{:S(2)}) async-start(), calls=%async_computation.17 | async-start | bytes 1474560 | tf_op jit(solution)/shard_map/reduce_scatter | solution.py:184
  407.7 38.2 %all-to-all-start.11 = ((bf16[256,4,1152]{2,0,1:T(8,128)(2,1)}), bf16[256,4,1152]{2,0,1:T(8,128)(2,1)}, u32[]{:S(2)}, u32[]{:S(2)}) async-start(bf16[256,4,1152]{2,0,1:T(8,128)(2,1)} %bitcast.209), calls=%async_computation.14 | async-start | bytes 4718592 | tf_op jit(solution)/shard_map/all_to_all | solution.py:166
  447.6 33.4 %all-to-all-start.7 = ((bf16[4,278,1152]{2,1,0:T(8,128)(2,1)}), bf16[4,278,1152]{2,1,0:T(8,128)(2,1)S(1)}, u32[]{:S(2)}, u32[]{:S(2)}) async-start(bf16[4,278,1152]{2,1,0:T(8,128)(2,1)} %broadcast_in_dim.101), calls=%async_computation.7 | async-start | bytes 5160960 | tf_op jit(solution)/shard_map/all_to_all | solution.py:150
  451.3 150.1 %reduce-scatter.7.cloned.1.call-start = ((), (), s32[]{:S(2)}) async-start(), calls=%async_computation.19 | async-start | bytes 995328 | tf_op jit(solution)/shard_map/reduce_scatter | solution.py:174
  455.6 170.7 %reduce-scatter.11.cloned.1.call-start = ((), (), s32[]{:S(2)}) async-start(), calls=%async_computation.22 | async-start | bytes 2985984 | tf_op jit(solution)/shard_map/reduce_scatter | solution.py:174
  482.6 81.4 %all-to-all-start.10 = ((bf16[256,8,576]{0,2,1:T(8,128)(2,1)}), bf16[256,8,576]{0,2,1:T(8,128)(2,1)S(1)}, u32[]{:S(2)}, u32[]{:S(2)}) async-start(bf16[256,8,576]{0,2,1:T(8,128)(2,1)} %bitcast.208), calls=%async_computation.12 | async-start | bytes 4718592 | tf_op jit(solution)/shard_map/all_to_all | solution.py:159
  563.9 53.2 %all-to-all-start.8 = ((bf16[752,8,144]{0,2,1:T(8,128)(2,1)}), bf16[752,8,144]{0,2,1:T(8,128)(2,1)}, u32[]{:S(2)}, u32[]{:S(2)}) async-start(bf16[752,8,144]{0,2,1:T(8,128)(2,1)} %pad_maximum_fusion), calls=%async_computation.8 | async-start | bytes 3538944 | tf_op jit(solution)/shard_map/all_to_all | solution.py:229
  568.3 59.9 %reduce-scatter.9.cloned.1.call-start = ((), (), s32[]{:S(2)}) async-start(), calls=%async_computation.21 | async-start | bytes 1843200 | tf_op jit(solution)/shard_map/reduce_scatter | solution.py:161
  594.4 11.0 %collective-permute-start.2 = (f32[288,144]{1,0:T(8,128)S(1)}, f32[288,144]{1,0:T(8,128)S(1)}, u32[]{:S(2)}, u32[]{:S(2)}) collective-permute-start(f32[288,144]{1,0:T(8,128)S(1)} %get-tuple-element.306), channel_id=1, source_target_pairs={{0,8},{4,20},{8,0},{12,12},{16,24},{20,4},{24,16},{28,28},{1,9},{5... | collective-permute-start | bytes 497672 | tf_op jit(solution)/shard_map/ppermute | solution.py:195
  598.2 13.5 %collective-permute-start.1 = (f32[288,144]{1,0:T(8,128)S(1)}, f32[288,144]{1,0:T(8,128)S(1)}, u32[]{:S(2)}, u32[]{:S(2)}) collective-permute-start(f32[288,144]{1,0:T(8,128)S(1)} %get-tuple-element.307), channel_id=1, source_target_pairs={{0,20},{4,0},{8,12},{12,24},{16,4},{20,16},{24,28},{28,8},{1,21},{... | collective-permute-start | bytes 497672 | tf_op jit(solution)/shard_map/ppermute | solution.py:195
  599.1 12.6 %collective-permute-start = (f32[288,144]{1,0:T(8,128)S(1)}, f32[288,144]{1,0:T(8,128)S(1)}, u32[]{:S(2)}, u32[]{:S(2)}) collective-permute-start(f32[288,144]{1,0:T(8,128)S(1)} %get-tuple-element.305), channel_id=1, source_target_pairs={{0,0},{4,12},{8,24},{12,4},{16,16},{20,28},{24,8},{28,20},{1,1},{5... | collective-permute-start | bytes 497672 | tf_op jit(solution)/shard_map/ppermute | solution.py:195
  (63 other events, 400.3 us)
Sparse Core Ops, SparseCore 0:
  143.7 53.6 all-gather.5
  199.3 42.5 all-gather.7
  243.7 37.3 all-gather.11
  283.1 56.1 all-gather.9
  407.1 43.7 reduce-scatter.4
  455.8 32.2 reduce-scatter.6
  490.4 70.5 reduce-scatter.10
  578.6 30.9 reduce-scatter.8
